TPU v7x, 32 devices: a whole 2x2x4 slice. The times are simulated.
32 devices in a mesh: member: 2 (over x), lat: 16 (over z, y, core).
Axes of the slice: x: 2, y: 2, z: 4, core: 2. Of those that a mesh axis runs over, the one named last changes fastest.
Arguments:
- field_in: float32 [24, 128, 128, 256], P('member', None, 'lat'), parts along dimension 0
- grad_out: float32 [24, 128, 128, 256], P('member', None, 'lat'), parts along dimension 0
- p_fwd: float32 [128, 128, 128], replicated
- p_inv: float32 [128, 128, 128], replicated
- w_mix: float32 [128, 128, 128, 2], replicated
Outputs:
- output 1: float32 [24, 128, 128, 256], P('member', None, 'lat'), parts along dimension 0
- output 2: float32 [256, 128, 128, 2], P('member'), parts along dimension 0
There are 2 independent parts. A program takes and returns all parts, laid end to end along the dimension named above; an argument that names none is the same for every part.
All inputs are finite; a program needn't handle non-finite values.
Results may differ from a plain program's by a relative error of at most 0.00656154.
Values are sent between devices in bfloat16 or wider.
A program may use at most 1 GiB of HBM per device.

v0:
```python
import math
import jax
import jax.numpy as jnp
from jax import lax
from jax.sharding import PartitionSpec as P


def gelu_grad(values):
    cumulative = 0.5 * (1.0 + lax.erf(values * math.sqrt(0.5)))
    density = jnp.exp(-0.5 * values * values) / math.sqrt(2.0 * math.pi)
    return cumulative + values * density


def mix_matrix(w_mix):
    w_real = w_mix[..., 0]
    w_imag = w_mix[..., 1]
    upper_half = jnp.stack([w_real, -w_imag], axis=-1)
    lower_half = jnp.stack([w_imag, w_real], axis=-1)
    return jnp.stack([upper_half, lower_half], axis=2).astype(jnp.bfloat16)


def analysis(values, mode_count, mode_gains):
    spectrum = jnp.fft.rfft(values, axis=-1)[..., :mode_count] * mode_gains
    return jnp.stack([spectrum.real, spectrum.imag], axis=-2).astype(jnp.bfloat16)


def synthesis(spec_pair, lon_count, mode_gains):
    complex_spec = lax.complex(spec_pair[..., 0, :].astype(jnp.float32), spec_pair[..., 1, :].astype(jnp.float32)) * mode_gains
    pad_width = [(0, 0)] * (complex_spec.ndim - 1) + [(0, lon_count // 2 + 1 - complex_spec.shape[-1])]
    return jnp.fft.irfft(jnp.pad(complex_spec, pad_width), n=lon_count, axis=-1)


def solution(mesh):
    lat_size = mesh.shape['lat']
    field_spec = P('member', None, 'lat', None)

    def local_step(field_loc, grad_loc, p_fwd, p_inv, w_mix):
        lon_count = field_loc.shape[-1]
        lat_count = p_fwd.shape[-1]
        m_local = lat_count // lat_size
        m_start = lax.axis_index('lat') * m_local
        root_lon = math.sqrt(lon_count)
        is_mean = jnp.arange(lat_count) == 0
        pw_own = lax.dynamic_slice_in_dim(p_fwd, m_start, m_local, axis=0).astype(jnp.bfloat16)
        pi_own = lax.dynamic_slice_in_dim(p_inv, m_start, m_local, axis=0).astype(jnp.bfloat16)
        w_big = mix_matrix(w_mix)
        four_lat = analysis(field_loc, lat_count, 1.0 / root_lon)
        four_own = lax.all_to_all(four_lat, 'lat', 4, 2, tiled=True)
        coeffs = jnp.einsum('mlt,bctrm->bclrm', pw_own, four_own, preferred_element_type=jnp.float32).astype(jnp.bfloat16)
        mixed_coef = jnp.einsum('losir,bilrm->bolsm', w_big, coeffs, preferred_element_type=jnp.float32).astype(jnp.bfloat16)
        back_own = jnp.einsum('mlt,bclrm->bctrm', pi_own, mixed_coef, preferred_element_type=jnp.float32).astype(jnp.bfloat16)
        back_lat = lax.all_to_all(back_own, 'lat', 2, 4, tiled=True)
        hidden = synthesis(back_lat, lon_count, root_lon)
        grad_hidden = grad_loc * gelu_grad(hidden)
        grad_back_lat = analysis(grad_hidden, lat_count, jnp.where(is_mean, 1.0, 2.0) / root_lon)
        grad_back_own = lax.all_to_all(grad_back_lat, 'lat', 4, 2, tiled=True)
        grad_mixed = jnp.einsum('mlt,bctrm->bclrm', pi_own, grad_back_own, preferred_element_type=jnp.float32).astype(jnp.bfloat16)
        gw_part = jnp.einsum('bolsm,bilrm->losir', grad_mixed, coeffs, preferred_element_type=jnp.float32)
        gw_total = lax.psum(gw_part, 'lat')
        grad_coef = jnp.einsum('losir,bolsm->bilrm', w_big, grad_mixed, preferred_element_type=jnp.float32).astype(jnp.bfloat16)
        grad_four_own = jnp.einsum('mlt,bclrm->bctrm', pw_own, grad_coef, preferred_element_type=jnp.float32).astype(jnp.bfloat16)
        grad_four_lat = lax.all_to_all(grad_four_own, 'lat', 2, 4, tiled=True)
        grad_field = grad_loc + synthesis(grad_four_lat, lon_count, jnp.where(is_mean, 1.0, 0.5) * root_lon)
        grad_wmix = jnp.stack([gw_total[:, :, 0, :, 0] + gw_total[:, :, 1, :, 1], gw_total[:, :, 1, :, 0] - gw_total[:, :, 0, :, 1]], axis=-1)
        return grad_field, grad_wmix

    return jax.shard_map(local_step, mesh=mesh, in_specs=(field_spec, field_spec, P(), P(), P()), out_specs=(field_spec, P('member', None, None, None)), check_vma=False)
```

profile of v0, /device:TPU:0, one launch (start us, length us, event | category | flops | bytes accessed | tf_op | source)
XLA Modules:
  0.0 1627.6 jit_solution(1592572339614100278)
XLA Ops:
  7.2 15.3 fusion.55
  22.5 15.2 fusion.57
  37.7 15.0 fusion.60
  52.7 6.1 fusion.75
  58.8 3.4 pad_maximum_fusion.3
  62.2 6.6 copy.82
  68.8 7.9 all-to-all-start
  76.8 20.4 %fusion.185 = (f32[128,128,128,1]{2,3,1,0:T(1,128)S(1)}, f32[128,128,128,1]{2,3,1,0:T(1,128)}) fusion(f32[128,128,128,2]{2,3,1,0:T(2,128)} %param.12), kind=kLoop, calls=%fused_computation.208 | loop fusion | bytes 33554432 | tf_op jit(solution)/shard_map/slice | solution.py:16
  97.1 9.4 convert.50
  109.6 4.7 negate_convert_fusion
  115.4 6.0 maximum_bitcast_fusion
  121.5 69.5 %all-to-all-done = bf16[12,128,8,2,128]{1,2,0,3,4:T(8,128)(2,1)} async-done(((bf16[12,128,8,2,128]{1,2,0,3,4:T(8,128)(2,1)}), bf16[12,128,8,2,128]{1,2,0,3,4:T(8,128)(2,1)}, u32[]{:S(2)}, u32[]{:S(2)}) %all-to-all-start) | async-done | bytes 6291488 | tf_op jit(solution)/shard_map/all_to_all | solution.py:48
  191.0 10.1 copy.84
  201.1 5.7 convert_bitcast_fusion.3
  206.8 9.0 copy.121
  215.7 12.0 fusion.33
  227.7 12.7 convert_bitcast_fusion.2
  240.4 16.4 %copy.91 = bf16[12,128,128,2,8]{1,3,0,4,2:T(2,128)(2,1)} copy(bf16[12,128,128,2,8]{2,1,3,0,4:T(8,128)(2,1)} %convert_bitcast_fusion.2) | data formatting | bytes 12582912 | tf_op jit(solution)/shard_map/convert_element_type | solution.py:51
  256.8 28.3 %all-to-all-start.1 = ((bf16[12,128,128,2,8]{1,3,0,4,2:T(2,128)(2,1)}), bf16[12,128,128,2,8]{1,3,0,4,2:T(2,128)(2,1)}, u32[]{:S(2)}, u32[]{:S(2)}) async-start(bf16[12,128,128,2,8]{1,3,0,4,2:T(2,128)(2,1)} %copy.91), calls=%async_computation.1 | async-start | bytes 12582912 | tf_op jit(solution)/shard_map/all_to_all | solution.py:52
  286.7 112.8 %all-to-all-done.1 = bf16[12,128,128,2,8]{1,3,0,4,2:T(2,128)(2,1)} async-done(((bf16[12,128,128,2,8]{1,3,0,4,2:T(2,128)(2,1)}), bf16[12,128,128,2,8]{1,3,0,4,2:T(2,128)(2,1)}, u32[]{:S(2)}, u32[]{:S(2)}) %all-to-all-start.1) | async-done | bytes 6291488 | tf_op jit(solution)/shard_map/all_to_all | solution.py:52
  399.4 4.2 copy.92
  405.4 4.0 fusion.186
  409.4 3.5 copy.157
  412.9 4.7 copy.158
  417.6 6.2 fusion.30
  426.5 4.3 slice.84
  430.8 50.6 %reverse.8 = f32[12,128,8,127]{3,1,2,0:T(8,128)} reverse(f32[12,128,8,127]{3,1,2,0:T(8,128)} %slice.84), dimensions={3} | reverse | bytes 12484608 | tf_op jit(solution)/shard_map/jit(fft)/reverse | solution.py:30
  481.4 7.1 slice.85
  488.5 50.6 %reverse.9 = f32[12,128,8,127]{3,1,2,0:T(8,128)} reverse(f32[12,128,8,127]{3,1,2,0:T(8,128)} %slice.85), dimensions={3} | reverse | bytes 12484608 | tf_op jit(solution)/shard_map/jit(fft)/reverse.1 | solution.py:30
  539.2 6.8 negate.4
  545.9 18.6 %fusion.20 = f32[12,128,8,256]{3,1,2,0:T(8,128)} fusion(f32[12,128,8,128]{3,1,2,0:T(8,128)} %copy-done.4, f32[12,128,8,127]{3,1,2,0:T(8,128)} %reverse.8), kind=kOutput, calls=%fused_computation.34 | convolution fusion | flops 9673441280 | bytes 25116672 | tf_op jit(solution)/shard_map/jit(fft)/dot.4 | solution.py:30
  564.6 20.3 %fusion.13 = f32[12,128,8,256]{3,1,2,0:T(8,128)} fusion(f32[12,128,8,128]{3,1,2,0:T(8,128)} %copy-done.4, f32[12,128,8,127]{3,1,2,0:T(8,128)} %reverse.8, f32[12,128,8,128]{3,1,2,0:T(8,128)S(1)} %bitcast.204, f32[12,128,8,127]{3,1,2,0:T(8,128)} %negate.4), kind=kOutput, calls=%fused_computation.27 | convolution fusion | flops 9682812928 | bytes 37650432 | tf_op jit(solution)/shard_map/jit(fft)/dot.3 | solution.py:30
  584.8 26.2 %fusion.8 = f32[12,128,8,256]{3,1,2,0:T(8,128)} fusion(f32[12,128,8,256]{3,1,2,0:T(8,128)} %fusion.13, f32[12,128,8,256]{3,1,2,0:T(8,128)} %fusion.20, f32[12,128,8,256]{3,2,1,0:T(8,128)} %param.9, f32[]{:T(128)S(6)} %multiply.91, f32[]{:T(128)S(6)} %multiply.89, f32[12,128,8,128]{3,1,2,0:T(8,128)S(1)} %bitcast.204, f32[12,128,8,127]{3,1,2,0:T(8,128)} %negate.4, ...), kind=kOutput, calls=%fused_computation.19 | convolution fusion | flops 9717153792 | bytes 63127560 | tf_op jit(solution)/shard_map/jit(fft)/dot.5 | solution.py:30
  611.0 17.3 %convolution_bitcast_fusion.2 = f32[12,128,8,256]{1,3,2,0:T(8,128)S(1)} fusion(f32[12,128,8,256]{3,1,2,0:T(8,128)} %fusion.8), kind=kOutput, calls=%fused_computation.104 | convolution fusion | flops 9663938560 | bytes 25165824 | tf_op jit(solution)/shard_map/jit(fft)/dot.6 | solution.py:23
  628.3 12.8 convolution_bitcast_fusion.1
  641.1 6.4 fusion.77
  650.9 6.8 copy.97
  657.6 28.1 %all-to-all-start.2 = ((bf16[12,128,8,2,128]{1,2,0,3,4:T(8,128)(2,1)}), bf16[12,128,8,2,128]{1,2,0,3,4:T(8,128)(2,1)}, u32[]{:S(2)}, u32[]{:S(2)}) async-start(bf16[12,128,8,2,128]{1,2,0,3,4:T(8,128)(2,1)} %copy.97), calls=%async_computation.2 | async-start | bytes 12582912 | tf_op jit(solution)/shard_map/all_to_all | solution.py:56
  685.8 12.5 copy.141
  698.2 101.8 %all-to-all-done.2 = bf16[12,128,8,2,128]{1,2,0,3,4:T(8,128)(2,1)} async-done(((bf16[12,128,8,2,128]{1,2,0,3,4:T(8,128)(2,1)}), bf16[12,128,8,2,128]{1,2,0,3,4:T(8,128)(2,1)}, u32[]{:S(2)}, u32[]{:S(2)}) %all-to-all-start.2) | async-done | bytes 6291488 | tf_op jit(solution)/shard_map/all_to_all | solution.py:56
  800.0 10.1 copy.99
  810.1 5.5 convert_bitcast_fusion.1
  815.5 9.1 copy.131
  824.6 12.3 copy.140
  836.9 18.2 %convolution_bitcast_fusion = f32[128,128,2,128,2]{3,1,4,2,0:T(8,128)} fusion(bf16[12,128,128,2,8,1]{1,0,4,5,3,2:T(8,128)(2,1)} %copy.140, bf16[12,128,128,2,8,1]{1,0,4,3,5,2:T(8,128)(2,1)} %copy.141), kind=kOutput, calls=%fused_computation.6 | convolution fusion | flops 1610612736 | bytes 46137344 | tf_op jit(solution)/shard_map/bolsm,bilrm->losir/dot_general | solution.py:58
  855.2 11.1 fusion.34
  866.3 12.7 convert_bitcast_fusion
  879.0 16.1 copy.104
  895.1 231.0 %all_to_all.68 = bf16[12,128,128,2,8]{1,3,0,4,2:T(2,128)(2,1)S(1)} all-to-all(bf16[12,128,128,2,8]{1,3,0,4,2:T(2,128)(2,1)} %copy.104), channel_id=1, replica_groups=mesh['member'=2,'lat'=16] {'lat'}, dimensions={2} | all-to-all | bytes 12582912 | tf_op jit(solution)/shard_map/all_to_all | solution.py:62
  1129.4 3.9 fusion.32
  1135.9 3.8 slice.92
  1139.7 48.4 %reverse.10 = f32[12,128,8,127]{1,3,2,0:T(8,128)} reverse(f32[12,128,8,127]{1,3,2,0:T(8,128)} %slice.92), dimensions={3} | reverse | bytes 12484608 | tf_op jit(solution)/shard_map/jit(fft)/reverse | solution.py:30
  1188.0 6.5 slice.93
  1194.6 48.6 %reverse.11 = f32[12,128,8,127]{1,3,2,0:T(8,128)} reverse(f32[12,128,8,127]{1,3,2,0:T(8,128)} %slice.93), dimensions={3} | reverse | bytes 12484608 | tf_op jit(solution)/shard_map/jit(fft)/reverse.1 | solution.py:30
  1243.2 6.7 negate.5
  1249.9 26.5 %fusion.22 = f32[12,128,8,256]{3,1,2,0:T(8,128)} fusion(f32[12,128,8,128]{1,3,2,0:T(8,128)S(1)} %bitcast.196, f32[12,128,8,127]{1,3,2,0:T(8,128)} %reverse.10), kind=kOutput, calls=%fused_computation.36 | convolution fusion | flops 9673441280 | bytes 25116672 | tf_op jit(solution)/shard_map/jit(fft)/dot.4 | solution.py:30
  1276.4 30.0 %fusion.11 = f32[12,128,8,256]{3,1,2,0:T(8,128)} fusion(f32[12,128,8,128]{1,3,2,0:T(8,128)} %copy-done.3, f32[12,128,8,127]{1,3,2,0:T(8,128)} %reverse.10, f32[12,128,8,128]{1,3,2,0:T(8,128)} %get-tuple-element.33, f32[12,128,8,127]{1,3,2,0:T(8,128)} %negate.5), kind=kOutput, calls=%fused_computation.25 | convolution fusion | flops 9682812928 | bytes 37650432 | tf_op jit(solution)/shard_map/jit(fft)/dot.3 | solution.py:30
  1306.4 35.3 %multiply_add_fusion = f32[12,128,8,256]{3,1,2,0:T(8,128)} fusion(f32[12,128,8,256]{3,1,2,0:T(8,128)} %fusion.11, f32[12,128,8,256]{3,1,2,0:T(8,128)} %fusion.22, f32[12,128,8,256]{3,2,1,0:T(8,128)} %param.9, f32[12,128,8,128]{1,3,2,0:T(8,128)} %get-tuple-element.33, f32[12,128,8,127]{1,3,2,0:T(8,128)} %negate.5), kind=kOutput, calls=%fused_computation.24 | convolution fusion | flops 9692315648 | bytes 62865408 | tf_op jit(solution)/shard_map/jit(fft)/dot.5 | solution.py:30
  1341.8 18.1 %copy.115 = f32[12,128,8,256]{3,2,1,0:T(8,128)} copy(f32[12,128,8,256]{3,1,2,0:T(8,128)} %multiply_add_fusion) | data formatting | bytes 25165824
  1359.9 217.2 %all-reduce.7.cloned.1.call-done = f32[128,128,2,128,2]{3,1,4,2,0:T(8,128)} async-done(((f32[128,128,2,128,2]{3,1,4,2,0:T(8,128)}), f32[128,128,2,128,2]{3,1,4,2,0:T(8,128)}) %all-reduce.7.cloned.1.call-update) | async-done | bytes 33554448 | tf_op jit(solution)/shard_map/psum | solution.py:59
  1577.1 11.9 fusion.24
  1589.0 11.8 fusion.26
  1600.7 6.5 pad_maximum_fusion.1
  1607.2 13.3 copy.116
  (35 shorter events, 19.5 us)
Async XLA Ops:
  7.2 15.3 copy-start.1
  68.8 122.2 %all-to-all-start = ((bf16[12,128,8,2,128]{1,2,0,3,4:T(8,128)(2,1)}), bf16[12,128,8,2,128]{1,2,0,3,4:T(8,128)(2,1)}, u32[]{:S(2)}, u32[]{:S(2)}) async-start(bf16[12,128,8,2,128]{1,2,0,3,4:T(8,128)(2,1)} %copy.82), calls=%async_computation | async-start | bytes 12582912 | tf_op jit(solution)/shard_map/all_to_all | solution.py:48
  97.1 9.4 copy-start.2
  109.6 4.7 copy-start.5
  109.6 5.9 copy-start.6
  256.8 142.6 %all-to-all-start.1 = ((bf16[12,128,128,2,8]{1,3,0,4,2:T(2,128)(2,1)}), bf16[12,128,128,2,8]{1,3,0,4,2:T(2,128)(2,1)}, u32[]{:S(2)}, u32[]{:S(2)}) async-start(bf16[12,128,128,2,8]{1,3,0,4,2:T(2,128)(2,1)} %copy.91), calls=%async_computation.1 | async-start | bytes 12582912 | tf_op jit(solution)/shard_map/all_to_all | solution.py:52
  423.8 2.6 copy-start.4
  539.2 25.4 %slice-start.2 = ((s8[6291456]{0:T(1024)(128)(4,1)}), s8[4194304]{0:T(1024)(128)(4,1)S(1)}, s32[]{:S(2)}) async-start(s8[6291456]{0:T(1024)(128)(4,1)} %bitcast.203), calls=%async_computation.7 | async-start | bytes 8388608
  545.9 18.6 %slice-start.3 = ((s8[6291456]{0:T(1024)(128)(4,1)}), s8[2097152]{0:T(1024)(128)(4,1)S(1)}, s32[]{:S(2)}) async-start(s8[6291456]{0:T(1024)(128)(4,1)} %bitcast.203), calls=%async_computation.8 | async-start | bytes 4194304
  611.0 17.3 %copy-start = (f32[12,128,8,256]{3,1,2,0:T(8,128)S(1)}, f32[12,128,8,256]{3,1,2,0:T(8,128)}, u32[]{:S(2)}) copy-start(f32[12,128,8,256]{3,1,2,0:T(8,128)} %fusion.8) | copy-start | bytes 37748740
  657.6 142.4 %all-to-all-start.2 = ((bf16[12,128,8,2,128]{1,2,0,3,4:T(8,128)(2,1)}), bf16[12,128,8,2,128]{1,2,0,3,4:T(8,128)(2,1)}, u32[]{:S(2)}, u32[]{:S(2)}) async-start(bf16[12,128,8,2,128]{1,2,0,3,4:T(8,128)(2,1)} %copy.97), calls=%async_computation.2 | async-start | bytes 12582912 | tf_op jit(solution)/shard_map/all_to_all | solution.py:56
  685.7 891.3 %all-reduce.7.cloned.1.call-start = ((), (), s32[]{:S(2)}) async-start(), calls=%async_computation.4 | async-start | bytes 67108864 | tf_op jit(solution)/shard_map/psum | solution.py:59
  1127.5 1.9 copy-start.7
  1133.2 2.7 copy-start.3
  1194.6 55.3 %slice-start = ((s8[6291456]{0:T(1024)(128)(4,1)}), s8[2097152]{0:T(1024)(128)(4,1)S(1)}, s32[]{:S(2)}) async-start(s8[6291456]{0:T(1024)(128)(4,1)} %bitcast.195), calls=%async_computation.5 | async-start | bytes 4194304
  1243.2 6.7 slice-start.1
Sparse Core Ops, SparseCore 0:
  855.3 721.7 all-reduce.6
where the time goes:
time: 1650 us; the launch traced here: 1630 us
  waiting for transfers between devices  501 us (30%)
  local copies, waits for them, and re-layouts  408 us (25%)
  matrix products  310 us (19%)
  blocking collectives  231 us (14%)
  other arithmetic  97.7 us (6%)
  starting transfers between devices  64.4 us (4%)
    all_to_all x1, blocking collectives, local_step(): grad_four_lat = lax.all_to_all(grad_four_own, 'lat', 2, 4, tiled=True)  231 us
    another operation x8, local copies, waits for them, and re-layouts, synthesis(): return jnp.fft.irfft(jnp.pad(complex_spec, pad_width), n=lon_count, axis=-1)  220 us
    psum x1, waiting for transfers between devices, local_step(): gw_total = lax.psum(gw_part, 'lat')  217 us
    another operation x6, matrix products, synthesis(): return jnp.fft.irfft(jnp.pad(complex_spec, pad_width), n=lon_count, axis=-1)  157 us
    all_to_all x1, waiting for transfers between devices, local_step(): back_lat = lax.all_to_all(back_own, 'lat', 2, 4, tiled=True)  113 us
    all_to_all x1, waiting for transfers between devices, local_step(): grad_back_own = lax.all_to_all(grad_back_lat, 'lat', 4, 2, tiled=True)  102 us
    another operation x5, matrix products, analysis(): spectrum = jnp.fft.rfft(values, axis=-1)[..., :mode_count] * mode_gains  75.6 us
    all_to_all x1, waiting for transfers between devices, local_step(): four_own = lax.all_to_all(four_lat, 'lat', 4, 2, tiled=True)  69.5 us
  transfers between devices with their start and end apart: 4, of which 4 were waited for; matrix products, arithmetic and copies ran while one was open for 20% of the time, Pallas kernels for 0%

commit v1 on v0

v1 whole, which is shorter than its diff:
```python
import functools
import math

import jax
import jax.numpy as jnp
import numpy as np
from jax import lax
from jax.experimental import pallas as pl
from jax.experimental.pallas import tpu as pltpu
from jax.sharding import PartitionSpec as P

MESH = pl.DeviceIdType.MESH
LANES = 128
SLOTS = 3
VMEM_LIMIT = 60 * 1024 * 1024
F32 = jnp.float32
BF16 = jnp.bfloat16

NN = (((1,), (0,)), ((), ()))
NT = (((1,), (1,)), ((), ()))
TN = (((0,), (0,)), ((), ()))


def dot(lhs, rhs, dims):
    return lax.dot_general(lhs, rhs, dims, preferred_element_type=F32)


def split_halves(values):
    high = values.astype(BF16)
    low = (values - high.astype(F32)).astype(BF16)
    return high, low


def dft_tables(group, m_local, lon_count):
    owner, slot, part = np.meshgrid(np.arange(group), np.arange(m_local), np.arange(2), indexing='ij')
    wave = (slot * group + owner).reshape(-1)
    part = part.reshape(-1)
    phase = 2.0 * np.pi * ((wave[:, None] * np.arange(lon_count)[None, :]) % lon_count) / lon_count
    base = np.where(part[:, None] == 0, np.cos(phase), -np.sin(phase)) / math.sqrt(lon_count)
    gains = np.where(wave == 0, 1.0, 2.0)[:, None]
    return base.astype(np.float32), (base * gains).astype(np.float32)


def two_halves(table):
    high = jnp.asarray(table).astype(BF16)
    low = (jnp.asarray(table) - high.astype(F32)).astype(BF16)
    return jnp.stack([high, low])


class Halves:
    def __init__(self, whole, b, halves, slot, sem, outward=False):
        self.copies = []
        for half in range(halves.shape[1]):
            ends = whole.at[b, :, pl.ds(half * LANES, LANES)], halves.at[slot, half]
            source, target = ends[::-1] if outward else ends
            self.copies.append(pltpu.make_async_copy(source, target, sem.at[slot, half]))

    def start(self):
        for copy in self.copies:
            copy.start()

    def wait(self):
        for copy in self.copies:
            copy.wait()


def read_row(halves, slot, t, channels, rows_local):
    at = pl.ds(t, channels, stride=rows_local)
    return jnp.concatenate([halves[slot, half, at, :] for half in range(halves.shape[1])], axis=1)


def write_row(halves, slot, t, channels, rows_local, values):
    at = pl.ds(t, channels, stride=rows_local)
    for half in range(halves.shape[1]):
        halves[slot, half, at, :] = values[:, half * LANES:(half + 1) * LANES]


class Exchange:
    def __init__(self, me, group, batch, send, recv, send_sem, recv_sem):
        self.me, self.group, self.batch = me, group, batch
        self.send, self.recv, self.send_sem, self.recv_sem = send, recv, send_sem, recv_sem

    def all_copies(self, b):
        slot = lax.rem(b, SLOTS)
        others = pl.ds(0, self.group - 1)
        return pltpu.make_async_remote_copy(
            self.send.at[slot, others], self.recv.at[b, others], self.send_sem.at[slot], self.recv_sem.at[b],
            device_id={'lat': lax.rem(self.me + 1, self.group)}, device_id_type=MESH)

    def reserve(self, b):
        @pl.when(b >= SLOTS)
        def _():
            self.all_copies(b - SLOTS).wait_send()

    def start(self, b):
        slot = lax.rem(b, SLOTS)
        self.recv[b, self.me] = self.send[slot, self.me]

        @pl.loop(1, self.group)
        def _(step):
            target = lax.rem(self.me + step, self.group)
            pltpu.make_async_remote_copy(
                self.send.at[slot, target], self.recv.at[b, self.me], self.send_sem.at[slot], self.recv_sem.at[b],
                device_id={'lat': target}, device_id_type=MESH).start()

    def arrive(self, b):
        self.all_copies(b).wait_recv()

    def drain(self):
        for b in range(max(0, self.batch - SLOTS), self.batch):
            self.all_copies(b).wait_send()


def enter(me, group):
    barrier = pltpu.get_barrier_semaphore()

    @pl.loop(1, group)
    def _(step):
        pl.semaphore_signal(barrier, inc=1, device_id={'lat': lax.rem(me + step, group)}, device_id_type=MESH)

    pl.semaphore_wait(barrier, group - 1)


def load_legendre(me, group, table_hbm, stage, sem):
    m_local = stage.shape[0]
    copies = [pltpu.make_async_copy(table_hbm.at[slot * group + me], stage.at[slot], sem) for slot in range(m_local)]
    for copy in copies:
        copy.start()
    pltpu.make_async_copy(table_hbm.at[pl.ds(0, m_local)], stage, sem).wait()


def expand_rows(stage, expanded, rows_local):
    m_local, degrees, lats = stage.shape
    row = lax.broadcasted_iota(jnp.int32, (lats, 2 * lats), 0)
    col = lax.broadcasted_iota(jnp.int32, (lats, 2 * lats), 1)
    source = col // (2 * rows_local)
    inner = col % (2 * rows_local)
    for part in range(2):
        pick = (row == source * rows_local + inner - part * rows_local) & (inner // rows_local == part)
        pick = pick.astype(F32).astype(BF16)
        for slot in range(m_local):
            expanded[slot, pl.ds(part * degrees, degrees), :] = dot(stage[slot].astype(BF16), pick, NN).astype(BF16)


def flip_rows(stage, flipped):
    for slot in range(stage.shape[0]):
        flipped[slot] = stage[slot].T.astype(BF16)


def analyse(values_at, table, turn, rows_local):
    modes = table.shape[1]
    for t in range(0, rows_local, 2):
        pair = jnp.concatenate([values_at(t), values_at(t + 1)], axis=0)
        high, low = split_halves(pair)
        out = dot(table[0], high, NT) + dot(table[0], low, NT) + dot(table[1], high, NT)
        channels = out.shape[1] // 2
        turn[pl.ds(t, modes, stride=rows_local), :] = out[:, :channels]
        turn[pl.ds(t + 1, modes, stride=rows_local), :] = out[:, channels:]


def pack_blocks(turn, send, slot):
    group, rows, lanes = send.shape[1:]
    for d in range(group):
        send[slot, d] = turn[pl.ds(d * rows, rows), :].astype(BF16)


def unpack_blocks(recv, b, turn):
    group, rows, lanes = recv.shape[1:]
    for d in range(group):
        turn[pl.ds(d * rows, rows), :] = recv[b, d].astype(F32)


def synthesise(turn, t, table, rows_local):
    modes = table.shape[1]
    spec = turn[pl.ds(t, modes, stride=rows_local), :].astype(BF16)
    return dot(spec, table[0], TN) + dot(spec, table[1], TN)


def legendre_forward(recv, b, expanded, out, rows_local):
    m_local = expanded.shape[0]
    degrees = expanded.shape[1] // 2
    group, _, lanes = recv.shape[1:]
    tile = 2 * rows_local
    for slot in range(m_local):
        rows = recv[b, :, pl.ds(slot * tile, tile), :].reshape(group * tile, lanes)
        res = dot(expanded[slot], rows, NN)
        for part in range(2):
            out[part, pl.ds(slot, degrees, stride=m_local), :] = res[part * degrees:(part + 1) * degrees]


def legendre_inverse(coef, flipped, send, slot_out, rows_local):
    m_local, lats, degrees = flipped.shape
    group = lats // rows_local
    tile = 2 * rows_local
    for slot in range(m_local):
        parts = [coef.at[part][pl.ds(slot, degrees, stride=m_local), :].astype(BF16) for part in range(2)]
        res = dot(flipped[slot], jnp.concatenate(parts, axis=1), NN)
        lanes = res.shape[1] // 2
        blocks = [res[:, part * lanes:(part + 1) * lanes].reshape(group, rows_local, lanes) for part in range(2)]
        send[slot_out, :, pl.ds(slot * tile, tile), :] = jnp.concatenate(blocks, axis=1).astype(BF16)


def gelu_slope(values):
    cumulative = 0.5 * (1.0 + lax.erf(values * math.sqrt(0.5)))
    density = jnp.exp(-0.5 * values * values) * (1.0 / math.sqrt(2.0 * math.pi))
    return cumulative + values * density


def mix_block(w_block):
    half = w_block.shape[0] // 2
    w_real = w_block[pl.ds(0, half, stride=2), :]
    w_imag = w_block[pl.ds(1, half, stride=2), :]
    top = jnp.concatenate([w_real, -w_imag], axis=1)
    bottom = jnp.concatenate([w_imag, w_real], axis=1)
    return jnp.concatenate([top, bottom], axis=0).astype(BF16)


def rows_of_degree(block, inner, m_local):
    batch = block.shape[0]
    lanes = block.shape[-1]
    parts = [block[:, part, pl.ds(inner * m_local, m_local), :].reshape(batch * m_local, lanes) for part in range(2)]
    return jnp.concatenate(parts, axis=1).astype(BF16)


def first_kernel(group, rows_local, field, table, p_fwd, coef_out, field_buf, stage, expanded, turn, send, recv,
                 coef_buf, in_sem, out_sem, p_sem, send_sem, recv_sem):
    me = lax.axis_index('lat')
    batch = field.shape[0]
    channels = field.shape[1] // rows_local

    def fetch(b):
        return Halves(field, b, field_buf, lax.rem(b, 2), in_sem)

    def put(b):
        return pltpu.make_async_copy(coef_buf.at[lax.rem(b, 2)], coef_out.at[b], out_sem.at[lax.rem(b, 2)])

    fetch(0).start()
    enter(me, group)
    swap = Exchange(me, group, batch, send, recv, send_sem, recv_sem)
    lag = 2

    def body(i, carry):
        @pl.when(i < batch)
        def _():
            @pl.when(i + 1 < batch)
            def _():
                fetch(i + 1).start()

            fetch(i).wait()
            half = lax.rem(i, 2)
            analyse(lambda t: read_row(field_buf, half, t, channels, rows_local), table, turn, rows_local)
            swap.reserve(i)
            pack_blocks(turn, send, lax.rem(i, SLOTS))
            swap.start(i)

        @pl.when(i == 0)
        def _():
            load_legendre(me, group, p_fwd, stage, p_sem)
            expand_rows(stage, expanded, rows_local)

        @pl.when(i >= lag)
        def _():
            b = i - lag
            swap.arrive(b)

            @pl.when(b >= 2)
            def _():
                put(b - 2).wait()

            legendre_forward(recv, b, expanded, coef_buf.at[lax.rem(b, 2)], rows_local)
            put(b).start()

        return carry

    lax.fori_loop(0, batch + lag, body, 0)
    swap.drain()
    put(batch - 2).wait()
    put(batch - 1).wait()


def mix_loop(w_hbm, in_hbms, bufs, w_buf, w_sem, in_sems, blocks, step):
    per = w_buf.shape[1]

    def copies(k):
        slot = lax.rem(k, 2)
        out = [pltpu.make_async_copy(w_hbm.at[pl.ds(k * per, per)], w_buf.at[slot], w_sem.at[slot])]
        for src, buf, sem in zip(in_hbms, bufs, in_sems):
            rows = buf.shape[3]
            out.append(pltpu.make_async_copy(src.at[:, :, pl.ds(k * rows, rows), :], buf.at[slot], sem.at[slot]))
        return out

    for copy in copies(0):
        copy.start()

    def body(k, carry):
        @pl.when(k + 1 < blocks)
        def _():
            for copy in copies(k + 1):
                copy.start()

        for copy in copies(k):
            copy.wait()
        step(k, lax.rem(k, 2))
        return carry

    lax.fori_loop(0, blocks, body, 0)


def second_kernel(group, rows_local, coef, w_mix, p_inv, table, grad, mixed_out, w_buf, coef_blk, mixed, stage, flipped,
                  expanded, turn, grad_buf, out_buf, send_a, recv_a, send_b, recv_b, w_sem, c_sem, in_sem, out_sem, p_sem,
                  send_a_sem, recv_a_sem, send_b_sem, recv_b_sem):
    me = lax.axis_index('lat')
    batch = grad.shape[0]
    channels = grad.shape[1] // rows_local
    m_local = stage.shape[0]
    per = w_buf.shape[1]
    degrees = stage.shape[1]

    def fetch(b):
        return Halves(grad, b, grad_buf, lax.rem(b, 2), in_sem)

    def put(b):
        return pltpu.make_async_copy(out_buf.at[lax.rem(b, 2)], mixed_out.at[b], out_sem.at[lax.rem(b, 2)])

    fetch(0).start()
    load_legendre(me, group, p_inv, stage, p_sem)
    flip_rows(stage, flipped)
    expand_rows(stage, expanded, rows_local)

    def mix(k, slot):
        for inner in range(per):
            rows = rows_of_degree(coef_blk.at[slot], inner, m_local)
            res = dot(rows, mix_block(w_buf.at[slot, inner]), NT)
            at = pl.ds(pl.multiple_of((k * per + inner) * m_local, m_local), m_local)
            for part in range(2):
                lanes = res.shape[1] // 2
                mixed[:, part, at, :] = res[:, part * lanes:(part + 1) * lanes].reshape(batch, m_local, lanes)

    mix_loop(w_mix, [coef], [coef_blk], w_buf, w_sem, [c_sem], degrees // per, mix)

    enter(me, group)
    swap_a = Exchange(me, group, batch, send_a, recv_a, send_a_sem, recv_a_sem)
    swap_b = Exchange(me, group, batch, send_b, recv_b, send_b_sem, recv_b_sem)
    lag = 2

    def body(i, carry):
        @pl.when(i < batch)
        def _():
            swap_a.reserve(i)
            legendre_inverse(mixed.at[i], flipped, send_a, lax.rem(i, SLOTS), rows_local)
            swap_a.start(i)

        @pl.when((i >= lag) & (i < batch + lag))
        def _():
            b = i - lag
            half = lax.rem(b, 2)

            @pl.when(b + 1 < batch)
            def _():
                fetch(b + 1).start()

            fetch(b).wait()
            swap_a.arrive(b)
            unpack_blocks(recv_a, b, turn)
            for t in range(rows_local):
                slope = gelu_slope(synthesise(turn, t, table, rows_local))
                given = read_row(grad_buf, half, t, channels, rows_local)
                write_row(grad_buf, half, t, channels, rows_local, given * slope)
            analyse(lambda t: read_row(grad_buf, half, t, channels, rows_local), table, turn, rows_local)
            swap_b.reserve(b)
            pack_blocks(turn, send_b, lax.rem(b, SLOTS))
            swap_b.start(b)

        @pl.when(i >= 2 * lag)
        def _():
            b = i - 2 * lag
            swap_b.arrive(b)

            @pl.when(b >= 2)
            def _():
                put(b - 2).wait()

            legendre_forward(recv_b, b, expanded, out_buf.at[lax.rem(b, 2)], rows_local)
            put(b).start()

        return carry

    lax.fori_loop(0, batch + 2 * lag, body, 0)
    swap_a.drain()
    swap_b.drain()
    put(batch - 2).wait()
    put(batch - 1).wait()


def weight_kernel(mixed, coef, w_mix, grad_w, back, w_buf, mixed_blk, coef_blk, gw_buf, back_buf, w_sem, m_sem, c_sem,
                  gw_sem, back_sem):
    per = w_buf.shape[1]
    batch = mixed.shape[0]
    degrees = w_mix.shape[0]
    m_local = mixed.shape[2] // degrees
    blocks = degrees // per

    def puts(k):
        slot = lax.rem(k, 2)
        rows = per * m_local
        return [pltpu.make_async_copy(gw_buf.at[slot], grad_w.at[pl.ds(k * per, per)], gw_sem.at[slot]),
                pltpu.make_async_copy(back_buf.at[slot], back.at[:, :, pl.ds(k * rows, rows), :], back_sem.at[slot])]

    def step(k, slot):
        @pl.when(k >= 2)
        def _():
            for copy in puts(k - 2):
                copy.wait()

        for inner in range(per):
            rows = rows_of_degree(mixed_blk.at[slot], inner, m_local)
            keep = rows_of_degree(coef_blk.at[slot], inner, m_local)
            res = dot(rows, mix_block(w_buf.at[slot, inner]), NN)
            at = pl.ds(inner * m_local, m_local)
            half = res.shape[1] // 2
            for part in range(2):
                back_buf[slot, :, part, at, :] = res[:, part * half:(part + 1) * half].reshape(batch, m_local, half)
            big = dot(rows, keep, TN)
            gw_buf[slot, inner, pl.ds(0, half, stride=2), :] = big[:half, :half] + big[half:, half:]
            gw_buf[slot, inner, pl.ds(1, half, stride=2), :] = big[half:, :half] - big[:half, half:]
        for copy in puts(k):
            copy.start()

    mix_loop(w_mix, [mixed, coef], [mixed_blk, coef_blk], w_buf, w_sem, [m_sem, c_sem], blocks, step)
    for k in (blocks - 2, blocks - 1):
        for copy in puts(k):
            copy.wait()


def last_kernel(group, rows_local, back, p_fwd, table, grad, field_out, back_buf, stage, flipped, turn, grad_buf, send, recv,
                b_sem, in_sem, out_sem, p_sem, send_sem, recv_sem):
    me = lax.axis_index('lat')
    batch = grad.shape[0]
    channels = grad.shape[1] // rows_local
    ring = grad_buf.shape[0]

    def fetch_back(b):
        return pltpu.make_async_copy(back.at[b], back_buf.at[lax.rem(b, 2)], b_sem.at[lax.rem(b, 2)])

    def fetch(b):
        return Halves(grad, b, grad_buf, lax.rem(b, ring), in_sem)

    def put(b):
        return Halves(field_out, b, grad_buf, lax.rem(b, ring), out_sem, outward=True)

    fetch_back(0).start()
    fetch(0).start()
    load_legendre(me, group, p_fwd, stage, p_sem)
    flip_rows(stage, flipped)
    enter(me, group)
    swap = Exchange(me, group, batch, send, recv, send_sem, recv_sem)
    lag = 2

    def body(i, carry):
        @pl.when(i < batch)
        def _():
            @pl.when(i + 1 < batch)
            def _():
                fetch_back(i + 1).start()

            fetch_back(i).wait()
            swap.reserve(i)
            legendre_inverse(back_buf.at[lax.rem(i, 2)], flipped, send, lax.rem(i, SLOTS), rows_local)
            swap.start(i)

        @pl.when(i >= lag)
        def _():
            b = i - lag
            half = lax.rem(b, ring)

            @pl.when(b >= ring - 1)
            def _():
                put(b - ring + 1).wait()

            @pl.when(b + 1 < batch)
            def _():
                fetch(b + 1).start()

            fetch(b).wait()
            swap.arrive(b)
            unpack_blocks(recv, b, turn)
            for t in range(rows_local):
                added = synthesise(turn, t, table, rows_local)
                given = read_row(grad_buf, half, t, channels, rows_local)
                write_row(grad_buf, half, t, channels, rows_local, given + added)
            put(b).start()

        return carry

    lax.fori_loop(0, batch + lag, body, 0)
    swap.drain()
    for b in range(batch - ring + 1, batch):
        put(b).wait()


def any_specs(n):
    return [pl.BlockSpec(memory_space=pl.ANY)] * n


def params(collective_id=None):
    if collective_id is None:
        return pltpu.CompilerParams(vmem_limit_bytes=VMEM_LIMIT)
    return pltpu.CompilerParams(collective_id=collective_id, has_side_effects=True, vmem_limit_bytes=VMEM_LIMIT)


def solution(mesh):
    group = mesh.shape['lat']
    field_spec = P('member', None, 'lat', None)

    def local_step(field_loc, grad_loc, p_fwd, p_inv, w_mix):
        batch, channels, rows_local, lon_count = field_loc.shape
        degrees, lats = p_fwd.shape[1:]
        m_local = p_fwd.shape[0] // group
        modes = group * m_local * 2
        base, gained = (two_halves(table) for table in dft_tables(group, m_local, lon_count))
        field = field_loc.reshape(batch, channels * rows_local, lon_count)
        grad = grad_loc.reshape(batch, channels * rows_local, lon_count)
        w_rows = jnp.swapaxes(w_mix, 2, 3).reshape(degrees, channels * 2, channels)
        dma, vmem = pltpu.SemaphoreType.DMA, pltpu.VMEM
        block_rows = m_local * 2 * rows_local
        coef_shape = (batch, 2, degrees * m_local, channels)
        send_t = vmem((SLOTS, group, block_rows, channels), BF16)
        recv_t = vmem((batch, group, block_rows, channels), BF16)
        turn_t = vmem((modes * rows_local, channels), F32)
        stage_t = vmem((m_local, degrees, lats), F32)
        expanded_t = vmem((m_local, 2 * degrees, 2 * lats), BF16)
        flipped_t = vmem((m_local, lats, degrees), BF16)
        pair_t = vmem((2, 2, degrees * m_local, channels), F32)
        field_t = vmem((2, lon_count // LANES, channels * rows_local, LANES), F32)
        table_spec = pl.BlockSpec(memory_space=pltpu.VMEM)
        any_spec = pl.BlockSpec(memory_space=pl.ANY)
        per = 8

        coef = pl.pallas_call(
            functools.partial(first_kernel, group, rows_local), name='first',
            out_shape=jax.ShapeDtypeStruct(coef_shape, F32),
            in_specs=[any_spec, table_spec, any_spec], out_specs=any_spec,
            scratch_shapes=[field_t, stage_t, expanded_t, turn_t, send_t, recv_t, pair_t, dma((2, 2)), dma((2,)), dma(()),
                            dma((SLOTS,)), dma((batch,))],
            compiler_params=params(0))(field, base, p_fwd)

        blk_t = vmem((2, batch, 2, per * m_local, channels), F32)
        w_t = vmem((2, per, channels * 2, channels), F32)
        mixed = pl.pallas_call(
            functools.partial(second_kernel, group, rows_local), name='second',
            out_shape=jax.ShapeDtypeStruct(coef_shape, F32),
            in_specs=[any_spec, any_spec, any_spec, table_spec, any_spec], out_specs=any_spec,
            scratch_shapes=[w_t, blk_t, vmem(coef_shape, F32), stage_t, flipped_t, expanded_t, turn_t, field_t, pair_t,
                            send_t, recv_t, send_t, recv_t, dma((2,)), dma((2,)), dma((2, 2)), dma((2,)), dma(()),
                            dma((SLOTS,)), dma((batch,)), dma((SLOTS,)), dma((batch,))],
            compiler_params=params(1))(coef, w_rows, p_inv, gained, grad)

        gw_part, back = pl.pallas_call(
            weight_kernel, name='weight',
            out_shape=[jax.ShapeDtypeStruct(w_rows.shape, F32), jax.ShapeDtypeStruct(coef_shape, F32)],
            in_specs=[any_spec] * 3, out_specs=[any_spec] * 2,
            scratch_shapes=[w_t, blk_t, blk_t, w_t, blk_t, dma((2,)), dma((2,)), dma((2,)), dma((2,)), dma((2,))],
            compiler_params=params())(mixed, coef, w_rows)
        gw_total = lax.psum(gw_part, 'lat')

        field_out = pl.pallas_call(
            functools.partial(last_kernel, group, rows_local), name='last',
            out_shape=jax.ShapeDtypeStruct(grad.shape, F32),
            in_specs=[any_spec, any_spec, table_spec, any_spec], out_specs=any_spec,
            scratch_shapes=[pair_t, stage_t, flipped_t, turn_t, vmem((3, lon_count // LANES, channels * rows_local, LANES), F32), send_t,
                            recv_t, dma((2,)), dma((3, 2)), dma((3, 2)), dma(()), dma((SLOTS,)), dma((batch,))],
            compiler_params=params(2))(back, p_fwd, base, grad)

        grad_wmix = jnp.swapaxes(gw_total.reshape(degrees, channels, 2, channels), 2, 3)
        return field_out.reshape(grad_loc.shape), grad_wmix

    return jax.shard_map(local_step, mesh=mesh, in_specs=(field_spec, field_spec, P(), P(), P()),
                         out_specs=(field_spec, P('member', None, None, None)), check_vma=False)
```

time: 1650 us -> 943 us (0.57); the launches traced: 1630 us -> 942 us
  Pallas kernels: 0 us -> 678 us
  local copies, waits for them, and re-layouts: 408 us -> 22.1 us
  matrix products: 310 us -> 0 us
  waiting for transfers between devices: 501 us -> 228 us
  blocking collectives: 231 us -> 0 us
  other arithmetic: 97.7 us -> 0 us
  starting transfers between devices: 64.4 us -> 0.04 us
    pallas_call x0 -> x4, Pallas kernels: none -> 678 us  [the longest x1 302 us: local_step(): pl.pallas_call(functools.partial(second_kernel, group, rows_local), name=...]
    all_to_all x3 -> x0, waiting for transfers between devices: 284 us -> none  [the longest x1 113 us: local_step(): back_lat = lax.all_to_all(back_own, 'lat', 2, 4, tiled=True)]
    another operation x10 -> x0, local copies, waits for them, and re-layouts: 233 us -> none  [the longest x8 220 us: synthesis(): return jnp.fft.irfft(jnp.pad(complex_spec, pad_width), n=lon_count, axis=-1)]
    another operation x11 -> x0, matrix products: 233 us -> none  [the longest x6 157 us: synthesis(): return jnp.fft.irfft(jnp.pad(complex_spec, pad_width), n=lon_count, axis=-1)]
    all_to_all x1 -> x0, blocking collectives: 231 us -> none  [local_step(): grad_four_lat = lax.all_to_all(grad_four_own, 'lat', 2, 4, tiled=True)]
    dot_general x7 -> x0, matrix products: 77.9 us -> none  [the longest x1 18.2 us: local_step(): jnp.einsum('bolsm,bilrm->losir', grad_mixed, coeffs, preferred_element_ty...]
    convert_element_type x6 -> x0, local copies, waits for them, and re-layouts: 75.3 us -> none  [the longest x2 21.4 us: local_step(): jnp.einsum('mlt,bctrm->bclrm', pw_own, four_own, preferred_element_type=j...]
    all_to_all x3 -> x0, starting transfers between devices: 64.3 us -> none  [the longest x1 28.3 us: local_step(): back_lat = lax.all_to_all(back_own, 'lat', 2, 4, tiled=True)]
  transfers between devices with their start and end apart: 4 -> 1, of which waited for: 4 -> 1; matrix products, arithmetic and copies ran while one was open for 20% -> 0% of each run, Pallas kernels for 0% -> 22%
where the time goes in v1:
time: 943 us; the launch traced here: 942 us
  Pallas kernels  678 us (72%)
  waiting for transfers between devices  228 us (24%)
  local copies, waits for them, and re-layouts  22.1 us (2%)
  between operations  14.1 us (1%)
    pallas_call x1, Pallas kernels, local_step(): pl.pallas_call(functools.partial(second_kernel, group, rows_local), name=...  302 us
    psum x1, waiting for transfers between devices, local_step(): gw_total = lax.psum(gw_part, 'lat')  228 us
    pallas_call x1, Pallas kernels, local_step(): pl.pallas_call(functools.partial(last_kernel, group, rows_local), name='l...  207 us
    pallas_call x1, Pallas kernels, local_step(): pl.pallas_call(functools.partial(first_kernel, group, rows_local), name='...  140 us
    pallas_call x1, Pallas kernels, local_step(): pl.pallas_call(weight_kernel, name='weight', out_shape=[jax.ShapeDtypeStr...  29.3 us
    unnamed x2, local copies, waits for them, and re-layouts  22.1 us
  transfers between devices with their start and end apart: 1, of which 1 were waited for; matrix products, arithmetic and copies ran while one was open for 0% of the time, Pallas kernels for 22%

profile of v1, /device:TPU:0, one launch (start us, length us, event | category | flops | bytes accessed | tf_op | source)
XLA Modules:
  0.0 942.3 jit_solution(15386096556007116293)
XLA Ops:
  7.2 0.0 all-reduce.2.cloned.1.call-start
  7.2 139.7 %first.1.coef = f32[12,2,1024,128]{3,2,1,0:T(8,128)} custom-call(f32[12,1024,256]{2,1,0:T(8,128)} %bitcast.15, bf16[2,256,256]{2,1,0:T(8,128)(2,1)} %constant.14.table, f32[128,128,128]{2,1,0:T(8,128)} %p_fwd.3), custom_call_target="tpu_custom_call" | custom-call | tf_op jit(solution)/shard_map/first/pallas_call | solution.py:539
  146.9 302.3 %second.1.mixed = f32[12,2,1024,128]{3,2,1,0:T(8,128)} custom-call(f32[12,2,1024,128]{3,2,1,0:T(8,128)} %first.1.coef, f32[128,256,128]{2,1,0:T(8,128)} %bitcast.9, f32[128,128,128]{2,1,0:T(8,128)} %p_inv.1, bf16[2,256,256]{2,1,0:T(8,128)(2,1)} %constant.21.table, f32[12,1024,256]{2,1,0:T(8,128)} %bitcast.12), custom_call_target="tpu_custom_call" | custom-call | tf_op jit(solution)/shard_map/second/pallas_call | solution.py:549
  449.2 29.3 %weight.1 = (f32[128,256,128]{2,1,0:T(8,128)}, f32[12,2,1024,128]{3,2,1,0:T(8,128)}) custom-call(f32[12,2,1024,128]{3,2,1,0:T(8,128)} %second.1.mixed, f32[12,2,1024,128]{3,2,1,0:T(8,128)} %first.1.coef, f32[128,256,128]{2,1,0:T(8,128)} %bitcast.10), custom_call_target="tpu_custom_call" | custom-call | tf_op jit(solution)/shard_map/weight/pallas_call | solution.py:558
  478.5 0.0 all-reduce.2.cloned.1.call-update
  478.5 207.0 %last.1 = f32[12,1024,256]{2,1,0:T(8,128)} custom-call(f32[12,2,1024,128]{3,2,1,0:T(8,128)} %get-tuple-element.4.back, f32[128,128,128]{2,1,0:T(8,128)} %p_fwd.3, bf16[2,256,256]{2,1,0:T(8,128)(2,1)} %constant.14.table, f32[12,1024,256]{2,1,0:T(8,128)} %bitcast.13), custom_call_target="tpu_custom_call" | custom-call | tf_op jit(solution)/shard_map/last/pallas_call | solution.py:566
  685.5 227.8 %all-reduce.2.cloned.1.call-done = f32[128,128,128,2]{2,3,1,0:T(2,128)} async-done(((f32[128,128,128,2]{2,3,1,0:T(2,128)}), f32[128,128,128,2]{2,3,1,0:T(2,128)}) %all-reduce.2.cloned.1.call-update) | async-done | bytes 16777232 | tf_op jit(solution)/shard_map/psum | solution.py:564
  913.3 10.2 %copy.11 = f32[12,128,8,256]{3,2,1,0:T(8,128)} copy(f32[12,128,8,256]{3,2,1,0:T(8,128)} %bitcast.11) | data formatting | bytes 25165824
  923.5 12.0 %copy.12 = f32[128,128,128,2]{2,3,1,0:T(2,128)} copy(f32[128,128,128,2]{2,3,1,0:T(2,128)} %all-reduce.2.cloned.1.call-done) | data formatting | bytes 33554432
Async XLA Ops:
  7.2 906.1 %all-reduce.2.cloned.1.call-start = ((), (), s32[]{:S(2)}) async-start(), calls=%async_computation | async-start | bytes 33554432 | tf_op jit(solution)/shard_map/psum | solution.py:564
Sparse Core Ops, SparseCore 0:
  478.6 434.6 all-reduce.1

commit v2 on v1

--- a/solution.py
+++ b/solution.py
@@ -392,90 +392,165 @@
     put(batch - 1).wait()
 
 
-def weight_kernel(mixed, coef, w_mix, grad_w, back, w_buf, mixed_blk, coef_blk, gw_buf, back_buf, w_sem, m_sem, c_sem,
-                  gw_sem, back_sem):
+class WeightSum:
+    def __init__(self, me, ring, sums, got, out, sems):
+        self.ring, self.sums, self.got, self.out, self.sems = ring, sums, got, out, sems
+        self.me = me
+        self.core, self.y = lax.rem(me, 2), lax.rem(me // 2, 2)
+        self.near, self.far = lax.rem(me // 4, 2), me // 8
+        self.quarter = sums.shape[1]
+        self.rows = sums.shape[2] // 2
+        self.degree = self.y * (self.quarter // 2) + self.near
+
+    def peer(self, phase):
+        step = (1, 2, 4, 8)[phase]
+        bit = (self.core, self.y, self.near, self.far)[phase]
+        return {'lat': self.me + step - 2 * step * bit}
+
+    def remote(self, phase, k, source, target, back):
+        return pltpu.make_async_remote_copy(source, target, self.sems.at[back, 0, phase, k], self.sems.at[back, 1, phase, k],
+                                            device_id=self.peer(phase), device_id_type=MESH)
+
+    def halving(self, phase, k):
+        if phase == 0:
+            source, target = self.ring.at[lax.rem(k, self.ring.shape[0]), 1 - self.core], self.sums.at[k]
+        elif phase == 1:
+            half = self.quarter // 2
+            source, target = self.sums.at[k, pl.ds((1 - self.y) * half, half)], self.got[0].at[k]
+        elif phase == 2:
+            source, target = self.sums.at[k, self.y * (self.quarter // 2) + 1 - self.near], self.got[1].at[k]
+        else:
+            at = pl.ds(pl.multiple_of((1 - self.far) * self.rows, self.rows), self.rows)
+            source, target = self.sums.at[k, self.degree, at], self.got[2].at[k]
+        return self.remote(phase, k, source, target, 0)
+
+    def absorb(self, phase, k):
+        self.halving(phase, k).wait()
+        if phase == 0:
+            self.sums[k] = self.sums[k] + self.ring[lax.rem(k, self.ring.shape[0]), self.core]
+        elif phase == 1:
+            half = self.quarter // 2
+            at = pl.ds(self.y * half, half)
+            self.sums[k, at] = self.sums[k, at] + self.got[0][k]
+        elif phase == 2:
+            self.sums[k, self.degree] = self.sums[k, self.degree] + self.got[1][k]
+        else:
+            at = self.last_rows()
+            self.sums[k, self.degree, at] = self.sums[k, self.degree, at] + self.got[2][k]
+
+    def last_rows(self):
+        return pl.ds(pl.multiple_of(self.far * self.rows, self.rows), self.rows)
+
+    def reduce_step(self, phase, k):
+        self.absorb(phase - 1, k)
+        if phase < 4:
+            self.halving(phase, k).start()
+        else:
+            self.settle(k).start()
+            self.doubling(3, k).start()
+
+    def settle(self, k):
+        at = self.last_rows()
+        degree = k * 2 * self.quarter + self.core * self.quarter + self.degree
+        return pltpu.make_async_copy(self.sums.at[k, self.degree, at], self.out.at[degree, at], self.sems.at[1, 2, 0, k])
+
+    def doubling(self, phase, k):
+        base = k * 2 * self.quarter + self.core * self.quarter
+        if phase == 3:
+            at = self.last_rows()
+            return self.remote(3, k, self.sums.at[k, self.degree, at], self.out.at[base + self.degree, at], 1)
+        if phase == 2:
+            span = pl.ds(base + self.degree, 1)
+        elif phase == 1:
+            half = self.quarter // 2
+            span = pl.ds(base + self.y * half, half)
+        else:
+            span = pl.ds(base, self.quarter)
+        return self.remote(phase, k, self.out.at[span], self.out.at[span], 1)
+
+    def gather_step(self, phase, k):
+        if phase == 2:
+            self.settle(k).wait()
+        self.doubling(phase + 1, k).wait()
+        if phase >= 0:
+            self.doubling(phase, k).start()
+
+
+def third_kernel(group, rows_local, mixed, coef, w_mix, p_fwd, table, grad, field_out, grad_w, w_buf, mixed_blk, coef_blk, ring,
+                 sums, got_a, got_b, got_c, back, stage, flipped, turn, grad_buf, send, recv, w_sem, m_sem, c_sem, gw_sem,
+                 in_sem, out_sem, p_sem, send_sem, recv_sem):
+    me = lax.axis_index('lat')
+    batch = grad.shape[0]
+    channels = grad.shape[1] // rows_local
+    depth = grad_buf.shape[0]
     per = w_buf.shape[1]
-    batch = mixed.shape[0]
     degrees = w_mix.shape[0]
-    m_local = mixed.shape[2] // degrees
+    m_local = stage.shape[0]
     blocks = degrees // per
 
-    def puts(k):
-        slot = lax.rem(k, 2)
-        rows = per * m_local
-        return [pltpu.make_async_copy(gw_buf.at[slot], grad_w.at[pl.ds(k * per, per)], gw_sem.at[slot]),
-                pltpu.make_async_copy(back_buf.at[slot], back.at[:, :, pl.ds(k * rows, rows), :], back_sem.at[slot])]
-
-    def step(k, slot):
-        @pl.when(k >= 2)
-        def _():
-            for copy in puts(k - 2):
-                copy.wait()
-
+    def fetch(b):
+        return Halves(grad, b, grad_buf, lax.rem(b, depth), in_sem)
+
+    def put(b):
+        return Halves(field_out, b, grad_buf, lax.rem(b, depth), out_sem, outward=True)
+
+    enter(me, group)
+    total = WeightSum(me, ring, sums, (got_a, got_b, got_c), grad_w, gw_sem)
+    swap = Exchange(me, group, batch, send, recv, send_sem, recv_sem)
+
+    def weigh(k, slot):
+        place = lax.rem(k, ring.shape[0])
         for inner in range(per):
             rows = rows_of_degree(mixed_blk.at[slot], inner, m_local)
             keep = rows_of_degree(coef_blk.at[slot], inner, m_local)
             res = dot(rows, mix_block(w_buf.at[slot, inner]), NN)
-            at = pl.ds(inner * m_local, m_local)
+            at = pl.ds(pl.multiple_of((k * per + inner) * m_local, m_local), m_local)
             half = res.shape[1] // 2
             for part in range(2):
-                back_buf[slot, :, part, at, :] = res[:, part * half:(part + 1) * half].reshape(batch, m_local, half)
+                back[:, part, at, :] = res[:, part * half:(part + 1) * half].reshape(batch, m_local, half)
             big = dot(rows, keep, TN)
-            gw_buf[slot, inner, pl.ds(0, half, stride=2), :] = big[:half, :half] + big[half:, half:]
-            gw_buf[slot, inner, pl.ds(1, half, stride=2), :] = big[half:, :half] - big[:half, half:]
-        for copy in puts(k):
-            copy.start()
-
-    mix_loop(w_mix, [mixed, coef], [mixed_blk, coef_blk], w_buf, w_sem, [m_sem, c_sem], blocks, step)
-    for k in (blocks - 2, blocks - 1):
-        for copy in puts(k):
-            copy.wait()
-
-
-def last_kernel(group, rows_local, back, p_fwd, table, grad, field_out, back_buf, stage, flipped, turn, grad_buf, send, recv,
-                b_sem, in_sem, out_sem, p_sem, send_sem, recv_sem):
-    me = lax.axis_index('lat')
-    batch = grad.shape[0]
-    channels = grad.shape[1] // rows_local
-    ring = grad_buf.shape[0]
-
-    def fetch_back(b):
-        return pltpu.make_async_copy(back.at[b], back_buf.at[lax.rem(b, 2)], b_sem.at[lax.rem(b, 2)])
-
-    def fetch(b):
-        return Halves(grad, b, grad_buf, lax.rem(b, ring), in_sem)
-
-    def put(b):
-        return Halves(field_out, b, grad_buf, lax.rem(b, ring), out_sem, outward=True)
-
-    fetch_back(0).start()
+            side, spot = inner // (per // 2), inner % (per // 2)
+            ring[place, side, spot, pl.ds(0, half, stride=2), :] = big[:half, :half] + big[half:, half:]
+            ring[place, side, spot, pl.ds(1, half, stride=2), :] = big[half:, :half] - big[:half, half:]
+        total.halving(0, k).start()
+
+        @pl.when(k >= 2)
+        def _():
+            total.reduce_step(1, k - 2)
+
+    mix_loop(w_mix, [mixed, coef], [mixed_blk, coef_blk], w_buf, w_sem, [m_sem, c_sem], blocks, weigh)
     fetch(0).start()
+    total.reduce_step(1, blocks - 2)
+    total.reduce_step(1, blocks - 1)
     load_legendre(me, group, p_fwd, stage, p_sem)
     flip_rows(stage, flipped)
-    enter(me, group)
-    swap = Exchange(me, group, batch, send, recv, send_sem, recv_sem)
     lag = 2
+    width = 2
 
     def body(i, carry):
         @pl.when(i < batch)
         def _():
-            @pl.when(i + 1 < batch)
+            swap.reserve(i)
+            legendre_inverse(back.at[i], flipped, send, lax.rem(i, SLOTS), rows_local)
+            swap.start(i)
+
+        steps = [(total.reduce_step, p) for p in (2, 3, 4)] + [(total.gather_step, p) for p in (2, 1, 0, -1)]
+        for late, (step, phase) in enumerate(steps):
+            for j in range(width):
+                k = (i - late) * width + j
+
+                @pl.when((k >= 0) & (k < blocks))
+                def _():
+                    step(phase, k)
+
+        @pl.when((i >= lag) & (i < batch + lag))
+        def _():
+            b = i - lag
+            half = lax.rem(b, depth)
+
+            @pl.when(b >= depth - 1)
             def _():
-                fetch_back(i + 1).start()
-
-            fetch_back(i).wait()
-            swap.reserve(i)
-            legendre_inverse(back_buf.at[lax.rem(i, 2)], flipped, send, lax.rem(i, SLOTS), rows_local)
-            swap.start(i)
-
-        @pl.when(i >= lag)
-        def _():
-            b = i - lag
-            half = lax.rem(b, ring)
-
-            @pl.when(b >= ring - 1)
-            def _():
-                put(b - ring + 1).wait()
+                put(b - depth + 1).wait()
 
             @pl.when(b + 1 < batch)
             def _():
@@ -492,9 +567,9 @@
 
         return carry
 
-    lax.fori_loop(0, batch + lag, body, 0)
+    lax.fori_loop(0, max(batch + lag, blocks // width + 6), body, 0)
     swap.drain()
-    for b in range(batch - ring + 1, batch):
+    for b in range(batch - depth + 1, batch):
         put(b).wait()
 
 
@@ -555,21 +630,20 @@
                             dma((SLOTS,)), dma((batch,)), dma((SLOTS,)), dma((batch,))],
             compiler_params=params(1))(coef, w_rows, p_inv, gained, grad)
 
-        gw_part, back = pl.pallas_call(
-            weight_kernel, name='weight',
-            out_shape=[jax.ShapeDtypeStruct(w_rows.shape, F32), jax.ShapeDtypeStruct(coef_shape, F32)],
-            in_specs=[any_spec] * 3, out_specs=[any_spec] * 2,
-            scratch_shapes=[w_t, blk_t, blk_t, w_t, blk_t, dma((2,)), dma((2,)), dma((2,)), dma((2,)), dma((2,))],
-            compiler_params=params())(mixed, coef, w_rows)
-        gw_total = lax.psum(gw_part, 'lat')
-
-        field_out = pl.pallas_call(
-            functools.partial(last_kernel, group, rows_local), name='last',
-            out_shape=jax.ShapeDtypeStruct(grad.shape, F32),
-            in_specs=[any_spec, any_spec, table_spec, any_spec], out_specs=any_spec,
-            scratch_shapes=[pair_t, stage_t, flipped_t, turn_t, vmem((3, lon_count // LANES, channels * rows_local, LANES), F32), send_t,
-                            recv_t, dma((2,)), dma((3, 2)), dma((3, 2)), dma(()), dma((SLOTS,)), dma((batch,))],
-            compiler_params=params(2))(back, p_fwd, base, grad)
+        blocks = degrees // per
+        field_out, gw_total = pl.pallas_call(
+            functools.partial(third_kernel, group, rows_local), name='third',
+            out_shape=[jax.ShapeDtypeStruct(grad.shape, F32), jax.ShapeDtypeStruct(w_rows.shape, F32)],
+            in_specs=[any_spec] * 4 + [table_spec, any_spec], out_specs=[any_spec] * 2,
+            scratch_shapes=[w_t, blk_t, blk_t, vmem((4, 2, per // 2, channels * 2, channels), F32),
+                            vmem((blocks, per // 2, channels * 2, channels), F32),
+                            vmem((blocks, per // 4, channels * 2, channels), F32),
+                            vmem((blocks, channels * 2, channels), F32), vmem((blocks, channels, channels), F32),
+                            vmem(coef_shape, F32), stage_t, flipped_t, turn_t,
+                            vmem((3, lon_count // LANES, channels * rows_local, LANES), F32), send_t, recv_t,
+                            dma((2,)), dma((2,)), dma((2,)), dma((2, 3, 4, blocks)), dma((3, 2)), dma((3, 2)), dma(()),
+                            dma((SLOTS,)), dma((batch,))],
+            compiler_params=params(2))(mixed, coef, w_rows, p_fwd, base, grad)
 
         grad_wmix = jnp.swapaxes(gw_total.reshape(degrees, channels, 2, channels), 2, 3)
         return field_out.reshape(grad_loc.shape), grad_wmix

time: 943 us -> 797 us (0.85)
  waiting for transfers between devices: 228 us -> 0 us
  Pallas kernels: 678 us -> 771 us
  between operations: 14.1 us -> 0.65 us
    psum x1 -> x0, waiting for transfers between devices: 228 us -> none  [local_step(): gw_total = lax.psum(gw_part, 'lat')]
    pallas_call x2 -> x1, Pallas kernels: 236 us -> 329 us  [local_step(): pl.pallas_call(functools.partial(third_kernel, group, rows_local), name='...]
  transfers between devices with their start and end apart: 1 -> 0, of which waited for: 1 -> 0; matrix products, arithmetic and copies ran while one was open for 0% -> 0% of each run, Pallas kernels for 22% -> 0%
where the time goes in v2:
time: 797 us; the launch traced here: 794 us
  Pallas kernels  771 us (97%)
  local copies, waits for them, and re-layouts  22.2 us (3%)
    pallas_call x1, Pallas kernels, local_step(): pl.pallas_call(functools.partial(third_kernel, group, rows_local), name='...  329 us
    pallas_call x1, Pallas kernels, local_step(): pl.pallas_call(functools.partial(second_kernel, group, rows_local), name=...  303 us
    pallas_call x1, Pallas kernels, local_step(): pl.pallas_call(functools.partial(first_kernel, group, rows_local), name='...  140 us
    unnamed x2, local copies, waits for them, and re-layouts  22.2 us

profile of v2, /device:TPU:0, one launch (start us, length us, event | category | flops | bytes accessed | tf_op | source)
XLA Modules:
  0.0 794.2 jit_solution(7644271248150387094)
XLA Ops:
  0.6 139.6 %first.1.coef = f32[12,2,1024,128]{3,2,1,0:T(8,128)} custom-call(f32[12,1024,256]{2,1,0:T(8,128)} %bitcast.14, bf16[2,256,256]{2,1,0:T(8,128)(2,1)} %constant.14.table, f32[128,128,128]{2,1,0:T(8,128)} %p_fwd.3), custom_call_target="tpu_custom_call" | custom-call | tf_op jit(solution)/shard_map/first/pallas_call | solution.py:614
  140.3 302.9 %second.1.mixed = f32[12,2,1024,128]{3,2,1,0:T(8,128)} custom-call(f32[12,2,1024,128]{3,2,1,0:T(8,128)} %first.1.coef, f32[128,256,128]{2,1,0:T(8,128)} %bitcast.9, f32[128,128,128]{2,1,0:T(8,128)} %p_inv.1, bf16[2,256,256]{2,1,0:T(8,128)(2,1)} %constant.21.table, f32[12,1024,256]{2,1,0:T(8,128)} %bitcast.11), custom_call_target="tpu_custom_call" | custom-call | tf_op jit(solution)/shard_map/second/pallas_call | solution.py:624
  443.2 328.8 %third.1 = (f32[12,1024,256]{2,1,0:T(8,128)}, f32[128,256,128]{2,1,0:T(8,128)}) custom-call(f32[12,2,1024,128]{3,2,1,0:T(8,128)} %second.1.mixed, f32[12,2,1024,128]{3,2,1,0:T(8,128)} %first.1.coef, f32[128,256,128]{2,1,0:T(8,128)} %bitcast.10, f32[128,128,128]{2,1,0:T(8,128)} %p_fwd.3, bf16[2,256,256]{2,1,0:T(8,128)(2,1)} %constant.14.table, ...), custom_call_target="tpu_custom_call" | custom-call | tf_op jit(solution)/shard_map/third/pallas_call | solution.py:634
  772.0 10.2 %copy.11 = f32[12,128,8,256]{3,2,1,0:T(8,128)} copy(f32[12,128,8,256]{3,2,1,0:T(8,128)} %bitcast.15) | data formatting | bytes 25165824
  782.2 12.0 %copy.12 = f32[128,128,128,2]{2,3,1,0:T(2,128)} copy(f32[128,128,128,2]{2,3,1,0:T(2,128)} %bitcast.13) | data formatting | bytes 33554432

commit v3 on v2

--- a/solution.py
+++ b/solution.py
@@ -497,6 +497,8 @@
     enter(me, group)
     total = WeightSum(me, ring, sums, (got_a, got_b, got_c), grad_w, gw_sem)
     swap = Exchange(me, group, batch, send, recv, send_sem, recv_sem)
+
+    early = 4
 
     def weigh(k, slot):
         place = lax.rem(k, ring.shape[0])
@@ -516,12 +518,16 @@
 
         @pl.when(k >= 2)
         def _():
-            total.reduce_step(1, k - 2)
+            total.absorb(0, k - 2)
+
+            @pl.when(k - 2 < early)
+            def _():
+                total.halving(1, k - 2).start()
 
     mix_loop(w_mix, [mixed, coef], [mixed_blk, coef_blk], w_buf, w_sem, [m_sem, c_sem], blocks, weigh)
     fetch(0).start()
-    total.reduce_step(1, blocks - 2)
-    total.reduce_step(1, blocks - 1)
+    total.absorb(0, blocks - 2)
+    total.absorb(0, blocks - 1)
     load_legendre(me, group, p_fwd, stage, p_sem)
     flip_rows(stage, flipped)
     lag = 2
@@ -533,6 +539,13 @@
             swap.reserve(i)
             legendre_inverse(back.at[i], flipped, send, lax.rem(i, SLOTS), rows_local)
             swap.start(i)
+
+        for j in range(width):
+            k = early + i * width + j
+
+            @pl.when(k < blocks)
+            def _():
+                total.halving(1, k).start()
 
         steps = [(total.reduce_step, p) for p in (2, 3, 4)] + [(total.gather_step, p) for p in (2, 1, 0, -1)]
         for late, (step, phase) in enumerate(steps):

time: 797 us -> 759 us (0.952)
  Pallas kernels: 771 us -> 732 us
    pallas_call x1, Pallas kernels: 329 us -> 290 us  [local_step(): pl.pallas_call(functools.partial(third_kernel, group, rows_local), name='...]
where the time goes in v3:
time: 759 us; the launch traced here: 755 us
  Pallas kernels  732 us (96%)
  local copies, waits for them, and re-layouts  22.2 us (3%)
    pallas_call x1, Pallas kernels, local_step(): pl.pallas_call(functools.partial(second_kernel, group, rows_local), name=...  303 us
    pallas_call x1, Pallas kernels, local_step(): pl.pallas_call(functools.partial(third_kernel, group, rows_local), name='...  290 us
    pallas_call x1, Pallas kernels, local_step(): pl.pallas_call(functools.partial(first_kernel, group, rows_local), name='...  140 us
    unnamed x2, local copies, waits for them, and re-layouts  22.2 us

profile of v3, /device:TPU:0, one launch (start us, length us, event | category | flops | bytes accessed | tf_op | source)
XLA Modules:
  0.0 755.0 jit_solution(1513260108324952701)
XLA Ops:
  0.6 139.6 %first.1.coef = f32[12,2,1024,128]{3,2,1,0:T(8,128)} custom-call(f32[12,1024,256]{2,1,0:T(8,128)} %bitcast.14, bf16[2,256,256]{2,1,0:T(8,128)(2,1)} %constant.14.table, f32[128,128,128]{2,1,0:T(8,128)} %p_fwd.3), custom_call_target="tpu_custom_call" | custom-call | tf_op jit(solution)/shard_map/first/pallas_call | solution.py:627
  140.3 302.9 %second.1.mixed = f32[12,2,1024,128]{3,2,1,0:T(8,128)} custom-call(f32[12,2,1024,128]{3,2,1,0:T(8,128)} %first.1.coef, f32[128,256,128]{2,1,0:T(8,128)} %bitcast.9, f32[128,128,128]{2,1,0:T(8,128)} %p_inv.1, bf16[2,256,256]{2,1,0:T(8,128)(2,1)} %constant.21.table, f32[12,1024,256]{2,1,0:T(8,128)} %bitcast.11), custom_call_target="tpu_custom_call" | custom-call | tf_op jit(solution)/shard_map/second/pallas_call | solution.py:637
  443.2 289.6 %third.1 = (f32[12,1024,256]{2,1,0:T(8,128)}, f32[128,256,128]{2,1,0:T(8,128)}) custom-call(f32[12,2,1024,128]{3,2,1,0:T(8,128)} %second.1.mixed, f32[12,2,1024,128]{3,2,1,0:T(8,128)} %first.1.coef, f32[128,256,128]{2,1,0:T(8,128)} %bitcast.10, f32[128,128,128]{2,1,0:T(8,128)} %p_fwd.3, bf16[2,256,256]{2,1,0:T(8,128)(2,1)} %constant.14.table, ...), custom_call_target="tpu_custom_call" | custom-call | tf_op jit(solution)/shard_map/third/pallas_call | solution.py:647
  732.8 10.2 %copy.11 = f32[12,128,8,256]{3,2,1,0:T(8,128)} copy(f32[12,128,8,256]{3,2,1,0:T(8,128)} %bitcast.15) | data formatting | bytes 25165824
  743.0 12.0 %copy.12 = f32[128,128,128,2]{2,3,1,0:T(2,128)} copy(f32[128,128,128,2]{2,3,1,0:T(2,128)} %bitcast.13) | data formatting | bytes 33554432

commit v4 on v3

--- a/solution.py
+++ b/solution.py
@@ -109,6 +109,111 @@
     def drain(self):
         for b in range(max(0, self.batch - SLOTS), self.batch):
             self.all_copies(b).wait_send()
+
+
+class BridgedExchange:
+    def __init__(self, me, group, batch, bufs, sems):
+        self.me, self.group, self.batch = me, group, batch
+        self.send, self.recv, self.bridge_send, self.bridge_recv, self.relay_send, self.flipped_far = bufs
+        self.send_sem, self.recv_sem, self.bridge_send_sem, self.bridge_recv_sem, self.relay_send_sem, self.relay_recv_sem = sems
+        self.half_size = group // 2
+        self.half = me // self.half_size
+        self.place = lax.rem(me, self.half_size)
+        self.twin = self.half_size + me - 2 * self.half_size * self.half
+        self.rows = self.send.shape[2]
+        self.late_rows = self.relay_send.shape[2]
+        self.early_rows = self.rows - self.late_rows
+        self.tile = self.late_rows // self.flipped_far.shape[0]
+        self.direct = self.early_rows // self.tile
+
+    def copy(self, source, target, send_sem, recv_sem, device):
+        return pltpu.make_async_remote_copy(source, target, send_sem, recv_sem, device_id={'lat': device},
+                                            device_id_type=MESH)
+
+    def all_direct(self, b):
+        slot = lax.rem(b, SLOTS)
+        count = (self.half_size - 1) * self.rows + self.half_size * self.early_rows
+        span = pl.ds(0, count // self.rows)
+        return self.copy(self.send.at[slot, span], self.recv.at[b, span], self.send_sem.at[slot], self.recv_sem.at[b], self.twin)
+
+    def all_relayed(self, b):
+        slot = lax.rem(b, SLOTS)
+        span, part = pl.ds(0, self.half_size - 1), pl.ds(0, self.late_rows)
+        return self.copy(self.relay_send.at[slot, span], self.recv.at[b, span, part], self.relay_send_sem.at[slot],
+                         self.relay_recv_sem.at[b], self.twin)
+
+    def bridge(self, b):
+        slot = lax.rem(b, SLOTS)
+        return self.copy(self.bridge_send.at[slot], self.bridge_recv.at[b], self.bridge_send_sem.at[slot],
+                         self.bridge_recv_sem.at[b], self.twin)
+
+    def reserve(self, b):
+        @pl.when(b >= SLOTS)
+        def _():
+            self.all_direct(b - SLOTS).wait_send()
+            self.bridge(b - SLOTS).wait_send()
+
+    def start(self, b):
+        slot = lax.rem(b, SLOTS)
+        self.bridge(b).start()
+        early = pl.ds(0, self.early_rows)
+
+        @pl.loop(0, self.half_size)
+        def _(step):
+            target = (1 - self.half) * self.half_size + lax.rem(self.place + step, self.half_size)
+            self.copy(self.send.at[slot, target, early], self.recv.at[b, self.me, early], self.send_sem.at[slot],
+                      self.recv_sem.at[b], target).start()
+
+        @pl.loop(1, self.half_size)
+        def _(step):
+            target = self.half * self.half_size + lax.rem(self.place + step, self.half_size)
+            self.copy(self.send.at[slot, target], self.recv.at[b, self.me], self.send_sem.at[slot], self.recv_sem.at[b],
+                      target).start()
+
+        self.recv[b, self.me] = self.send[slot, self.me]
+
+    def relay(self, b):
+        slot = lax.rem(b, SLOTS)
+
+        @pl.when(b >= SLOTS)
+        def _():
+            self.all_relayed(b - SLOTS).wait_send()
+
+        self.bridge(b).wait_recv()
+        lats, degrees = self.flipped_far.shape[1:]
+        own = pl.ds(pl.multiple_of(self.half * (lats // 2), lats // 2), lats // 2)
+        at = 0
+        for late in range(self.flipped_far.shape[0]):
+            first = (self.direct + late) * self.group
+            count = degrees - first
+            parts = []
+            for part in range(2):
+                rows = self.bridge_recv[b, part, pl.ds(at, count), :]
+                parts.append(jnp.concatenate([jnp.zeros((first, rows.shape[1]), BF16), rows], axis=0))
+            at += count
+            res = dot(self.flipped_far[late, own, :], jnp.concatenate(parts, axis=1), NN)
+            lanes = res.shape[1] // 2
+            blocks = [res[:, part * lanes:(part + 1) * lanes].reshape(self.half_size, self.tile // 2, lanes) for part in range(2)]
+            self.relay_send[slot, :, pl.ds(late * self.tile, self.tile), :] = jnp.concatenate(blocks, axis=1).astype(BF16)
+        late_at = pl.ds(self.early_rows, self.late_rows)
+
+        @pl.loop(1, self.half_size)
+        def _(step):
+            place = lax.rem(self.place + step, self.half_size)
+            self.copy(self.relay_send.at[slot, place], self.recv.at[b, self.twin, late_at], self.relay_send_sem.at[slot],
+                      self.relay_recv_sem.at[b], self.half * self.half_size + place).start()
+
+        self.recv[b, self.twin, late_at] = self.relay_send[slot, self.place]
+
+    def arrive(self, b):
+        self.all_direct(b).wait_recv()
+        self.all_relayed(b).wait_recv()
+
+    def drain(self):
+        for b in range(max(0, self.batch - SLOTS), self.batch):
+            self.all_direct(b).wait_send()
+            self.bridge(b).wait_send()
+            self.all_relayed(b).wait_send()
 
 
 def enter(me, group):
@@ -142,6 +247,16 @@
             expanded[slot, pl.ds(part * degrees, degrees), :] = dot(stage[slot].astype(BF16), pick, NN).astype(BF16)
 
 
+def flip_far(swap, table_hbm, stage, sem):
+    late = swap.flipped_far.shape[0]
+    copies = [pltpu.make_async_copy(table_hbm.at[(swap.direct + n) * swap.group + swap.twin], stage.at[n], sem) for n in range(late)]
+    for copy in copies:
+        copy.start()
+    pltpu.make_async_copy(table_hbm.at[pl.ds(0, late)], stage.at[pl.ds(0, late)], sem).wait()
+    for n in range(late):
+        swap.flipped_far[n] = stage[n].T.astype(BF16)
+
+
 def flip_rows(stage, flipped):
     for slot in range(stage.shape[0]):
         flipped[slot] = stage[slot].T.astype(BF16)
@@ -188,12 +303,19 @@
             out[part, pl.ds(slot, degrees, stride=m_local), :] = res[part * degrees:(part + 1) * degrees]
 
 
-def legendre_inverse(coef, flipped, send, slot_out, rows_local):
+def legendre_inverse(coef, flipped, swap, slot_out, rows_local):
     m_local, lats, degrees = flipped.shape
+    send = swap.send
+    at = 0
     group = lats // rows_local
     tile = 2 * rows_local
     for slot in range(m_local):
         parts = [coef.at[part][pl.ds(slot, degrees, stride=m_local), :].astype(BF16) for part in range(2)]
+        if slot >= swap.direct:
+            first = slot * group
+            for part in range(2):
+                swap.bridge_send[slot_out, part, pl.ds(at, degrees - first), :] = parts[part][first:]
+            at += degrees - first
         res = dot(flipped[slot], jnp.concatenate(parts, axis=1), NN)
         lanes = res.shape[1] // 2
         blocks = [res[:, part * lanes:(part + 1) * lanes].reshape(group, rows_local, lanes) for part in range(2)]
@@ -307,8 +429,8 @@
 
 
 def second_kernel(group, rows_local, coef, w_mix, p_inv, table, grad, mixed_out, w_buf, coef_blk, mixed, stage, flipped,
-                  expanded, turn, grad_buf, out_buf, send_a, recv_a, send_b, recv_b, w_sem, c_sem, in_sem, out_sem, p_sem,
-                  send_a_sem, recv_a_sem, send_b_sem, recv_b_sem):
+                  expanded, turn, grad_buf, out_buf, bridged, send_b, recv_b, w_sem, c_sem, in_sem, out_sem, p_sem,
+                  bridged_sems, send_b_sem, recv_b_sem):
     me = lax.axis_index('lat')
     batch = grad.shape[0]
     channels = grad.shape[1] // rows_local
@@ -323,9 +445,11 @@
         return pltpu.make_async_copy(out_buf.at[lax.rem(b, 2)], mixed_out.at[b], out_sem.at[lax.rem(b, 2)])
 
     fetch(0).start()
+    swap_a = BridgedExchange(me, group, batch, bridged, bridged_sems)
     load_legendre(me, group, p_inv, stage, p_sem)
     flip_rows(stage, flipped)
     expand_rows(stage, expanded, rows_local)
+    flip_far(swap_a, p_inv, stage, p_sem)
 
     def mix(k, slot):
         for inner in range(per):
@@ -339,16 +463,19 @@
     mix_loop(w_mix, [coef], [coef_blk], w_buf, w_sem, [c_sem], degrees // per, mix)
 
     enter(me, group)
-    swap_a = Exchange(me, group, batch, send_a, recv_a, send_a_sem, recv_a_sem)
     swap_b = Exchange(me, group, batch, send_b, recv_b, send_b_sem, recv_b_sem)
-    lag = 2
+    lag, lag_b = 2, 2
 
     def body(i, carry):
         @pl.when(i < batch)
         def _():
             swap_a.reserve(i)
-            legendre_inverse(mixed.at[i], flipped, send_a, lax.rem(i, SLOTS), rows_local)
+            legendre_inverse(mixed.at[i], flipped, swap_a, lax.rem(i, SLOTS), rows_local)
             swap_a.start(i)
+
+        @pl.when((i >= 1) & (i < batch + 1))
+        def _():
+            swap_a.relay(i - 1)
 
         @pl.when((i >= lag) & (i < batch + lag))
         def _():
@@ -361,7 +488,7 @@
 
             fetch(b).wait()
             swap_a.arrive(b)
-            unpack_blocks(recv_a, b, turn)
+            unpack_blocks(swap_a.recv, b, turn)
             for t in range(rows_local):
                 slope = gelu_slope(synthesise(turn, t, table, rows_local))
                 given = read_row(grad_buf, half, t, channels, rows_local)
@@ -371,9 +498,9 @@
             pack_blocks(turn, send_b, lax.rem(b, SLOTS))
             swap_b.start(b)
 
-        @pl.when(i >= 2 * lag)
-        def _():
-            b = i - 2 * lag
+        @pl.when(i >= lag + lag_b)
+        def _():
+            b = i - lag - lag_b
             swap_b.arrive(b)
 
             @pl.when(b >= 2)
@@ -385,7 +512,7 @@
 
         return carry
 
-    lax.fori_loop(0, batch + 2 * lag, body, 0)
+    lax.fori_loop(0, batch + lag + lag_b, body, 0)
     swap_a.drain()
     swap_b.drain()
     put(batch - 2).wait()
@@ -477,8 +604,8 @@
 
 
 def third_kernel(group, rows_local, mixed, coef, w_mix, p_fwd, table, grad, field_out, grad_w, w_buf, mixed_blk, coef_blk, ring,
-                 sums, got_a, got_b, got_c, back, stage, flipped, turn, grad_buf, send, recv, w_sem, m_sem, c_sem, gw_sem,
-                 in_sem, out_sem, p_sem, send_sem, recv_sem):
+                 sums, got_a, got_b, got_c, back, stage, flipped, turn, grad_buf, bridged, w_sem, m_sem, c_sem, gw_sem,
+                 in_sem, out_sem, p_sem, bridged_sems):
     me = lax.axis_index('lat')
     batch = grad.shape[0]
     channels = grad.shape[1] // rows_local
@@ -496,7 +623,7 @@
 
     enter(me, group)
     total = WeightSum(me, ring, sums, (got_a, got_b, got_c), grad_w, gw_sem)
-    swap = Exchange(me, group, batch, send, recv, send_sem, recv_sem)
+    swap = BridgedExchange(me, group, batch, bridged, bridged_sems)
 
     early = 4
 
@@ -530,6 +657,7 @@
     total.absorb(0, blocks - 1)
     load_legendre(me, group, p_fwd, stage, p_sem)
     flip_rows(stage, flipped)
+    flip_far(swap, p_fwd, stage, p_sem)
     lag = 2
     width = 2
 
@@ -537,8 +665,12 @@
         @pl.when(i < batch)
         def _():
             swap.reserve(i)
-            legendre_inverse(back.at[i], flipped, send, lax.rem(i, SLOTS), rows_local)
+            legendre_inverse(back.at[i], flipped, swap, lax.rem(i, SLOTS), rows_local)
             swap.start(i)
+
+        @pl.when((i >= 1) & (i < batch + 1))
+        def _():
+            swap.relay(i - 1)
 
         for j in range(width):
             k = early + i * width + j
@@ -571,7 +703,7 @@
 
             fetch(b).wait()
             swap.arrive(b)
-            unpack_blocks(recv, b, turn)
+            unpack_blocks(swap.recv, b, turn)
             for t in range(rows_local):
                 added = synthesise(turn, t, table, rows_local)
                 given = read_row(grad_buf, half, t, channels, rows_local)
@@ -623,6 +755,12 @@
         table_spec = pl.BlockSpec(memory_space=pltpu.VMEM)
         any_spec = pl.BlockSpec(memory_space=pl.ANY)
         per = 8
+        late = sum(degrees - slot * group < lats // 2 for slot in range(m_local))
+        far_rows = sum(degrees - slot * group for slot in range(m_local - late, m_local))
+        late_rows = late * 2 * rows_local
+        bridged_t = (send_t, recv_t, vmem((SLOTS, 2, far_rows, channels), BF16), vmem((batch, 2, far_rows, channels), BF16),
+                     vmem((SLOTS, group // 2, late_rows, channels), BF16), vmem((late, lats, degrees), BF16))
+        bridged_sems = (dma((SLOTS,)), dma((batch,))) * 3
 
         coef = pl.pallas_call(
             functools.partial(first_kernel, group, rows_local), name='first',
@@ -639,8 +777,8 @@
             out_shape=jax.ShapeDtypeStruct(coef_shape, F32),
             in_specs=[any_spec, any_spec, any_spec, table_spec, any_spec], out_specs=any_spec,
             scratch_shapes=[w_t, blk_t, vmem(coef_shape, F32), stage_t, flipped_t, expanded_t, turn_t, field_t, pair_t,
-                            send_t, recv_t, send_t, recv_t, dma((2,)), dma((2,)), dma((2, 2)), dma((2,)), dma(()),
-                            dma((SLOTS,)), dma((batch,)), dma((SLOTS,)), dma((batch,))],
+                            bridged_t, send_t, recv_t, dma((2,)), dma((2,)), dma((2, 2)), dma((2,)), dma(()),
+                            bridged_sems, dma((SLOTS,)), dma((batch,))],
             compiler_params=params(1))(coef, w_rows, p_inv, gained, grad)
 
         blocks = degrees // per
@@ -653,9 +791,9 @@
                             vmem((blocks, per // 4, channels * 2, channels), F32),
                             vmem((blocks, channels * 2, channels), F32), vmem((blocks, channels, channels), F32),
                             vmem(coef_shape, F32), stage_t, flipped_t, turn_t,
-                            vmem((3, lon_count // LANES, channels * rows_local, LANES), F32), send_t, recv_t,
+                            vmem((3, lon_count // LANES, channels * rows_local, LANES), F32), bridged_t,
                             dma((2,)), dma((2,)), dma((2,)), dma((2, 3, 4, blocks)), dma((3, 2)), dma((3, 2)), dma(()),
-                            dma((SLOTS,)), dma((batch,))],
+                            bridged_sems],
             compiler_params=params(2))(mixed, coef, w_rows, p_fwd, base, grad)
 
         grad_wmix = jnp.swapaxes(gw_total.reshape(degrees, channels, 2, channels), 2, 3)

time: 759 us -> 733 us (0.966)
  Pallas kernels: 732 us -> 709 us
    pallas_call x1, Pallas kernels: 303 us -> 277 us  [local_step(): pl.pallas_call(functools.partial(second_kernel, group, rows_local), name=...]
where the time goes in v4:
time: 733 us; the launch traced here: 732 us
  Pallas kernels  709 us (97%)
  local copies, waits for them, and re-layouts  22.2 us (3%)
    pallas_call x1, Pallas kernels, local_step(): pl.pallas_call(functools.partial(third_kernel, group, rows_local), name='...  292 us
    pallas_call x1, Pallas kernels, local_step(): pl.pallas_call(functools.partial(second_kernel, group, rows_local), name=...  277 us
    pallas_call x1, Pallas kernels, local_step(): pl.pallas_call(functools.partial(first_kernel, group, rows_local), name='...  140 us
    unnamed x2, local copies, waits for them, and re-layouts  22.2 us

profile of v4, /device:TPU:0, one launch (start us, length us, event | category | flops | bytes accessed | tf_op | source)
XLA Modules:
  0.0 731.7 jit_solution(13180402155640077769)
XLA Ops:
  0.6 139.6 %first.1.coef = f32[12,2,1024,128]{3,2,1,0:T(8,128)} custom-call(f32[12,1024,256]{2,1,0:T(8,128)} %bitcast.14, bf16[2,256,256]{2,1,0:T(8,128)(2,1)} %constant.14.table, f32[128,128,128]{2,1,0:T(8,128)} %p_fwd.3), custom_call_target="tpu_custom_call" | custom-call | tf_op jit(solution)/shard_map/first/pallas_call | solution.py:765
  140.3 277.0 %second.1.mixed = f32[12,2,1024,128]{3,2,1,0:T(8,128)} custom-call(f32[12,2,1024,128]{3,2,1,0:T(8,128)} %first.1.coef, f32[128,256,128]{2,1,0:T(8,128)} %bitcast.9, f32[128,128,128]{2,1,0:T(8,128)} %p_inv.1, bf16[2,256,256]{2,1,0:T(8,128)(2,1)} %constant.21.table, f32[12,1024,256]{2,1,0:T(8,128)} %bitcast.11), custom_call_target="tpu_custom_call" | custom-call | tf_op jit(solution)/shard_map/second/pallas_call | solution.py:775
  417.3 292.3 %third.1 = (f32[12,1024,256]{2,1,0:T(8,128)}, f32[128,256,128]{2,1,0:T(8,128)}) custom-call(f32[12,2,1024,128]{3,2,1,0:T(8,128)} %second.1.mixed, f32[12,2,1024,128]{3,2,1,0:T(8,128)} %first.1.coef, f32[128,256,128]{2,1,0:T(8,128)} %bitcast.10, f32[128,128,128]{2,1,0:T(8,128)} %p_fwd.3, bf16[2,256,256]{2,1,0:T(8,128)(2,1)} %constant.14.table, ...), custom_call_target="tpu_custom_call" | custom-call | tf_op jit(solution)/shard_map/third/pallas_call | solution.py:785
  709.6 10.2 %copy.11 = f32[12,128,8,256]{3,2,1,0:T(8,128)} copy(f32[12,128,8,256]{3,2,1,0:T(8,128)} %bitcast.15) | data formatting | bytes 25165824
  719.7 12.0 %copy.12 = f32[128,128,128,2]{2,3,1,0:T(2,128)} copy(f32[128,128,128,2]{2,3,1,0:T(2,128)} %bitcast.13) | data formatting | bytes 33554432

commit v5 on v4

--- a/solution.py
+++ b/solution.py
@@ -216,6 +216,80 @@
             self.all_relayed(b).wait_send()
 
 
+class Share:
+    def __init__(self, me, group, batch, send, message, out, sems):
+        self.batch, self.send, self.message, self.out = batch, send, message, out
+        self.send_sem, self.recv_sem, self.local_sem = sems
+        self.size = group // 2
+        self.base = me // self.size * self.size
+        self.place = lax.rem(me, self.size)
+
+    def rank(self, place):
+        return place // 4 + 2 * (lax.rem(place, 4) // 2) + 4 * lax.rem(place, 2)
+
+    def copy(self, slot, source, b, target, place):
+        return pltpu.make_async_remote_copy(
+            self.send.at[slot, source], self.out.at[b, target], self.send_sem.at[slot], self.recv_sem.at[b],
+            device_id={'lat': self.base + place}, device_id_type=MESH)
+
+    def every(self, b):
+        span = pl.ds(0, self.size - 1)
+        return self.copy(lax.rem(b, SLOTS), span, b, span, lax.rem(self.place + 1, self.size))
+
+    def keep(self, b):
+        slot = lax.rem(b, SLOTS)
+        return pltpu.make_async_copy(self.send.at[slot, self.rank(self.place)], self.out.at[b, self.place],
+                                     self.local_sem.at[slot])
+
+    def give(self, b, coef):
+        slot_b = lax.rem(b, SLOTS)
+
+        @pl.when(b >= SLOTS)
+        def _():
+            self.every(b - SLOTS).wait_send()
+            self.keep(b - SLOTS).wait()
+
+        size = self.size
+        m_local = size
+        tile = 2 * size
+
+        def rows(part, slot, rank, first, count):
+            return coef[part, pl.ds((first * size + rank) * m_local + slot, count, stride=size * m_local), :]
+
+        for rank in range(size):
+            for part in range(2):
+                for pair in range(m_local // 2):
+                    block = rows(part, pair, rank, 0, tile)
+                    if pair:
+                        block = block + rows(part, m_local - pair, rank, 2 * (m_local - pair), tile)
+                    self.message[rank, pl.ds((part * (m_local // 2) + pair) * tile, tile), :] = block
+                self.message[rank, pl.ds(m_local * tile + part * size, size), :] = rows(part, m_local // 2, rank, size, size)
+        for rank in range(size):
+            self.send[slot_b, rank] = self.message[rank].astype(BF16)
+        self.keep(b).start()
+
+        @pl.loop(1, size)
+        def _(step):
+            place = lax.rem(self.place + step, size)
+            self.copy(slot_b, self.rank(place), b, self.place, place).start()
+
+    def drain(self):
+        for b in range(max(0, self.batch - SLOTS), self.batch):
+            self.every(b).wait_send()
+            self.keep(b).wait()
+
+        @pl.loop(0, self.batch)
+        def _(b):
+            self.every(b).wait_recv()
+
+
+def clear_after(coef, degrees_rows):
+    slots, parts, rows, lanes = coef.shape
+    for slot in range(slots):
+        for part in range(parts):
+            coef[slot, part, pl.ds(degrees_rows, rows - degrees_rows), :] = jnp.zeros((rows - degrees_rows, lanes), F32)
+
+
 def enter(me, group):
     barrier = pltpu.get_barrier_semaphore()
 
@@ -344,8 +418,8 @@
     return jnp.concatenate(parts, axis=1).astype(BF16)
 
 
-def first_kernel(group, rows_local, field, table, p_fwd, coef_out, field_buf, stage, expanded, turn, send, recv,
-                 coef_buf, in_sem, out_sem, p_sem, send_sem, recv_sem):
+def first_kernel(group, rows_local, field, table, p_fwd, coef_out, shared, field_buf, stage, expanded, turn, send, recv,
+                 coef_buf, share_bufs, in_sem, out_sem, p_sem, send_sem, recv_sem, share_sems):
     me = lax.axis_index('lat')
     batch = field.shape[0]
     channels = field.shape[1] // rows_local
@@ -354,10 +428,13 @@
         return Halves(field, b, field_buf, lax.rem(b, 2), in_sem)
 
     def put(b):
-        return pltpu.make_async_copy(coef_buf.at[lax.rem(b, 2)], coef_out.at[b], out_sem.at[lax.rem(b, 2)])
+        whole = pl.ds(0, coef_out.shape[2])
+        return pltpu.make_async_copy(coef_buf.at[lax.rem(b, 2), :, whole], coef_out.at[b], out_sem.at[lax.rem(b, 2)])
 
     fetch(0).start()
     enter(me, group)
+    share = Share(me, group, batch, *share_bufs, shared, share_sems)
+    clear_after(coef_buf, coef_out.shape[2])
     swap = Exchange(me, group, batch, send, recv, send_sem, recv_sem)
     lag = 2
 
@@ -391,11 +468,13 @@
 
             legendre_forward(recv, b, expanded, coef_buf.at[lax.rem(b, 2)], rows_local)
             put(b).start()
+            share.give(b, coef_buf.at[lax.rem(b, 2)])
 
         return carry
 
     lax.fori_loop(0, batch + lag, body, 0)
     swap.drain()
+    share.drain()
     put(batch - 2).wait()
     put(batch - 1).wait()
 
@@ -428,9 +507,9 @@
     lax.fori_loop(0, blocks, body, 0)
 
 
-def second_kernel(group, rows_local, coef, w_mix, p_inv, table, grad, mixed_out, w_buf, coef_blk, mixed, stage, flipped,
-                  expanded, turn, grad_buf, out_buf, bridged, send_b, recv_b, w_sem, c_sem, in_sem, out_sem, p_sem,
-                  bridged_sems, send_b_sem, recv_b_sem):
+def second_kernel(group, rows_local, coef, w_mix, p_inv, table, grad, mixed_out, shared, w_buf, coef_blk, mixed, stage,
+                  flipped, expanded, turn, grad_buf, out_buf, bridged, send_b, recv_b, share_bufs, w_sem, c_sem, in_sem, out_sem,
+                  p_sem, bridged_sems, send_b_sem, recv_b_sem, share_sems):
     me = lax.axis_index('lat')
     batch = grad.shape[0]
     channels = grad.shape[1] // rows_local
@@ -442,7 +521,8 @@
         return Halves(grad, b, grad_buf, lax.rem(b, 2), in_sem)
 
     def put(b):
-        return pltpu.make_async_copy(out_buf.at[lax.rem(b, 2)], mixed_out.at[b], out_sem.at[lax.rem(b, 2)])
+        whole = pl.ds(0, mixed_out.shape[2])
+        return pltpu.make_async_copy(out_buf.at[lax.rem(b, 2), :, whole], mixed_out.at[b], out_sem.at[lax.rem(b, 2)])
 
     fetch(0).start()
     swap_a = BridgedExchange(me, group, batch, bridged, bridged_sems)
@@ -450,6 +530,8 @@
     flip_rows(stage, flipped)
     expand_rows(stage, expanded, rows_local)
     flip_far(swap_a, p_inv, stage, p_sem)
+    share = Share(me, group, batch, *share_bufs, shared, share_sems)
+    clear_after(out_buf, mixed_out.shape[2])
 
     def mix(k, slot):
         for inner in range(per):
@@ -509,91 +591,56 @@
 
             legendre_forward(recv_b, b, expanded, out_buf.at[lax.rem(b, 2)], rows_local)
             put(b).start()
+            share.give(b, out_buf.at[lax.rem(b, 2)])
 
         return carry
 
     lax.fori_loop(0, batch + lag + lag_b, body, 0)
     swap_a.drain()
     swap_b.drain()
+    share.drain()
     put(batch - 2).wait()
     put(batch - 1).wait()
 
 
 class WeightSum:
-    def __init__(self, me, ring, sums, got, out, sems):
-        self.ring, self.sums, self.got, self.out, self.sems = ring, sums, got, out, sems
-        self.me = me
+    def __init__(self, me, group, sums, got, out, sems):
+        self.me, self.sums, self.got, self.out, self.sems = me, sums, got, out, sems
         self.core, self.y = lax.rem(me, 2), lax.rem(me // 2, 2)
-        self.near, self.far = lax.rem(me // 4, 2), me // 8
-        self.quarter = sums.shape[1]
-        self.rows = sums.shape[2] // 2
-        self.degree = self.y * (self.quarter // 2) + self.near
+        self.near, self.far = lax.rem(me // 4, 2), me // (group // 2)
+        self.rank = self.near + 2 * self.y + 4 * self.core
 
     def peer(self, phase):
         step = (1, 2, 4, 8)[phase]
         bit = (self.core, self.y, self.near, self.far)[phase]
         return {'lat': self.me + step - 2 * step * bit}
 
-    def remote(self, phase, k, source, target, back):
-        return pltpu.make_async_remote_copy(source, target, self.sems.at[back, 0, phase, k], self.sems.at[back, 1, phase, k],
+    def remote(self, phase, k, source, target, stage):
+        return pltpu.make_async_remote_copy(source, target, self.sems.at[0, stage, k], self.sems.at[1, stage, k],
                                             device_id=self.peer(phase), device_id_type=MESH)
 
-    def halving(self, phase, k):
-        if phase == 0:
-            source, target = self.ring.at[lax.rem(k, self.ring.shape[0]), 1 - self.core], self.sums.at[k]
-        elif phase == 1:
-            half = self.quarter // 2
-            source, target = self.sums.at[k, pl.ds((1 - self.y) * half, half)], self.got[0].at[k]
-        elif phase == 2:
-            source, target = self.sums.at[k, self.y * (self.quarter // 2) + 1 - self.near], self.got[1].at[k]
-        else:
-            at = pl.ds(pl.multiple_of((1 - self.far) * self.rows, self.rows), self.rows)
-            source, target = self.sums.at[k, self.degree, at], self.got[2].at[k]
-        return self.remote(phase, k, source, target, 0)
-
-    def absorb(self, phase, k):
-        self.halving(phase, k).wait()
-        if phase == 0:
-            self.sums[k] = self.sums[k] + self.ring[lax.rem(k, self.ring.shape[0]), self.core]
-        elif phase == 1:
-            half = self.quarter // 2
-            at = pl.ds(self.y * half, half)
-            self.sums[k, at] = self.sums[k, at] + self.got[0][k]
-        elif phase == 2:
-            self.sums[k, self.degree] = self.sums[k, self.degree] + self.got[1][k]
-        else:
-            at = self.last_rows()
-            self.sums[k, self.degree, at] = self.sums[k, self.degree, at] + self.got[2][k]
-
-    def last_rows(self):
-        return pl.ds(pl.multiple_of(self.far * self.rows, self.rows), self.rows)
-
-    def reduce_step(self, phase, k):
-        self.absorb(phase - 1, k)
-        if phase < 4:
-            self.halving(phase, k).start()
-        else:
-            self.settle(k).start()
-            self.doubling(3, k).start()
+    def halving(self, k):
+        return self.remote(3, k, self.sums.at[2 * k + 1 - self.far], self.got.at[k], 4)
 
     def settle(self, k):
-        at = self.last_rows()
-        degree = k * 2 * self.quarter + self.core * self.quarter + self.degree
-        return pltpu.make_async_copy(self.sums.at[k, self.degree, at], self.out.at[degree, at], self.sems.at[1, 2, 0, k])
+        mine = 2 * k + self.far
+        return pltpu.make_async_copy(self.sums.at[mine], self.out.at[mine, self.rank], self.sems.at[0, 5, k])
 
     def doubling(self, phase, k):
-        base = k * 2 * self.quarter + self.core * self.quarter
         if phase == 3:
-            at = self.last_rows()
-            return self.remote(3, k, self.sums.at[k, self.degree, at], self.out.at[base + self.degree, at], 1)
-        if phase == 2:
-            span = pl.ds(base + self.degree, 1)
-        elif phase == 1:
-            half = self.quarter // 2
-            span = pl.ds(base + self.y * half, half)
-        else:
-            span = pl.ds(base, self.quarter)
-        return self.remote(phase, k, self.out.at[span], self.out.at[span], 1)
+            mine = 2 * k + self.far
+            return self.remote(3, k, self.sums.at[mine], self.out.at[mine, self.rank], 3)
+        width = (4, 2, 1)[phase]
+        first = (4 * self.core, 4 * self.core + 2 * self.y, self.rank)[phase]
+        span = self.out.at[pl.ds(2 * k, 2), pl.ds(first, width)]
+        return self.remote(phase, k, span, span, phase)
+
+    def reduce_step(self, k):
+        self.halving(k).wait()
+        mine = 2 * k + self.far
+        self.sums[mine] = self.sums[mine] + self.got[k]
+        self.settle(k).start()
+        self.doubling(3, k).start()
 
     def gather_step(self, phase, k):
         if phase == 2:
@@ -603,9 +650,41 @@
             self.doubling(phase, k).start()
 
 
-def third_kernel(group, rows_local, mixed, coef, w_mix, p_fwd, table, grad, field_out, grad_w, w_buf, mixed_blk, coef_blk, ring,
-                 sums, got_a, got_b, got_c, back, stage, flipped, turn, grad_buf, bridged, w_sem, m_sem, c_sem, gw_sem,
-                 in_sem, out_sem, p_sem, bridged_sems):
+def shared_place(part, slot, step, m_local):
+    tile = 2 * m_local
+    if slot == m_local // 2:
+        return m_local * tile + part * m_local + step - m_local
+    pair = min(slot, m_local - slot) if slot else 0
+    shift = 0 if slot < m_local // 2 else 2 * slot
+    return (part * (m_local // 2) + pair) * tile + step - shift
+
+
+def weigh(shared, batch_rows, sums, m_local):
+    block_rows = shared.shape[1] // batch_rows
+
+    @pl.loop(0, sums.shape[0])
+    def _(step):
+        sides = []
+        for which in range(2):
+            slots = []
+            for slot in range(m_local):
+                used = step >= 2 * slot
+                parts = []
+                for part in range(2):
+                    place = jnp.where(used, shared_place(part, slot, step, m_local), 0)
+                    rows = shared[which, pl.ds(place, batch_rows, stride=block_rows), :]
+                    parts.append(jnp.where(used, rows, 0.0))
+                slots.append(jnp.concatenate(parts, axis=1))
+            sides.append(jnp.concatenate(slots, axis=0).astype(BF16))
+        big = dot(sides[0], sides[1], TN)
+        half = big.shape[0] // 2
+        sums[step, pl.ds(0, half, stride=2), :] = big[:half, :half] + big[half:, half:]
+        sums[step, pl.ds(1, half, stride=2), :] = big[half:, :half] - big[:half, half:]
+
+
+def third_kernel(group, rows_local, mixed, shared_mixed, shared_coef, w_mix, p_fwd, table, grad, field_out, grad_w, w_buf,
+                 mixed_blk, shared_half, shared, sums, got, back, stage, flipped, turn, grad_buf, bridged, w_sem, m_sem, s_sem,
+                 gw_sem, in_sem, out_sem, p_sem, bridged_sems):
     me = lax.axis_index('lat')
     batch = grad.shape[0]
     channels = grad.shape[1] // rows_local
@@ -613,7 +692,7 @@
     per = w_buf.shape[1]
     degrees = w_mix.shape[0]
     m_local = stage.shape[0]
-    blocks = degrees // per
+    sources = shared_mixed.shape[1]
 
     def fetch(b):
         return Halves(grad, b, grad_buf, lax.rem(b, depth), in_sem)
@@ -621,45 +700,47 @@
     def put(b):
         return Halves(field_out, b, grad_buf, lax.rem(b, depth), out_sem, outward=True)
 
+    def fetch_shared(which, b):
+        return pltpu.make_async_copy((shared_mixed, shared_coef)[which].at[b], shared_half.at[which, b], s_sem.at[which, b])
+
+    for which in range(2):
+        @pl.loop(0, batch)
+        def _(b):
+            fetch_shared(which, b).start()
+
     enter(me, group)
-    total = WeightSum(me, ring, sums, (got_a, got_b, got_c), grad_w, gw_sem)
+    total = WeightSum(me, group, sums, got, grad_w, gw_sem)
     swap = BridgedExchange(me, group, batch, bridged, bridged_sems)
 
-    early = 4
-
-    def weigh(k, slot):
-        place = lax.rem(k, ring.shape[0])
+    for which in range(2):
+        @pl.loop(0, batch)
+        def _(b):
+            fetch_shared(which, b).wait()
+            rows = shared_half.shape[3]
+            for source in range(sources):
+                at = pl.multiple_of((b * sources + source) * rows, 8)
+                shared[which, pl.ds(at, rows), :] = shared_half[which, b, source].astype(F32)
+
+    weigh(shared, batch * sources, sums, m_local)
+    chunks = sums.shape[0] // 2
+    for k in range(chunks):
+        total.halving(k).start()
+
+    def unmix(k, slot):
         for inner in range(per):
             rows = rows_of_degree(mixed_blk.at[slot], inner, m_local)
-            keep = rows_of_degree(coef_blk.at[slot], inner, m_local)
             res = dot(rows, mix_block(w_buf.at[slot, inner]), NN)
             at = pl.ds(pl.multiple_of((k * per + inner) * m_local, m_local), m_local)
             half = res.shape[1] // 2
             for part in range(2):
                 back[:, part, at, :] = res[:, part * half:(part + 1) * half].reshape(batch, m_local, half)
-            big = dot(rows, keep, TN)
-            side, spot = inner // (per // 2), inner % (per // 2)
-            ring[place, side, spot, pl.ds(0, half, stride=2), :] = big[:half, :half] + big[half:, half:]
-            ring[place, side, spot, pl.ds(1, half, stride=2), :] = big[half:, :half] - big[:half, half:]
-        total.halving(0, k).start()
-
-        @pl.when(k >= 2)
-        def _():
-            total.absorb(0, k - 2)
-
-            @pl.when(k - 2 < early)
-            def _():
-                total.halving(1, k - 2).start()
-
-    mix_loop(w_mix, [mixed, coef], [mixed_blk, coef_blk], w_buf, w_sem, [m_sem, c_sem], blocks, weigh)
+
+    mix_loop(w_mix, [mixed], [mixed_blk], w_buf, w_sem, [m_sem], degrees // per, unmix)
     fetch(0).start()
-    total.absorb(0, blocks - 2)
-    total.absorb(0, blocks - 1)
     load_legendre(me, group, p_fwd, stage, p_sem)
     flip_rows(stage, flipped)
     flip_far(swap, p_fwd, stage, p_sem)
     lag = 2
-    width = 2
 
     def body(i, carry):
         @pl.when(i < batch)
@@ -672,21 +753,13 @@
         def _():
             swap.relay(i - 1)
 
-        for j in range(width):
-            k = early + i * width + j
-
-            @pl.when(k < blocks)
+        steps = [total.reduce_step] + [functools.partial(total.gather_step, p) for p in (2, 1, 0, -1)]
+        for late, step in enumerate(steps):
+            k = i - late
+
+            @pl.when((k >= 0) & (k < chunks))
             def _():
-                total.halving(1, k).start()
-
-        steps = [(total.reduce_step, p) for p in (2, 3, 4)] + [(total.gather_step, p) for p in (2, 1, 0, -1)]
-        for late, (step, phase) in enumerate(steps):
-            for j in range(width):
-                k = (i - late) * width + j
-
-                @pl.when((k >= 0) & (k < blocks))
-                def _():
-                    step(phase, k)
+                step(k)
 
         @pl.when((i >= lag) & (i < batch + lag))
         def _():
@@ -712,7 +785,7 @@
 
         return carry
 
-    lax.fori_loop(0, max(batch + lag, blocks // width + 6), body, 0)
+    lax.fori_loop(0, max(batch + lag, chunks + 4), body, 0)
     swap.drain()
     for b in range(batch - depth + 1, batch):
         put(b).wait()
@@ -762,39 +835,45 @@
                      vmem((SLOTS, group // 2, late_rows, channels), BF16), vmem((late, lats, degrees), BF16))
         bridged_sems = (dma((SLOTS,)), dma((batch,))) * 3
 
-        coef = pl.pallas_call(
+        ranks = group // 2
+        share_rows = (m_local + 1) * 2 * ranks
+        share_out = jax.ShapeDtypeStruct((batch, ranks, share_rows, channels), BF16)
+        share_t = (vmem((SLOTS, ranks, share_rows, channels), BF16), vmem((ranks, share_rows, channels), F32))
+        share_sems = (dma((SLOTS,)), dma((batch,)), dma((SLOTS,)))
+        padded_t = vmem((2, 2, 2 * degrees * m_local, channels), F32)
+
+        coef, shared_coef = pl.pallas_call(
             functools.partial(first_kernel, group, rows_local), name='first',
-            out_shape=jax.ShapeDtypeStruct(coef_shape, F32),
-            in_specs=[any_spec, table_spec, any_spec], out_specs=any_spec,
-            scratch_shapes=[field_t, stage_t, expanded_t, turn_t, send_t, recv_t, pair_t, dma((2, 2)), dma((2,)), dma(()),
-                            dma((SLOTS,)), dma((batch,))],
+            out_shape=[jax.ShapeDtypeStruct(coef_shape, F32), share_out],
+            in_specs=[any_spec, table_spec, any_spec], out_specs=[any_spec] * 2,
+            scratch_shapes=[field_t, stage_t, expanded_t, turn_t, send_t, recv_t, padded_t, share_t, dma((2, 2)), dma((2,)),
+                            dma(()), dma((SLOTS,)), dma((batch,)), share_sems],
             compiler_params=params(0))(field, base, p_fwd)
 
         blk_t = vmem((2, batch, 2, per * m_local, channels), F32)
         w_t = vmem((2, per, channels * 2, channels), F32)
-        mixed = pl.pallas_call(
+        mixed, shared_mixed = pl.pallas_call(
             functools.partial(second_kernel, group, rows_local), name='second',
-            out_shape=jax.ShapeDtypeStruct(coef_shape, F32),
-            in_specs=[any_spec, any_spec, any_spec, table_spec, any_spec], out_specs=any_spec,
-            scratch_shapes=[w_t, blk_t, vmem(coef_shape, F32), stage_t, flipped_t, expanded_t, turn_t, field_t, pair_t,
-                            bridged_t, send_t, recv_t, dma((2,)), dma((2,)), dma((2, 2)), dma((2,)), dma(()),
-                            bridged_sems, dma((SLOTS,)), dma((batch,))],
+            out_shape=[jax.ShapeDtypeStruct(coef_shape, F32), share_out],
+            in_specs=[any_spec, any_spec, any_spec, table_spec, any_spec], out_specs=[any_spec] * 2,
+            scratch_shapes=[w_t, blk_t, vmem(coef_shape, F32), stage_t, flipped_t, expanded_t, turn_t, field_t, padded_t,
+                            bridged_t, send_t, recv_t, share_t, dma((2,)), dma((2,)), dma((2, 2)), dma((2,)), dma(()),
+                            bridged_sems, dma((SLOTS,)), dma((batch,)), share_sems],
             compiler_params=params(1))(coef, w_rows, p_inv, gained, grad)
 
-        blocks = degrees // per
+        steps = degrees // ranks
+        w_rect = (channels * 2, channels)
         field_out, gw_total = pl.pallas_call(
             functools.partial(third_kernel, group, rows_local), name='third',
-            out_shape=[jax.ShapeDtypeStruct(grad.shape, F32), jax.ShapeDtypeStruct(w_rows.shape, F32)],
-            in_specs=[any_spec] * 4 + [table_spec, any_spec], out_specs=[any_spec] * 2,
-            scratch_shapes=[w_t, blk_t, blk_t, vmem((4, 2, per // 2, channels * 2, channels), F32),
-                            vmem((blocks, per // 2, channels * 2, channels), F32),
-                            vmem((blocks, per // 4, channels * 2, channels), F32),
-                            vmem((blocks, channels * 2, channels), F32), vmem((blocks, channels, channels), F32),
-                            vmem(coef_shape, F32), stage_t, flipped_t, turn_t,
+            out_shape=[jax.ShapeDtypeStruct(grad.shape, F32), jax.ShapeDtypeStruct((steps, ranks) + w_rect, F32)],
+            in_specs=[any_spec] * 5 + [table_spec, any_spec], out_specs=[any_spec] * 2,
+            scratch_shapes=[w_t, blk_t, vmem((2, batch, ranks, share_rows, channels), BF16),
+                            vmem((2, batch * ranks * share_rows, channels), F32), vmem((steps,) + w_rect, F32),
+                            vmem((steps // 2,) + w_rect, F32), vmem(coef_shape, F32), stage_t, flipped_t, turn_t,
                             vmem((3, lon_count // LANES, channels * rows_local, LANES), F32), bridged_t,
-                            dma((2,)), dma((2,)), dma((2,)), dma((2, 3, 4, blocks)), dma((3, 2)), dma((3, 2)), dma(()),
+                            dma((2,)), dma((2,)), dma((2, batch)), dma((2, 6, steps // 2)), dma((3, 2)), dma((3, 2)), dma(()),
                             bridged_sems],
-            compiler_params=params(2))(mixed, coef, w_rows, p_fwd, base, grad)
+            compiler_params=params(2))(mixed, shared_mixed, shared_coef, w_rows, p_fwd, base, grad)
 
         grad_wmix = jnp.swapaxes(gw_total.reshape(degrees, channels, 2, channels), 2, 3)
         return field_out.reshape(grad_loc.shape), grad_wmix

time: 733 us -> 716 us (0.977)
  Pallas kernels: 709 us -> 691 us
    pallas_call x1, Pallas kernels: 292 us -> 261 us  [local_step(): pl.pallas_call(functools.partial(third_kernel, group, rows_local), name='...]
    pallas_call x1, Pallas kernels: 140 us -> 149 us  [local_step(): pl.pallas_call(functools.partial(first_kernel, group, rows_local), name='...]
where the time goes in v5:
time: 716 us; the launch traced here: 714 us
  Pallas kernels  691 us (97%)
  local copies, waits for them, and re-layouts  22.2 us (3%)
    pallas_call x1, Pallas kernels, local_step(): pl.pallas_call(functools.partial(second_kernel, group, rows_local), name=...  281 us
    pallas_call x1, Pallas kernels, local_step(): pl.pallas_call(functools.partial(third_kernel, group, rows_local), name='...  261 us
    pallas_call x1, Pallas kernels, local_step(): pl.pallas_call(functools.partial(first_kernel, group, rows_local), name='...  149 us
    unnamed x2, local copies, waits for them, and re-layouts  22.2 us

profile of v5, /device:TPU:0, one launch (start us, length us, event | category | flops | bytes accessed | tf_op | source)
XLA Modules:
  0.0 713.9 jit_solution(16696321751299139831)
XLA Ops:
  0.6 149.1 %first.1 = (f32[12,2,1024,128]{3,2,1,0:T(8,128)}, bf16[12,8,144,128]{3,2,1,0:T(8,128)(2,1)}) custom-call(f32[12,1024,256]{2,1,0:T(8,128)} %bitcast.15, bf16[2,256,256]{2,1,0:T(8,128)(2,1)} %constant.14.table, f32[128,128,128]{2,1,0:T(8,128)} %p_fwd.3), custom_call_target="tpu_custom_call" | custom-call | tf_op jit(solution)/shard_map/first/pallas_call | solution.py:845
  149.7 280.5 %second.1 = (f32[12,2,1024,128]{3,2,1,0:T(8,128)}, bf16[12,8,144,128]{3,2,1,0:T(8,128)(2,1)}) custom-call(f32[12,2,1024,128]{3,2,1,0:T(8,128)} %get-tuple-element.8.coef, f32[128,256,128]{2,1,0:T(8,128)} %bitcast.9, f32[128,128,128]{2,1,0:T(8,128)} %p_inv.1, bf16[2,256,256]{2,1,0:T(8,128)(2,1)} %constant.21.table, f32[12,1024,256]{2,1,0:T(8,128)} %bitcast.11), custom_call_target="tpu_custom_call" | custom-call | tf_op jit(solution)/shard_map/second/pallas_call | solution.py:855
  430.3 261.5 %third.1 = (f32[12,1024,256]{2,1,0:T(8,128)}, f32[16,8,256,128]{3,2,1,0:T(8,128)}) custom-call(f32[12,2,1024,128]{3,2,1,0:T(8,128)} %get-tuple-element.9.mixed, bf16[12,8,144,128]{3,2,1,0:T(8,128)(2,1)} %get-tuple-element.10.shared_mixed, bf16[12,8,144,128]{3,2,1,0:T(8,128)(2,1)} %get-tuple-element.11.shared_coef, f32[128,256,128]{2,1,0:T(8,128)} %bitcast.10, ...), custom_call_target="tpu_custom_call" | custom-call | tf_op jit(solution)/shard_map/third/pallas_call | solution.py:866
  691.7 10.2 %copy.11 = f32[12,128,8,256]{3,2,1,0:T(8,128)} copy(f32[12,128,8,256]{3,2,1,0:T(8,128)} %bitcast.14) | data formatting | bytes 25165824
  701.9 12.0 %copy.12 = f32[128,128,128,2]{2,3,1,0:T(2,128)} copy(f32[128,128,128,2]{2,3,1,0:T(2,128)} %bitcast.13) | data formatting | bytes 33554432

commit v6 on v5

--- a/solution.py
+++ b/solution.py
@@ -12,6 +12,7 @@
 MESH = pl.DeviceIdType.MESH
 LANES = 128
 SLOTS = 3
+DEPTH = 4
 VMEM_LIMIT = 60 * 1024 * 1024
 F32 = jnp.float32
 BF16 = jnp.bfloat16
@@ -217,8 +218,8 @@
 
 
 class Share:
-    def __init__(self, me, group, batch, send, message, out, sems):
-        self.batch, self.send, self.message, self.out = batch, send, message, out
+    def __init__(self, me, group, batch, send, message, out, sems, resident=False):
+        self.batch, self.send, self.message, self.out, self.resident = batch, send, message, out, resident
         self.send_sem, self.recv_sem, self.local_sem = sems
         self.size = group // 2
         self.base = me // self.size * self.size
@@ -247,7 +248,8 @@
         @pl.when(b >= SLOTS)
         def _():
             self.every(b - SLOTS).wait_send()
-            self.keep(b - SLOTS).wait()
+            if not self.resident:
+                self.keep(b - SLOTS).wait()
 
         size = self.size
         m_local = size
@@ -266,7 +268,10 @@
                 self.message[rank, pl.ds(m_local * tile + part * size, size), :] = rows(part, m_local // 2, rank, size, size)
         for rank in range(size):
             self.send[slot_b, rank] = self.message[rank].astype(BF16)
-        self.keep(b).start()
+        if self.resident:
+            self.out[b, self.place] = self.send[slot_b, self.rank(self.place)]
+        else:
+            self.keep(b).start()
 
         @pl.loop(1, size)
         def _(step):
@@ -276,11 +281,15 @@
     def drain(self):
         for b in range(max(0, self.batch - SLOTS), self.batch):
             self.every(b).wait_send()
-            self.keep(b).wait()
-
-        @pl.loop(0, self.batch)
-        def _(b):
-            self.every(b).wait_recv()
+            if not self.resident:
+                self.keep(b).wait()
+        if not self.resident:
+            @pl.loop(0, self.batch)
+            def _(b):
+                self.every(b).wait_recv()
+
+    def arrive(self, b):
+        self.every(b).wait_recv()
 
 
 def clear_after(coef, degrees_rows):
@@ -290,22 +299,23 @@
             coef[slot, part, pl.ds(degrees_rows, rows - degrees_rows), :] = jnp.zeros((rows - degrees_rows, lanes), F32)
 
 
-def enter(me, group):
+def greet(me, group):
     barrier = pltpu.get_barrier_semaphore()
 
     @pl.loop(1, group)
     def _(step):
         pl.semaphore_signal(barrier, inc=1, device_id={'lat': lax.rem(me + step, group)}, device_id_type=MESH)
 
-    pl.semaphore_wait(barrier, group - 1)
+
+def meet(group):
+    pl.semaphore_wait(pltpu.get_barrier_semaphore(), group - 1)
 
 
 def load_legendre(me, group, table_hbm, stage, sem):
     m_local = stage.shape[0]
-    copies = [pltpu.make_async_copy(table_hbm.at[slot * group + me], stage.at[slot], sem) for slot in range(m_local)]
-    for copy in copies:
-        copy.start()
-    pltpu.make_async_copy(table_hbm.at[pl.ds(0, m_local)], stage, sem).wait()
+    for slot in range(m_local):
+        pltpu.make_async_copy(table_hbm.at[slot * group + me], stage.at[slot], sem).start()
+    return pltpu.make_async_copy(table_hbm.at[pl.ds(0, m_local)], stage, sem)
 
 
 def expand_rows(stage, expanded, rows_local):
@@ -321,14 +331,11 @@
             expanded[slot, pl.ds(part * degrees, degrees), :] = dot(stage[slot].astype(BF16), pick, NN).astype(BF16)
 
 
-def flip_far(swap, table_hbm, stage, sem):
-    late = swap.flipped_far.shape[0]
-    copies = [pltpu.make_async_copy(table_hbm.at[(swap.direct + n) * swap.group + swap.twin], stage.at[n], sem) for n in range(late)]
-    for copy in copies:
-        copy.start()
-    pltpu.make_async_copy(table_hbm.at[pl.ds(0, late)], stage.at[pl.ds(0, late)], sem).wait()
+def load_far(swap, table_hbm, stage, sem):
+    late = stage.shape[0]
     for n in range(late):
-        swap.flipped_far[n] = stage[n].T.astype(BF16)
+        pltpu.make_async_copy(table_hbm.at[(swap.direct + n) * swap.group + swap.twin], stage.at[n], sem).start()
+    return pltpu.make_async_copy(table_hbm.at[pl.ds(0, late)], stage, sem)
 
 
 def flip_rows(stage, flipped):
@@ -418,8 +425,9 @@
     return jnp.concatenate(parts, axis=1).astype(BF16)
 
 
-def first_kernel(group, rows_local, field, table, p_fwd, coef_out, shared, field_buf, stage, expanded, turn, send, recv,
-                 coef_buf, share_bufs, in_sem, out_sem, p_sem, send_sem, recv_sem, share_sems):
+def first_kernel(group, rows_local, field, table, p_fwd, w_mix, coef_out, shared, w_big, field_buf, stage, expanded, turn, send,
+                 recv, coef_buf, share_bufs, w_in, w_out, in_sem, out_sem, p_sem, send_sem, recv_sem, share_sems, w_in_sem,
+                 w_out_sem):
     me = lax.axis_index('lat')
     batch = field.shape[0]
     channels = field.shape[1] // rows_local
@@ -431,12 +439,24 @@
         whole = pl.ds(0, coef_out.shape[2])
         return pltpu.make_async_copy(coef_buf.at[lax.rem(b, 2), :, whole], coef_out.at[b], out_sem.at[lax.rem(b, 2)])
 
+    per = w_in.shape[1]
+    blocks = w_mix.shape[0] // per
+
+    def fetch_w(k):
+        return pltpu.make_async_copy(w_mix.at[pl.ds(k * per, per)], w_in.at[lax.rem(k, 2)], w_in_sem.at[lax.rem(k, 2)])
+
+    def put_w(k):
+        return pltpu.make_async_copy(w_out.at[lax.rem(k, 2)], w_big.at[pl.ds(k * per, per)], w_out_sem.at[lax.rem(k, 2)])
+
     fetch(0).start()
-    enter(me, group)
+    loading = load_legendre(me, group, p_fwd, stage, p_sem)
+    fetch_w(0).start()
+    greet(me, group)
     share = Share(me, group, batch, *share_bufs, shared, share_sems)
     clear_after(coef_buf, coef_out.shape[2])
     swap = Exchange(me, group, batch, send, recv, send_sem, recv_sem)
     lag = 2
+    meet(group)
 
     def body(i, carry):
         @pl.when(i < batch)
@@ -454,8 +474,28 @@
 
         @pl.when(i == 0)
         def _():
-            load_legendre(me, group, p_fwd, stage, p_sem)
+            loading.wait()
             expand_rows(stage, expanded, rows_local)
+
+        @pl.when(i < blocks)
+        def _():
+            fetch_w(i).wait()
+
+            @pl.when(i + 1 < blocks)
+            def _():
+                fetch_w(i + 1).start()
+
+            @pl.when(i >= 2)
+            def _():
+                put_w(i - 2).wait()
+
+            half = lax.rem(i, 2)
+
+            @pl.loop(0, per)
+            def _(inner):
+                w_out[half, inner] = mix_block(w_in.at[half, inner])
+
+            put_w(i).start()
 
         @pl.when(i >= lag)
         def _():
@@ -477,39 +517,44 @@
     share.drain()
     put(batch - 2).wait()
     put(batch - 1).wait()
-
-
-def mix_loop(w_hbm, in_hbms, bufs, w_buf, w_sem, in_sems, blocks, step):
-    per = w_buf.shape[1]
+    put_w(blocks - 2).wait()
+    put_w(blocks - 1).wait()
+
+
+def mix_loop(w_hbm, in_hbms, bufs, w_buf, w_sem, in_sems, blocks, step, meanwhile):
+    depth, per = w_buf.shape[:2]
 
     def copies(k):
-        slot = lax.rem(k, 2)
+        slot = lax.rem(k, depth)
         out = [pltpu.make_async_copy(w_hbm.at[pl.ds(k * per, per)], w_buf.at[slot], w_sem.at[slot])]
         for src, buf, sem in zip(in_hbms, bufs, in_sems):
             rows = buf.shape[3]
             out.append(pltpu.make_async_copy(src.at[:, :, pl.ds(k * rows, rows), :], buf.at[slot], sem.at[slot]))
         return out
 
-    for copy in copies(0):
-        copy.start()
+    for k in range(depth - 1):
+        for copy in copies(k):
+            copy.start()
+    meanwhile()
 
     def body(k, carry):
-        @pl.when(k + 1 < blocks)
-        def _():
-            for copy in copies(k + 1):
+        @pl.when(k + depth - 1 < blocks)
+        def _():
+            for copy in copies(k + depth - 1):
                 copy.start()
 
         for copy in copies(k):
             copy.wait()
-        step(k, lax.rem(k, 2))
+        step(k, lax.rem(k, depth))
         return carry
 
     lax.fori_loop(0, blocks, body, 0)
 
 
-def second_kernel(group, rows_local, coef, w_mix, p_inv, table, grad, mixed_out, shared, w_buf, coef_blk, mixed, stage,
-                  flipped, expanded, turn, grad_buf, out_buf, bridged, send_b, recv_b, share_bufs, w_sem, c_sem, in_sem, out_sem,
-                  p_sem, bridged_sems, send_b_sem, recv_b_sem, share_sems):
+def second_kernel(group, rows_local, coef, shared_coef, w_mix, p_inv, table, grad, mixed_out, sums_out, w_buf, coef_blk, mixed,
+                  stage, flipped, expanded, turn, grad_buf, out_buf, bridged, send_b, recv_b, share_bufs, shared_recv, shared_half,
+                  shared, sums, w_sem, c_sem, in_sem, out_sem, p_sem, bridged_sems, send_b_sem, recv_b_sem, share_sems, s_sem,
+                  stage_far, far_sem):
     me = lax.axis_index('lat')
     batch = grad.shape[0]
     channels = grad.shape[1] // rows_local
@@ -524,27 +569,47 @@
         whole = pl.ds(0, mixed_out.shape[2])
         return pltpu.make_async_copy(out_buf.at[lax.rem(b, 2), :, whole], mixed_out.at[b], out_sem.at[lax.rem(b, 2)])
 
+    greet(me, group)
     fetch(0).start()
     swap_a = BridgedExchange(me, group, batch, bridged, bridged_sems)
-    load_legendre(me, group, p_inv, stage, p_sem)
-    flip_rows(stage, flipped)
-    expand_rows(stage, expanded, rows_local)
-    flip_far(swap_a, p_inv, stage, p_sem)
-    share = Share(me, group, batch, *share_bufs, shared, share_sems)
+    loading = load_legendre(me, group, p_inv, stage, p_sem)
+    loading_far = load_far(swap_a, p_inv, stage_far, far_sem)
+
+    def prepare():
+        sums[...] = jnp.zeros_like(sums)
+        loading.wait()
+        flip_rows(stage, flipped)
+        expand_rows(stage, expanded, rows_local)
+        loading_far.wait()
+        flip_rows(stage_far, swap_a.flipped_far)
+
+    share = Share(me, group, batch, *share_bufs, shared_recv, share_sems, resident=True)
     clear_after(out_buf, mixed_out.shape[2])
+    sources, share_rows = shared_recv.shape[1:3]
+    def fetch_shared(b):
+        return pltpu.make_async_copy(shared_coef.at[b], shared_half.at[lax.rem(b, 3)], s_sem.at[lax.rem(b, 3)])
+
+    def weigh_sample(b):
+        fetch_shared(b).wait()
+        share.arrive(b)
+        for source in range(sources):
+            at = pl.ds(source * (shared.shape[1] // sources), share_rows)
+            shared[0, at, :] = shared_recv[b, source].astype(F32)
+            shared[1, at, :] = shared_half[lax.rem(b, 3), source].astype(F32)
+        weigh(shared, sources, sums, m_local)
 
     def mix(k, slot):
         for inner in range(per):
             rows = rows_of_degree(coef_blk.at[slot], inner, m_local)
-            res = dot(rows, mix_block(w_buf.at[slot, inner]), NT)
+            res = dot(rows, w_buf[slot, inner], NT)
             at = pl.ds(pl.multiple_of((k * per + inner) * m_local, m_local), m_local)
             for part in range(2):
                 lanes = res.shape[1] // 2
                 mixed[:, part, at, :] = res[:, part * lanes:(part + 1) * lanes].reshape(batch, m_local, lanes)
 
-    mix_loop(w_mix, [coef], [coef_blk], w_buf, w_sem, [c_sem], degrees // per, mix)
-
-    enter(me, group)
+    mix_loop(w_mix, [coef], [coef_blk], w_buf, w_sem, [c_sem], degrees // per, mix, prepare)
+
+    meet(group)
     swap_b = Exchange(me, group, batch, send_b, recv_b, send_b_sem, recv_b_sem)
     lag, lag_b = 2, 2
 
@@ -583,6 +648,11 @@
         @pl.when(i >= lag + lag_b)
         def _():
             b = i - lag - lag_b
+
+            @pl.when(b >= 2)
+            def _():
+                weigh_sample(b - 2)
+
             swap_b.arrive(b)
 
             @pl.when(b >= 2)
@@ -592,13 +662,19 @@
             legendre_forward(recv_b, b, expanded, out_buf.at[lax.rem(b, 2)], rows_local)
             put(b).start()
             share.give(b, out_buf.at[lax.rem(b, 2)])
+            fetch_shared(b).start()
 
         return carry
 
     lax.fori_loop(0, batch + lag + lag_b, body, 0)
+    weigh_sample(batch - 2)
+    weigh_sample(batch - 1)
+    total = pltpu.make_async_copy(sums, sums_out, p_sem)
+    total.start()
     swap_a.drain()
     swap_b.drain()
     share.drain()
+    total.wait()
     put(batch - 2).wait()
     put(batch - 1).wait()
 
@@ -659,8 +735,8 @@
     return (part * (m_local // 2) + pair) * tile + step - shift
 
 
-def weigh(shared, batch_rows, sums, m_local):
-    block_rows = shared.shape[1] // batch_rows
+def weigh(shared, sources, sums, m_local):
+    stride = shared.shape[1] // sources
 
     @pl.loop(0, sums.shape[0])
     def _(step):
@@ -672,19 +748,20 @@
                 parts = []
                 for part in range(2):
                     place = jnp.where(used, shared_place(part, slot, step, m_local), 0)
-                    rows = shared[which, pl.ds(place, batch_rows, stride=block_rows), :]
+                    rows = shared[which, pl.ds(place, sources, stride=stride), :]
                     parts.append(jnp.where(used, rows, 0.0))
                 slots.append(jnp.concatenate(parts, axis=1))
             sides.append(jnp.concatenate(slots, axis=0).astype(BF16))
         big = dot(sides[0], sides[1], TN)
         half = big.shape[0] // 2
-        sums[step, pl.ds(0, half, stride=2), :] = big[:half, :half] + big[half:, half:]
-        sums[step, pl.ds(1, half, stride=2), :] = big[half:, :half] - big[:half, half:]
-
-
-def third_kernel(group, rows_local, mixed, shared_mixed, shared_coef, w_mix, p_fwd, table, grad, field_out, grad_w, w_buf,
-                 mixed_blk, shared_half, shared, sums, got, back, stage, flipped, turn, grad_buf, bridged, w_sem, m_sem, s_sem,
-                 gw_sem, in_sem, out_sem, p_sem, bridged_sems):
+        real, imag = pl.ds(0, half, stride=2), pl.ds(1, half, stride=2)
+        sums[step, real, :] = sums[step, real, :] + (big[:half, :half] + big[half:, half:])
+        sums[step, imag, :] = sums[step, imag, :] + (big[half:, :half] - big[:half, half:])
+
+
+def third_kernel(group, rows_local, mixed, part_sums, w_mix, p_fwd, table, grad, field_out, grad_w, w_buf, mixed_blk, sums, got,
+                 back, stage, flipped, turn, grad_buf, bridged, w_sem, m_sem, s_sem, gw_sem, in_sem, out_sem, p_sem, bridged_sems,
+                 stage_far, far_sem):
     me = lax.axis_index('lat')
     batch = grad.shape[0]
     channels = grad.shape[1] // rows_local
@@ -692,7 +769,6 @@
     per = w_buf.shape[1]
     degrees = w_mix.shape[0]
     m_local = stage.shape[0]
-    sources = shared_mixed.shape[1]
 
     def fetch(b):
         return Halves(grad, b, grad_buf, lax.rem(b, depth), in_sem)
@@ -700,28 +776,15 @@
     def put(b):
         return Halves(field_out, b, grad_buf, lax.rem(b, depth), out_sem, outward=True)
 
-    def fetch_shared(which, b):
-        return pltpu.make_async_copy((shared_mixed, shared_coef)[which].at[b], shared_half.at[which, b], s_sem.at[which, b])
-
-    for which in range(2):
-        @pl.loop(0, batch)
-        def _(b):
-            fetch_shared(which, b).start()
-
-    enter(me, group)
+    load_sums = pltpu.make_async_copy(part_sums, sums, s_sem)
+    load_sums.start()
+    greet(me, group)
     total = WeightSum(me, group, sums, got, grad_w, gw_sem)
     swap = BridgedExchange(me, group, batch, bridged, bridged_sems)
-
-    for which in range(2):
-        @pl.loop(0, batch)
-        def _(b):
-            fetch_shared(which, b).wait()
-            rows = shared_half.shape[3]
-            for source in range(sources):
-                at = pl.multiple_of((b * sources + source) * rows, 8)
-                shared[which, pl.ds(at, rows), :] = shared_half[which, b, source].astype(F32)
-
-    weigh(shared, batch * sources, sums, m_local)
+    loading = load_legendre(me, group, p_fwd, stage, p_sem)
+    loading_far = load_far(swap, p_fwd, stage_far, far_sem)
+    load_sums.wait()
+    meet(group)
     chunks = sums.shape[0] // 2
     for k in range(chunks):
         total.halving(k).start()
@@ -729,17 +792,20 @@
     def unmix(k, slot):
         for inner in range(per):
             rows = rows_of_degree(mixed_blk.at[slot], inner, m_local)
-            res = dot(rows, mix_block(w_buf.at[slot, inner]), NN)
+            res = dot(rows, w_buf[slot, inner], NN)
             at = pl.ds(pl.multiple_of((k * per + inner) * m_local, m_local), m_local)
             half = res.shape[1] // 2
             for part in range(2):
                 back[:, part, at, :] = res[:, part * half:(part + 1) * half].reshape(batch, m_local, half)
 
-    mix_loop(w_mix, [mixed], [mixed_blk], w_buf, w_sem, [m_sem], degrees // per, unmix)
+    def prepare():
+        loading.wait()
+        flip_rows(stage, flipped)
+        loading_far.wait()
+        flip_rows(stage_far, swap.flipped_far)
+
+    mix_loop(w_mix, [mixed], [mixed_blk], w_buf, w_sem, [m_sem], degrees // per, unmix, prepare)
     fetch(0).start()
-    load_legendre(me, group, p_fwd, stage, p_sem)
-    flip_rows(stage, flipped)
-    flip_far(swap, p_fwd, stage, p_sem)
     lag = 2
 
     def body(i, carry):
@@ -754,7 +820,7 @@
             swap.relay(i - 1)
 
         steps = [total.reduce_step] + [functools.partial(total.gather_step, p) for p in (2, 1, 0, -1)]
-        for late, step in enumerate(steps):
+        for late, step in reversed(list(enumerate(steps))):
             k = i - late
 
             @pl.when((k >= 0) & (k < chunks))
@@ -842,38 +908,43 @@
         share_sems = (dma((SLOTS,)), dma((batch,)), dma((SLOTS,)))
         padded_t = vmem((2, 2, 2 * degrees * m_local, channels), F32)
 
-        coef, shared_coef = pl.pallas_call(
+        w_wide = 16
+        big_shape = (2 * channels, 2 * channels)
+        far_stage_t = vmem((late, degrees, lats), F32)
+        coef, shared_coef, w_big = pl.pallas_call(
             functools.partial(first_kernel, group, rows_local), name='first',
-            out_shape=[jax.ShapeDtypeStruct(coef_shape, F32), share_out],
-            in_specs=[any_spec, table_spec, any_spec], out_specs=[any_spec] * 2,
-            scratch_shapes=[field_t, stage_t, expanded_t, turn_t, send_t, recv_t, padded_t, share_t, dma((2, 2)), dma((2,)),
-                            dma(()), dma((SLOTS,)), dma((batch,)), share_sems],
-            compiler_params=params(0))(field, base, p_fwd)
-
-        blk_t = vmem((2, batch, 2, per * m_local, channels), F32)
-        w_t = vmem((2, per, channels * 2, channels), F32)
-        mixed, shared_mixed = pl.pallas_call(
+            out_shape=[jax.ShapeDtypeStruct(coef_shape, F32), share_out, jax.ShapeDtypeStruct((degrees,) + big_shape, BF16)],
+            in_specs=[any_spec, table_spec, any_spec, any_spec], out_specs=[any_spec] * 3,
+            scratch_shapes=[field_t, stage_t, expanded_t, turn_t, send_t, recv_t, padded_t, share_t,
+                            vmem((2, w_wide, 2 * channels, channels), F32), vmem((2, w_wide) + big_shape, BF16),
+                            dma((2, 2)), dma((2,)), dma(()), dma((SLOTS,)), dma((batch,)), share_sems, dma((2,)), dma((2,))],
+            compiler_params=params(0))(field, base, p_fwd, w_rows)
+
+        blk_t = vmem((DEPTH, batch, 2, per * m_local, channels), F32)
+        w_t = vmem((DEPTH, per) + big_shape, BF16)
+        steps = degrees // ranks
+        sums_shape = (steps, channels * 2, channels)
+        mixed, sums = pl.pallas_call(
             functools.partial(second_kernel, group, rows_local), name='second',
-            out_shape=[jax.ShapeDtypeStruct(coef_shape, F32), share_out],
-            in_specs=[any_spec, any_spec, any_spec, table_spec, any_spec], out_specs=[any_spec] * 2,
+            out_shape=[jax.ShapeDtypeStruct(coef_shape, F32), jax.ShapeDtypeStruct(sums_shape, F32)],
+            in_specs=[any_spec] * 4 + [table_spec, any_spec], out_specs=[any_spec] * 2,
             scratch_shapes=[w_t, blk_t, vmem(coef_shape, F32), stage_t, flipped_t, expanded_t, turn_t, field_t, padded_t,
-                            bridged_t, send_t, recv_t, share_t, dma((2,)), dma((2,)), dma((2, 2)), dma((2,)), dma(()),
-                            bridged_sems, dma((SLOTS,)), dma((batch,)), share_sems],
-            compiler_params=params(1))(coef, w_rows, p_inv, gained, grad)
-
-        steps = degrees // ranks
+                            bridged_t, send_t, recv_t, share_t, vmem(share_out.shape, BF16), vmem((3,) + share_out.shape[1:], BF16),
+                            vmem((2, ranks * (share_rows + 8), channels), F32), vmem(sums_shape, F32),
+                            dma((DEPTH,)), dma((DEPTH,)), dma((2, 2)), dma((2,)), dma(()),
+                            bridged_sems, dma((SLOTS,)), dma((batch,)), share_sems, dma((3,)), far_stage_t, dma(())],
+            compiler_params=params(1))(coef, shared_coef, w_big, p_inv, gained, grad)
+
         w_rect = (channels * 2, channels)
         field_out, gw_total = pl.pallas_call(
             functools.partial(third_kernel, group, rows_local), name='third',
             out_shape=[jax.ShapeDtypeStruct(grad.shape, F32), jax.ShapeDtypeStruct((steps, ranks) + w_rect, F32)],
-            in_specs=[any_spec] * 5 + [table_spec, any_spec], out_specs=[any_spec] * 2,
-            scratch_shapes=[w_t, blk_t, vmem((2, batch, ranks, share_rows, channels), BF16),
-                            vmem((2, batch * ranks * share_rows, channels), F32), vmem((steps,) + w_rect, F32),
-                            vmem((steps // 2,) + w_rect, F32), vmem(coef_shape, F32), stage_t, flipped_t, turn_t,
+            in_specs=[any_spec] * 4 + [table_spec, any_spec], out_specs=[any_spec] * 2,
+            scratch_shapes=[w_t, blk_t, vmem(sums_shape, F32), vmem((steps // 2,) + w_rect, F32), vmem(coef_shape, F32), stage_t, flipped_t, turn_t,
                             vmem((3, lon_count // LANES, channels * rows_local, LANES), F32), bridged_t,
-                            dma((2,)), dma((2,)), dma((2, batch)), dma((2, 6, steps // 2)), dma((3, 2)), dma((3, 2)), dma(()),
-                            bridged_sems],
-            compiler_params=params(2))(mixed, shared_mixed, shared_coef, w_rows, p_fwd, base, grad)
+                            dma((DEPTH,)), dma((DEPTH,)), dma(()), dma((2, 6, steps // 2)), dma((3, 2)), dma((3, 2)), dma(()),
+                            bridged_sems, far_stage_t, dma(())],
+            compiler_params=params(2))(mixed, sums, w_big, p_fwd, base, grad)
 
         grad_wmix = jnp.swapaxes(gw_total.reshape(degrees, channels, 2, channels), 2, 3)
         return field_out.reshape(grad_loc.shape), grad_wmix

time: 716 us -> 690 us (0.964)
  Pallas kernels: 691 us -> 666 us
    pallas_call x1, Pallas kernels: 261 us -> 237 us  [local_step(): pl.pallas_call(functools.partial(third_kernel, group, rows_local), name='...]
where the time goes in v6:
time: 690 us; the launch traced here: 689 us
  Pallas kernels  666 us (97%)
  local copies, waits for them, and re-layouts  22.2 us (3%)
    pallas_call x1, Pallas kernels, local_step(): pl.pallas_call(functools.partial(second_kernel, group, rows_local), name=...  280 us
    pallas_call x1, Pallas kernels, local_step(): pl.pallas_call(functools.partial(third_kernel, group, rows_local), name='...  237 us
    pallas_call x1, Pallas kernels, local_step(): pl.pallas_call(functools.partial(first_kernel, group, rows_local), name='...  149 us
    unnamed x2, local copies, waits for them, and re-layouts  22.2 us

profile of v6, /device:TPU:0, one launch (start us, length us, event | category | flops | bytes accessed | tf_op | source)
XLA Modules:
  0.0 688.7 jit_solution(9657935061701336110)
XLA Ops:
  0.6 148.9 %first.1 = (f32[12,2,1024,128]{3,2,1,0:T(8,128)}, bf16[12,8,144,128]{3,2,1,0:T(8,128)(2,1)}, bf16[128,256,256]{2,1,0:T(8,128)(2,1)}) custom-call(f32[12,1024,256]{2,1,0:T(8,128)} %bitcast.14, bf16[2,256,256]{2,1,0:T(8,128)(2,1)} %constant.14.table, f32[128,128,128]{2,1,0:T(8,128)} %p_fwd.3, f32[128,256,128]{2,1,0:T(8,128)} %bitcast.11), custom_call_target="tpu_custom_call" | custom-call | tf_op jit(solution)/shard_map/first/pallas_call | solution.py:914
  149.5 280.1 %second.1 = (f32[12,2,1024,128]{3,2,1,0:T(8,128)}, f32[16,256,128]{2,1,0:T(8,128)}) custom-call(f32[12,2,1024,128]{3,2,1,0:T(8,128)} %get-tuple-element.9.coef, bf16[12,8,144,128]{3,2,1,0:T(8,128)(2,1)} %get-tuple-element.10.shared_coef, bf16[128,256,256]{2,1,0:T(8,128)(2,1)} %get-tuple-element.11.w_mix, f32[128,128,128]{2,1,0:T(8,128)} %p_inv.1, ...), custom_call_target="tpu_custom_call" | custom-call | tf_op jit(solution)/shard_map/second/pallas_call | solution.py:927
  429.6 237.0 %third.1 = (f32[12,1024,256]{2,1,0:T(8,128)}, f32[16,8,256,128]{3,2,1,0:T(8,128)}) custom-call(f32[12,2,1024,128]{3,2,1,0:T(8,128)} %get-tuple-element.12.mixed, f32[16,256,128]{2,1,0:T(8,128)} %get-tuple-element.13.part_sums, bf16[128,256,256]{2,1,0:T(8,128)(2,1)} %get-tuple-element.11.w_mix, f32[128,128,128]{2,1,0:T(8,128)} %p_fwd.3, ...), custom_call_target="tpu_custom_call" | custom-call | tf_op jit(solution)/shard_map/third/pallas_call | solution.py:939
  666.6 10.2 %copy.11 = f32[12,128,8,256]{3,2,1,0:T(8,128)} copy(f32[12,128,8,256]{3,2,1,0:T(8,128)} %bitcast.13) | data formatting | bytes 25165824
  676.7 12.0 %copy.12 = f32[128,128,128,2]{2,3,1,0:T(2,128)} copy(f32[128,128,128,2]{2,3,1,0:T(2,128)} %bitcast.12) | data formatting | bytes 33554432

commit v7 on v6

--- a/solution.py
+++ b/solution.py
@@ -13,6 +13,7 @@
 LANES = 128
 SLOTS = 3
 DEPTH = 4
+BUNCH = 3
 VMEM_LIMIT = 60 * 1024 * 1024
 F32 = jnp.float32
 BF16 = jnp.bfloat16
@@ -218,8 +219,8 @@
 
 
 class Share:
-    def __init__(self, me, group, batch, send, message, out, sems, resident=False):
-        self.batch, self.send, self.message, self.out, self.resident = batch, send, message, out, resident
+    def __init__(self, me, group, batch, send, message, out, sems):
+        self.batch, self.send, self.message, self.out = batch, send, message, out
         self.send_sem, self.recv_sem, self.local_sem = sems
         self.size = group // 2
         self.base = me // self.size * self.size
@@ -248,8 +249,6 @@
         @pl.when(b >= SLOTS)
         def _():
             self.every(b - SLOTS).wait_send()
-            if not self.resident:
-                self.keep(b - SLOTS).wait()
 
         size = self.size
         m_local = size
@@ -268,35 +267,26 @@
                 self.message[rank, pl.ds(m_local * tile + part * size, size), :] = rows(part, m_local // 2, rank, size, size)
         for rank in range(size):
             self.send[slot_b, rank] = self.message[rank].astype(BF16)
-        if self.resident:
-            self.out[b, self.place] = self.send[slot_b, self.rank(self.place)]
-        else:
-            self.keep(b).start()
+        self.keep(b).start()
 
         @pl.loop(1, size)
         def _(step):
             place = lax.rem(self.place + step, size)
             self.copy(slot_b, self.rank(place), b, self.place, place).start()
 
+        self.keep(b).wait()
+
     def drain(self):
         for b in range(max(0, self.batch - SLOTS), self.batch):
             self.every(b).wait_send()
-            if not self.resident:
-                self.keep(b).wait()
-        if not self.resident:
-            @pl.loop(0, self.batch)
-            def _(b):
-                self.every(b).wait_recv()
 
     def arrive(self, b):
         self.every(b).wait_recv()
 
 
-def clear_after(coef, degrees_rows):
-    slots, parts, rows, lanes = coef.shape
-    for slot in range(slots):
-        for part in range(parts):
-            coef[slot, part, pl.ds(degrees_rows, rows - degrees_rows), :] = jnp.zeros((rows - degrees_rows, lanes), F32)
+def clear_after(coef, used):
+    for part in range(coef.shape[0]):
+        coef[part, pl.ds(used, coef.shape[1] - used), :] = jnp.zeros((coef.shape[1] - used, coef.shape[2]), F32)
 
 
 def greet(me, group):
@@ -311,11 +301,24 @@
     pl.semaphore_wait(pltpu.get_barrier_semaphore(), group - 1)
 
 
-def load_legendre(me, group, table_hbm, stage, sem):
-    m_local = stage.shape[0]
-    for slot in range(m_local):
-        pltpu.make_async_copy(table_hbm.at[slot * group + me], stage.at[slot], sem).start()
-    return pltpu.make_async_copy(table_hbm.at[pl.ds(0, m_local)], stage, sem)
+class Tables:
+    def __init__(self, waves, whole, stage, sem):
+        self.waves, self.whole, self.stage, self.sem = waves, whole, stage, sem
+
+    def start(self):
+        for n, wave in enumerate(self.waves):
+            pltpu.make_async_copy(self.whole.at[wave], self.stage.at[n], self.sem).start()
+
+    def wait(self):
+        pltpu.make_async_copy(self.whole.at[pl.ds(0, len(self.waves))], self.stage, self.sem).wait()
+
+
+def own_tables(me, group, whole, stage, sem):
+    return Tables([slot * group + me for slot in range(stage.shape[0])], whole, stage, sem)
+
+
+def far_tables(swap, whole, stage, sem):
+    return Tables([(swap.direct + n) * swap.group + swap.twin for n in range(stage.shape[0])], whole, stage, sem)
 
 
 def expand_rows(stage, expanded, rows_local):
@@ -329,13 +332,6 @@
         pick = pick.astype(F32).astype(BF16)
         for slot in range(m_local):
             expanded[slot, pl.ds(part * degrees, degrees), :] = dot(stage[slot].astype(BF16), pick, NN).astype(BF16)
-
-
-def load_far(swap, table_hbm, stage, sem):
-    late = stage.shape[0]
-    for n in range(late):
-        pltpu.make_async_copy(table_hbm.at[(swap.direct + n) * swap.group + swap.twin], stage.at[n], sem).start()
-    return pltpu.make_async_copy(table_hbm.at[pl.ds(0, late)], stage, sem)
 
 
 def flip_rows(stage, flipped):
@@ -409,13 +405,9 @@
     return cumulative + values * density
 
 
-def mix_block(w_block):
-    half = w_block.shape[0] // 2
-    w_real = w_block[pl.ds(0, half, stride=2), :]
-    w_imag = w_block[pl.ds(1, half, stride=2), :]
-    top = jnp.concatenate([w_real, -w_imag], axis=1)
-    bottom = jnp.concatenate([w_imag, w_real], axis=1)
-    return jnp.concatenate([top, bottom], axis=0).astype(BF16)
+def mix_block(planes):
+    real, imag = planes[0], planes[1]
+    return jnp.concatenate([jnp.concatenate([real, -imag], axis=1), jnp.concatenate([imag, real], axis=1)], axis=0)
 
 
 def rows_of_degree(block, inner, m_local):
@@ -425,100 +417,215 @@
     return jnp.concatenate(parts, axis=1).astype(BF16)
 
 
-def first_kernel(group, rows_local, field, table, p_fwd, w_mix, coef_out, shared, w_big, field_buf, stage, expanded, turn, send,
-                 recv, coef_buf, share_bufs, w_in, w_out, in_sem, out_sem, p_sem, send_sem, recv_sem, share_sems, w_in_sem,
-                 w_out_sem):
+def front_kernel(group, rows_local, field, grad, base, gained, p_fwd, p_inv, w_mix, mixed_out, sums_out, planes_out, coef_shared,
+                 mixed_shared, field_buf, grad_buf, turn, stage, stage_far, expanded_fwd, expanded_inv, flipped, send_f, recv_f,
+                 padded, coef, mixed, w_in, planes, bridged, send_d, recv_d, message, share_send_a, share_send_d, halves,
+                 shared, sums, out_buf, field_sem, grad_sem, p_sem, far_sem, send_f_sem, recv_f_sem, w_sem, planes_sem,
+                 bridged_sems, send_d_sem, recv_d_sem, share_a_sems, share_d_sems, half_sem, out_sem, sums_sem):
     me = lax.axis_index('lat')
     batch = field.shape[0]
     channels = field.shape[1] // rows_local
-
-    def fetch(b):
-        return Halves(field, b, field_buf, lax.rem(b, 2), in_sem)
+    m_local, degrees = stage.shape[:2]
+    used = degrees * m_local
+    bunch = coef.shape[0]
+    sources, share_rows = coef_shared.shape[1:3]
+
+    def fetch_field(b):
+        return Halves(field, b, field_buf, lax.rem(b, 2), field_sem)
+
+    def fetch_grad(b):
+        return Halves(grad, b, grad_buf, lax.rem(b, 2), grad_sem)
 
     def put(b):
-        whole = pl.ds(0, coef_out.shape[2])
-        return pltpu.make_async_copy(coef_buf.at[lax.rem(b, 2), :, whole], coef_out.at[b], out_sem.at[lax.rem(b, 2)])
-
-    per = w_in.shape[1]
-    blocks = w_mix.shape[0] // per
-
-    def fetch_w(k):
-        return pltpu.make_async_copy(w_mix.at[pl.ds(k * per, per)], w_in.at[lax.rem(k, 2)], w_in_sem.at[lax.rem(k, 2)])
-
-    def put_w(k):
-        return pltpu.make_async_copy(w_out.at[lax.rem(k, 2)], w_big.at[pl.ds(k * per, per)], w_out_sem.at[lax.rem(k, 2)])
-
-    fetch(0).start()
-    loading = load_legendre(me, group, p_fwd, stage, p_sem)
-    fetch_w(0).start()
+        return pltpu.make_async_copy(out_buf.at[lax.rem(b, 2)], mixed_out.at[b], out_sem.at[lax.rem(b, 2)])
+
+    def put_planes():
+        return pltpu.make_async_copy(planes, planes_out, planes_sem)
+
+    def fetch_shares(b):
+        slot = lax.rem(b, 2)
+        return [pltpu.make_async_copy(whole.at[b], halves.at[slot, which], half_sem.at[slot, which])
+                for which, whole in enumerate((mixed_shared, coef_shared))]
+
     greet(me, group)
-    share = Share(me, group, batch, *share_bufs, shared, share_sems)
-    clear_after(coef_buf, coef_out.shape[2])
-    swap = Exchange(me, group, batch, send, recv, send_sem, recv_sem)
-    lag = 2
+    fetch_field(0).start()
+    fetch_grad(0).start()
+    loading = own_tables(me, group, p_fwd, stage, p_sem)
+    loading_inv = own_tables(me, group, p_inv, stage, p_sem)
+    loading.start()
+    swap_f = Exchange(me, group, batch, send_f, recv_f, send_f_sem, recv_f_sem)
+    swap_g = BridgedExchange(me, group, batch, bridged, bridged_sems)
+    swap_d = Exchange(me, group, batch, send_d, recv_d, send_d_sem, recv_d_sem)
+    share_a = Share(me, group, batch, share_send_a, message, coef_shared, share_a_sems)
+    share_d = Share(me, group, batch, share_send_d, message, mixed_shared, share_d_sems)
+    loading_far = far_tables(swap_g, p_inv, stage_far, far_sem)
+    loading_far.start()
+    clear_after(padded, used)
     meet(group)
+
+    def build_planes():
+        depth, per = w_in.shape[:2]
+        blocks = degrees // per
+        half = w_in.shape[2] // 2
+
+        def fetch(k):
+            return pltpu.make_async_copy(w_mix.at[pl.ds(k * per, per)], w_in.at[lax.rem(k, depth)], w_sem.at[lax.rem(k, depth)])
+
+        for k in range(depth - 1):
+            fetch(k).start()
+
+        @pl.loop(0, blocks)
+        def _(k):
+            @pl.when(k + depth - 1 < blocks)
+            def _():
+                fetch(k + depth - 1).start()
+
+            fetch(k).wait()
+            for inner in range(per):
+                rows = w_in.at[lax.rem(k, depth), inner]
+                for part in range(2):
+                    planes[k * per + inner, part] = rows[pl.ds(part, half, stride=2), :].astype(BF16)
+
+        put_planes().start()
+
+    def mix_bunch():
+        @pl.loop(0, degrees // 8)
+        def _(k):
+            for inner in range(8):
+                at = pl.ds(pl.multiple_of((k * 8 + inner) * m_local, m_local), m_local)
+                rows = [coef[:, part, at, :].reshape(bunch * m_local, channels) for part in range(2)]
+                res = dot(jnp.concatenate(rows, axis=1).astype(BF16), mix_block(planes[k * 8 + inner]), NT)
+                for part in range(2):
+                    mixed[:, part, at, :] = res[:, part * channels:(part + 1) * channels].reshape(bunch, m_local, channels)
+
+    def weigh_sample(b):
+        for copy in fetch_shares(b):
+            copy.wait()
+        for which in range(2):
+            for source in range(sources):
+                at = pl.ds(source * (shared.shape[1] // sources), share_rows)
+                shared[which, at, :] = halves[lax.rem(b, 2), which, source].astype(F32)
+        weigh(shared, sources, sums, m_local)
+
+    def collect(b):
+        share_a.arrive(b)
+        share_d.arrive(b)
+        for copy in fetch_shares(b):
+            copy.start()
+
+    lag_a, lag_b, lag_c, lag_d = 2, 4, 6, 8
 
     def body(i, carry):
         @pl.when(i < batch)
         def _():
             @pl.when(i + 1 < batch)
             def _():
-                fetch(i + 1).start()
-
-            fetch(i).wait()
+                fetch_field(i + 1).start()
+
+            fetch_field(i).wait()
             half = lax.rem(i, 2)
-            analyse(lambda t: read_row(field_buf, half, t, channels, rows_local), table, turn, rows_local)
-            swap.reserve(i)
-            pack_blocks(turn, send, lax.rem(i, SLOTS))
-            swap.start(i)
+            analyse(lambda t: read_row(field_buf, half, t, channels, rows_local), base, turn, rows_local)
+            swap_f.reserve(i)
+            pack_blocks(turn, send_f, lax.rem(i, SLOTS))
+            swap_f.start(i)
 
         @pl.when(i == 0)
         def _():
             loading.wait()
-            expand_rows(stage, expanded, rows_local)
-
-        @pl.when(i < blocks)
-        def _():
-            fetch_w(i).wait()
-
-            @pl.when(i + 1 < blocks)
+            expand_rows(stage, expanded_fwd, rows_local)
+            loading_inv.start()
+            loading_far.wait()
+            flip_rows(stage_far, swap_g.flipped_far)
+
+        @pl.when(i == 1)
+        def _():
+            build_planes()
+            loading_inv.wait()
+            expand_rows(stage, expanded_inv, rows_local)
+            flip_rows(stage, flipped)
+            sums[...] = jnp.zeros_like(sums)
+
+        @pl.when((i >= lag_a) & (i < batch + lag_a))
+        def _():
+            b = i - lag_a
+            swap_f.arrive(b)
+            legendre_forward(recv_f, b, expanded_fwd, padded, rows_local)
+            coef[lax.rem(b, bunch)] = padded[:, pl.ds(0, used), :]
+            share_a.give(b, padded)
+
+            @pl.when(lax.rem(b, bunch) == bunch - 1)
             def _():
-                fetch_w(i + 1).start()
-
-            @pl.when(i >= 2)
+                mix_bunch()
+
+        @pl.when((i >= lag_b) & (i < batch + lag_b))
+        def _():
+            b = i - lag_b
+            swap_g.reserve(b)
+            legendre_inverse(mixed.at[lax.rem(b, bunch)], flipped, swap_g, lax.rem(b, SLOTS), rows_local)
+            swap_g.start(b)
+
+        @pl.when((i >= lag_b + 1) & (i < batch + lag_b + 1))
+        def _():
+            swap_g.relay(i - lag_b - 1)
+
+        @pl.when((i >= lag_c) & (i < batch + lag_c))
+        def _():
+            b = i - lag_c
+            half = lax.rem(b, 2)
+
+            @pl.when(b + 1 < batch)
             def _():
-                put_w(i - 2).wait()
-
-            half = lax.rem(i, 2)
-
-            @pl.loop(0, per)
-            def _(inner):
-                w_out[half, inner] = mix_block(w_in.at[half, inner])
-
-            put_w(i).start()
-
-        @pl.when(i >= lag)
-        def _():
-            b = i - lag
-            swap.arrive(b)
+                fetch_grad(b + 1).start()
+
+            fetch_grad(b).wait()
+            swap_g.arrive(b)
+            unpack_blocks(swap_g.recv, b, turn)
+            for t in range(rows_local):
+                slope = gelu_slope(synthesise(turn, t, gained, rows_local))
+                given = read_row(grad_buf, half, t, channels, rows_local)
+                write_row(grad_buf, half, t, channels, rows_local, given * slope)
+            analyse(lambda t: read_row(grad_buf, half, t, channels, rows_local), gained, turn, rows_local)
+            swap_d.reserve(b)
+            pack_blocks(turn, send_d, lax.rem(b, SLOTS))
+            swap_d.start(b)
+
+        @pl.when(i >= lag_d)
+        def _():
+            b = i - lag_d
+
+            @pl.when(b >= 2)
+            def _():
+                weigh_sample(b - 2)
+
+            @pl.when(b >= 1)
+            def _():
+                collect(b - 1)
+
+            swap_d.arrive(b)
 
             @pl.when(b >= 2)
             def _():
                 put(b - 2).wait()
 
-            legendre_forward(recv, b, expanded, coef_buf.at[lax.rem(b, 2)], rows_local)
+            legendre_forward(recv_d, b, expanded_inv, padded, rows_local)
+            out_buf[lax.rem(b, 2)] = padded[:, pl.ds(0, used), :]
             put(b).start()
-            share.give(b, coef_buf.at[lax.rem(b, 2)])
+            share_d.give(b, padded)
 
         return carry
 
-    lax.fori_loop(0, batch + lag, body, 0)
-    swap.drain()
-    share.drain()
+    lax.fori_loop(0, batch + lag_d, body, 0)
+    weigh_sample(batch - 2)
+    collect(batch - 1)
+    weigh_sample(batch - 1)
+    total = pltpu.make_async_copy(sums, sums_out, sums_sem)
+    total.start()
+    for swap in (swap_f, swap_g, swap_d, share_a, share_d):
+        swap.drain()
+    put_planes().wait()
     put(batch - 2).wait()
     put(batch - 1).wait()
-    put_w(blocks - 2).wait()
-    put_w(blocks - 1).wait()
+    total.wait()
 
 
 def mix_loop(w_hbm, in_hbms, bufs, w_buf, w_sem, in_sems, blocks, step, meanwhile):
@@ -549,134 +656,6 @@
         return carry
 
     lax.fori_loop(0, blocks, body, 0)
-
-
-def second_kernel(group, rows_local, coef, shared_coef, w_mix, p_inv, table, grad, mixed_out, sums_out, w_buf, coef_blk, mixed,
-                  stage, flipped, expanded, turn, grad_buf, out_buf, bridged, send_b, recv_b, share_bufs, shared_recv, shared_half,
-                  shared, sums, w_sem, c_sem, in_sem, out_sem, p_sem, bridged_sems, send_b_sem, recv_b_sem, share_sems, s_sem,
-                  stage_far, far_sem):
-    me = lax.axis_index('lat')
-    batch = grad.shape[0]
-    channels = grad.shape[1] // rows_local
-    m_local = stage.shape[0]
-    per = w_buf.shape[1]
-    degrees = stage.shape[1]
-
-    def fetch(b):
-        return Halves(grad, b, grad_buf, lax.rem(b, 2), in_sem)
-
-    def put(b):
-        whole = pl.ds(0, mixed_out.shape[2])
-        return pltpu.make_async_copy(out_buf.at[lax.rem(b, 2), :, whole], mixed_out.at[b], out_sem.at[lax.rem(b, 2)])
-
-    greet(me, group)
-    fetch(0).start()
-    swap_a = BridgedExchange(me, group, batch, bridged, bridged_sems)
-    loading = load_legendre(me, group, p_inv, stage, p_sem)
-    loading_far = load_far(swap_a, p_inv, stage_far, far_sem)
-
-    def prepare():
-        sums[...] = jnp.zeros_like(sums)
-        loading.wait()
-        flip_rows(stage, flipped)
-        expand_rows(stage, expanded, rows_local)
-        loading_far.wait()
-        flip_rows(stage_far, swap_a.flipped_far)
-
-    share = Share(me, group, batch, *share_bufs, shared_recv, share_sems, resident=True)
-    clear_after(out_buf, mixed_out.shape[2])
-    sources, share_rows = shared_recv.shape[1:3]
-    def fetch_shared(b):
-        return pltpu.make_async_copy(shared_coef.at[b], shared_half.at[lax.rem(b, 3)], s_sem.at[lax.rem(b, 3)])
-
-    def weigh_sample(b):
-        fetch_shared(b).wait()
-        share.arrive(b)
-        for source in range(sources):
-            at = pl.ds(source * (shared.shape[1] // sources), share_rows)
-            shared[0, at, :] = shared_recv[b, source].astype(F32)
-            shared[1, at, :] = shared_half[lax.rem(b, 3), source].astype(F32)
-        weigh(shared, sources, sums, m_local)
-
-    def mix(k, slot):
-        for inner in range(per):
-            rows = rows_of_degree(coef_blk.at[slot], inner, m_local)
-            res = dot(rows, w_buf[slot, inner], NT)
-            at = pl.ds(pl.multiple_of((k * per + inner) * m_local, m_local), m_local)
-            for part in range(2):
-                lanes = res.shape[1] // 2
-                mixed[:, part, at, :] = res[:, part * lanes:(part + 1) * lanes].reshape(batch, m_local, lanes)
-
-    mix_loop(w_mix, [coef], [coef_blk], w_buf, w_sem, [c_sem], degrees // per, mix, prepare)
-
-    meet(group)
-    swap_b = Exchange(me, group, batch, send_b, recv_b, send_b_sem, recv_b_sem)
-    lag, lag_b = 2, 2
-
-    def body(i, carry):
-        @pl.when(i < batch)
-        def _():
-            swap_a.reserve(i)
-            legendre_inverse(mixed.at[i], flipped, swap_a, lax.rem(i, SLOTS), rows_local)
-            swap_a.start(i)
-
-        @pl.when((i >= 1) & (i < batch + 1))
-        def _():
-            swap_a.relay(i - 1)
-
-        @pl.when((i >= lag) & (i < batch + lag))
-        def _():
-            b = i - lag
-            half = lax.rem(b, 2)
-
-            @pl.when(b + 1 < batch)
-            def _():
-                fetch(b + 1).start()
-
-            fetch(b).wait()
-            swap_a.arrive(b)
-            unpack_blocks(swap_a.recv, b, turn)
-            for t in range(rows_local):
-                slope = gelu_slope(synthesise(turn, t, table, rows_local))
-                given = read_row(grad_buf, half, t, channels, rows_local)
-                write_row(grad_buf, half, t, channels, rows_local, given * slope)
-            analyse(lambda t: read_row(grad_buf, half, t, channels, rows_local), table, turn, rows_local)
-            swap_b.reserve(b)
-            pack_blocks(turn, send_b, lax.rem(b, SLOTS))
-            swap_b.start(b)
-
-        @pl.when(i >= lag + lag_b)
-        def _():
-            b = i - lag - lag_b
-
-            @pl.when(b >= 2)
-            def _():
-                weigh_sample(b - 2)
-
-            swap_b.arrive(b)
-
-            @pl.when(b >= 2)
-            def _():
-                put(b - 2).wait()
-
-            legendre_forward(recv_b, b, expanded, out_buf.at[lax.rem(b, 2)], rows_local)
-            put(b).start()
-            share.give(b, out_buf.at[lax.rem(b, 2)])
-            fetch_shared(b).start()
-
-        return carry
-
-    lax.fori_loop(0, batch + lag + lag_b, body, 0)
-    weigh_sample(batch - 2)
-    weigh_sample(batch - 1)
-    total = pltpu.make_async_copy(sums, sums_out, p_sem)
-    total.start()
-    swap_a.drain()
-    swap_b.drain()
-    share.drain()
-    total.wait()
-    put(batch - 2).wait()
-    put(batch - 1).wait()
 
 
 class WeightSum:
@@ -781,18 +760,20 @@
     greet(me, group)
     total = WeightSum(me, group, sums, got, grad_w, gw_sem)
     swap = BridgedExchange(me, group, batch, bridged, bridged_sems)
-    loading = load_legendre(me, group, p_fwd, stage, p_sem)
-    loading_far = load_far(swap, p_fwd, stage_far, far_sem)
+    loading = own_tables(me, group, p_fwd, stage, p_sem)
+    loading_far = far_tables(swap, p_fwd, stage_far, far_sem)
+    loading.start()
+    loading_far.start()
     load_sums.wait()
     meet(group)
     chunks = sums.shape[0] // 2
-    for k in range(chunks):
+    for k in range(2):
         total.halving(k).start()
 
     def unmix(k, slot):
         for inner in range(per):
             rows = rows_of_degree(mixed_blk.at[slot], inner, m_local)
-            res = dot(rows, w_buf[slot, inner], NN)
+            res = dot(rows, mix_block(w_buf[slot, inner]), NN)
             at = pl.ds(pl.multiple_of((k * per + inner) * m_local, m_local), m_local)
             half = res.shape[1] // 2
             for part in range(2):
@@ -820,13 +801,6 @@
             swap.relay(i - 1)
 
         steps = [total.reduce_step] + [functools.partial(total.gather_step, p) for p in (2, 1, 0, -1)]
-        for late, step in reversed(list(enumerate(steps))):
-            k = i - late
-
-            @pl.when((k >= 0) & (k < chunks))
-            def _():
-                step(k)
-
         @pl.when((i >= lag) & (i < batch + lag))
         def _():
             b = i - lag
@@ -848,6 +822,17 @@
                 given = read_row(grad_buf, half, t, channels, rows_local)
                 write_row(grad_buf, half, t, channels, rows_local, given + added)
             put(b).start()
+
+        @pl.when(i + 2 < chunks)
+        def _():
+            total.halving(i + 2).start()
+
+        for late, step in reversed(list(enumerate(steps))):
+            k = i - late
+
+            @pl.when((k >= 0) & (k < chunks))
+            def _():
+                step(k)
 
         return carry
 
@@ -889,7 +874,6 @@
         stage_t = vmem((m_local, degrees, lats), F32)
         expanded_t = vmem((m_local, 2 * degrees, 2 * lats), BF16)
         flipped_t = vmem((m_local, lats, degrees), BF16)
-        pair_t = vmem((2, 2, degrees * m_local, channels), F32)
         field_t = vmem((2, lon_count // LANES, channels * rows_local, LANES), F32)
         table_spec = pl.BlockSpec(memory_space=pltpu.VMEM)
         any_spec = pl.BlockSpec(memory_space=pl.ANY)
@@ -904,36 +888,31 @@
         ranks = group // 2
         share_rows = (m_local + 1) * 2 * ranks
         share_out = jax.ShapeDtypeStruct((batch, ranks, share_rows, channels), BF16)
-        share_t = (vmem((SLOTS, ranks, share_rows, channels), BF16), vmem((ranks, share_rows, channels), F32))
         share_sems = (dma((SLOTS,)), dma((batch,)), dma((SLOTS,)))
-        padded_t = vmem((2, 2, 2 * degrees * m_local, channels), F32)
-
-        w_wide = 16
-        big_shape = (2 * channels, 2 * channels)
+
+        blk_t = vmem((DEPTH, batch, 2, per * m_local, channels), F32)
+        w_t = vmem((DEPTH, per, 2, channels, channels), BF16)
         far_stage_t = vmem((late, degrees, lats), F32)
-        coef, shared_coef, w_big = pl.pallas_call(
-            functools.partial(first_kernel, group, rows_local), name='first',
-            out_shape=[jax.ShapeDtypeStruct(coef_shape, F32), share_out, jax.ShapeDtypeStruct((degrees,) + big_shape, BF16)],
-            in_specs=[any_spec, table_spec, any_spec, any_spec], out_specs=[any_spec] * 3,
-            scratch_shapes=[field_t, stage_t, expanded_t, turn_t, send_t, recv_t, padded_t, share_t,
-                            vmem((2, w_wide, 2 * channels, channels), F32), vmem((2, w_wide) + big_shape, BF16),
-                            dma((2, 2)), dma((2,)), dma(()), dma((SLOTS,)), dma((batch,)), share_sems, dma((2,)), dma((2,))],
-            compiler_params=params(0))(field, base, p_fwd, w_rows)
-
-        blk_t = vmem((DEPTH, batch, 2, per * m_local, channels), F32)
-        w_t = vmem((DEPTH, per) + big_shape, BF16)
         steps = degrees // ranks
         sums_shape = (steps, channels * 2, channels)
-        mixed, sums = pl.pallas_call(
-            functools.partial(second_kernel, group, rows_local), name='second',
-            out_shape=[jax.ShapeDtypeStruct(coef_shape, F32), jax.ShapeDtypeStruct(sums_shape, F32)],
-            in_specs=[any_spec] * 4 + [table_spec, any_spec], out_specs=[any_spec] * 2,
-            scratch_shapes=[w_t, blk_t, vmem(coef_shape, F32), stage_t, flipped_t, expanded_t, turn_t, field_t, padded_t,
-                            bridged_t, send_t, recv_t, share_t, vmem(share_out.shape, BF16), vmem((3,) + share_out.shape[1:], BF16),
-                            vmem((2, ranks * (share_rows + 8), channels), F32), vmem(sums_shape, F32),
-                            dma((DEPTH,)), dma((DEPTH,)), dma((2, 2)), dma((2,)), dma(()),
-                            bridged_sems, dma((SLOTS,)), dma((batch,)), share_sems, dma((3,)), far_stage_t, dma(())],
-            compiler_params=params(1))(coef, shared_coef, w_big, p_inv, gained, grad)
+        planes_shape = (degrees, 2, channels, channels)
+        single_t = vmem((BUNCH,) + coef_shape[1:], F32)
+        share_send_t = vmem((SLOTS, ranks, share_rows, channels), BF16)
+        swap_sems = (dma((SLOTS,)), dma((batch,)))
+        mixed, sums, planes, _, _ = pl.pallas_call(
+            functools.partial(front_kernel, group, rows_local), name='front',
+            out_shape=[jax.ShapeDtypeStruct(coef_shape, F32), jax.ShapeDtypeStruct(sums_shape, F32),
+                       jax.ShapeDtypeStruct(planes_shape, BF16), share_out, share_out],
+            in_specs=[any_spec, any_spec, table_spec, table_spec, any_spec, any_spec, any_spec], out_specs=[any_spec] * 5,
+            scratch_shapes=[field_t, field_t, turn_t, stage_t, far_stage_t, expanded_t, expanded_t, flipped_t, send_t, recv_t,
+                            vmem((2, 2 * degrees * m_local, channels), F32), single_t, single_t,
+                            vmem((4, 4, channels * 2, channels), F32), vmem(planes_shape, BF16), bridged_t, send_t, recv_t,
+                            vmem((ranks, share_rows, channels), F32), share_send_t, share_send_t,
+                            vmem((2, 2) + share_out.shape[1:], BF16), vmem((2, ranks * (share_rows + 8), channels), F32),
+                            vmem(sums_shape, F32), vmem((2,) + coef_shape[1:], F32),
+                            dma((2, 2)), dma((2, 2)), dma(()), dma(()), *swap_sems, dma((4,)), dma(()), bridged_sems, *swap_sems,
+                            share_sems, share_sems, dma((2, 2)), dma((2,)), dma(())],
+            compiler_params=params(0))(field, grad, base, gained, p_fwd, p_inv, w_rows)
 
         w_rect = (channels * 2, channels)
         field_out, gw_total = pl.pallas_call(
@@ -944,7 +923,7 @@
                             vmem((3, lon_count // LANES, channels * rows_local, LANES), F32), bridged_t,
                             dma((DEPTH,)), dma((DEPTH,)), dma(()), dma((2, 6, steps // 2)), dma((3, 2)), dma((3, 2)), dma(()),
                             bridged_sems, far_stage_t, dma(())],
-            compiler_params=params(2))(mixed, sums, w_big, p_fwd, base, grad)
+            compiler_params=params(2))(mixed, sums, planes, p_fwd, base, grad)
 
         grad_wmix = jnp.swapaxes(gw_total.reshape(degrees, channels, 2, channels), 2, 3)
         return field_out.reshape(grad_loc.shape), grad_wmix

time: 690 us -> 659 us (0.955)
  Pallas kernels: 666 us -> 635 us
    pallas_call x2 -> x1, Pallas kernels: 429 us -> 407 us  [local_step(): pl.pallas_call(functools.partial(front_kernel, group, rows_local), name='...]
    pallas_call x1, Pallas kernels: 237 us -> 228 us  [local_step(): pl.pallas_call(functools.partial(third_kernel, group, rows_local), name='...]
where the time goes in v7:
time: 659 us; the launch traced here: 657 us
  Pallas kernels  635 us (96%)
  local copies, waits for them, and re-layouts  22.2 us (3%)
    pallas_call x1, Pallas kernels, local_step(): pl.pallas_call(functools.partial(front_kernel, group, rows_local), name='...  407 us
    pallas_call x1, Pallas kernels, local_step(): pl.pallas_call(functools.partial(third_kernel, group, rows_local), name='...  228 us
    unnamed x2, local copies, waits for them, and re-layouts  22.2 us

profile of v7, /device:TPU:0, one launch (start us, length us, event | category | flops | bytes accessed | tf_op | source)
XLA Modules:
  0.0 657.4 jit_solution(7729095958057886557)
XLA Ops:
  0.6 406.8 %front.1 = (f32[12,2,1024,128]{3,2,1,0:T(8,128)}, f32[16,256,128]{2,1,0:T(8,128)}, bf16[128,2,128,128]{3,2,1,0:T(8,128)(2,1)}, bf16[12,8,144,128]{3,2,1,0:T(8,128)(2,1)}, bf16[12,8,144,128]{3,2,1,0:T(8,128)(2,1)}) custom-call(f32[12,1024,256]{2,1,0:T(8,128)} %bitcast.13, f32[12,1024,256]{2,1,0:T(8,128)} %bitcast.9, ...), custom_call_target="tpu_custom_call" | custom-call | tf_op jit(solution)/shard_map/front/pallas_call | solution.py:902
  407.4 227.8 %third.1 = (f32[12,1024,256]{2,1,0:T(8,128)}, f32[16,8,256,128]{3,2,1,0:T(8,128)}) custom-call(f32[12,2,1024,128]{3,2,1,0:T(8,128)} %get-tuple-element.7.mixed, f32[16,256,128]{2,1,0:T(8,128)} %get-tuple-element.8.part_sums, bf16[128,2,128,128]{3,2,1,0:T(8,128)(2,1)} %get-tuple-element.9.w_mix, f32[128,128,128]{2,1,0:T(8,128)} %p_fwd.3, ...), custom_call_target="tpu_custom_call" | custom-call | tf_op jit(solution)/shard_map/third/pallas_call | solution.py:918
  635.2 10.2 %copy.11 = f32[12,128,8,256]{3,2,1,0:T(8,128)} copy(f32[12,128,8,256]{3,2,1,0:T(8,128)} %bitcast.14) | data formatting | bytes 25165824
  645.4 12.0 %copy.12 = f32[128,128,128,2]{2,3,1,0:T(2,128)} copy(f32[128,128,128,2]{2,3,1,0:T(2,128)} %bitcast.12) | data formatting | bytes 33554432

commit v8 on v7

--- a/solution.py
+++ b/solution.py
@@ -14,6 +14,8 @@
 SLOTS = 3
 DEPTH = 4
 BUNCH = 3
+PIECES = 2
+RING = 6
 VMEM_LIMIT = 60 * 1024 * 1024
 F32 = jnp.float32
 BF16 = jnp.bfloat16
@@ -100,7 +102,7 @@
 
         @pl.loop(1, self.group)
         def _(step):
-            target = lax.rem(self.me + step, self.group)
+            target = jnp.bitwise_xor(self.me, self.group - step)
             pltpu.make_async_remote_copy(
                 self.send.at[slot, target], self.recv.at[b, self.me], self.send_sem.at[slot], self.recv_sem.at[b],
                 device_id={'lat': target}, device_id_type=MESH).start()
@@ -162,13 +164,13 @@
 
         @pl.loop(0, self.half_size)
         def _(step):
-            target = (1 - self.half) * self.half_size + lax.rem(self.place + step, self.half_size)
+            target = jnp.bitwise_xor(self.me, 2 * self.half_size - 1 - step)
             self.copy(self.send.at[slot, target, early], self.recv.at[b, self.me, early], self.send_sem.at[slot],
                       self.recv_sem.at[b], target).start()
 
         @pl.loop(1, self.half_size)
         def _(step):
-            target = self.half * self.half_size + lax.rem(self.place + step, self.half_size)
+            target = jnp.bitwise_xor(self.me, self.half_size - step)
             self.copy(self.send.at[slot, target], self.recv.at[b, self.me], self.send_sem.at[slot], self.recv_sem.at[b],
                       target).start()
 
@@ -201,7 +203,7 @@
 
         @pl.loop(1, self.half_size)
         def _(step):
-            place = lax.rem(self.place + step, self.half_size)
+            place = jnp.bitwise_xor(self.place, self.half_size - step)
             self.copy(self.relay_send.at[slot, place], self.recv.at[b, self.twin, late_at], self.relay_send_sem.at[slot],
                       self.relay_recv_sem.at[b], self.half * self.half_size + place).start()
 
@@ -271,7 +273,7 @@
 
         @pl.loop(1, size)
         def _(step):
-            place = lax.rem(self.place + step, size)
+            place = jnp.bitwise_xor(self.place, size - step)
             self.copy(slot_b, self.rank(place), b, self.place, place).start()
 
         self.keep(b).wait()
@@ -675,25 +677,34 @@
                                             device_id=self.peer(phase), device_id_type=MESH)
 
     def halving(self, k):
-        return self.remote(3, k, self.sums.at[2 * k + 1 - self.far], self.got.at[k], 4)
+        pair, at = self.piece(k)
+        return self.remote(3, k, self.sums.at[2 * pair + 1 - self.far, at], self.got.at[k], 4)
+
+    def piece(self, k):
+        rows = self.got.shape[1]
+        pieces = self.sums.shape[1] // rows
+        return k // pieces, pl.ds(pl.multiple_of(lax.rem(k, pieces) * rows, rows), rows)
 
     def settle(self, k):
-        mine = 2 * k + self.far
-        return pltpu.make_async_copy(self.sums.at[mine], self.out.at[mine, self.rank], self.sems.at[0, 5, k])
+        pair, at = self.piece(k)
+        mine = 2 * pair + self.far
+        return pltpu.make_async_copy(self.sums.at[mine, at], self.out.at[mine, self.rank, at], self.sems.at[0, 5, k])
 
     def doubling(self, phase, k):
+        pair, at = self.piece(k)
         if phase == 3:
-            mine = 2 * k + self.far
-            return self.remote(3, k, self.sums.at[mine], self.out.at[mine, self.rank], 3)
+            mine = 2 * pair + self.far
+            return self.remote(3, k, self.sums.at[mine, at], self.out.at[mine, self.rank, at], 3)
         width = (4, 2, 1)[phase]
         first = (4 * self.core, 4 * self.core + 2 * self.y, self.rank)[phase]
-        span = self.out.at[pl.ds(2 * k, 2), pl.ds(first, width)]
+        span = self.out.at[pl.ds(2 * pair, 2), pl.ds(first, width), at]
         return self.remote(phase, k, span, span, phase)
 
     def reduce_step(self, k):
         self.halving(k).wait()
-        mine = 2 * k + self.far
-        self.sums[mine] = self.sums[mine] + self.got[k]
+        pair, at = self.piece(k)
+        mine = 2 * pair + self.far
+        self.sums[mine, at] = self.sums[mine, at] + self.got[k]
         self.settle(k).start()
         self.doubling(3, k).start()
 
@@ -766,8 +777,8 @@
     loading_far.start()
     load_sums.wait()
     meet(group)
-    chunks = sums.shape[0] // 2
-    for k in range(2):
+    chunks = got.shape[0]
+    for k in range(4):
         total.halving(k).start()
 
     def unmix(k, slot):
@@ -790,6 +801,22 @@
     lag = 2
 
     def body(i, carry):
+        steps = [total.reduce_step] + [functools.partial(total.gather_step, p) for p in (2, 1, 0, -1)]
+        steps = [total.reduce_step] + [functools.partial(total.gather_step, p) for p in (2, 1, 0, -1)]
+        def advance(sub):
+            @pl.when(i * 2 + sub + 4 < chunks)
+            def _():
+                total.halving(i * 2 + sub + 4).start()
+
+            for late, step in reversed(list(enumerate(steps))):
+                k = (i - late) * 2 + sub
+
+                @pl.when((k >= 0) & (k < chunks))
+                def _():
+                    step(k)
+
+        advance(0)
+
         @pl.when(i < batch)
         def _():
             swap.reserve(i)
@@ -800,7 +827,7 @@
         def _():
             swap.relay(i - 1)
 
-        steps = [total.reduce_step] + [functools.partial(total.gather_step, p) for p in (2, 1, 0, -1)]
+
         @pl.when((i >= lag) & (i < batch + lag))
         def _():
             b = i - lag
@@ -823,23 +850,40 @@
                 write_row(grad_buf, half, t, channels, rows_local, given + added)
             put(b).start()
 
-        @pl.when(i + 2 < chunks)
-        def _():
-            total.halving(i + 2).start()
-
-        for late, step in reversed(list(enumerate(steps))):
-            k = i - late
-
-            @pl.when((k >= 0) & (k < chunks))
-            def _():
-                step(k)
-
+        advance(1)
         return carry
 
-    lax.fori_loop(0, max(batch + lag, chunks + 4), body, 0)
+    lax.fori_loop(0, max(batch + lag, chunks // 2 + 4), body, 0)
     swap.drain()
     for b in range(batch - depth + 1, batch):
         put(b).wait()
+
+
+def finish_kernel(first, second, first_out, second_out, first_ring, second_ring, in_sem, out_sem):
+    depth = first_ring.shape[0]
+    pieces = []
+    for side, (source, target, ring) in enumerate(((first, first_out, first_ring), (second, second_out, second_ring))):
+        for n in range(source.shape[0]):
+            slot = n % depth
+            take = pltpu.make_async_copy(source.at[n], ring.at[slot], in_sem.at[side, slot])
+            give = pltpu.make_async_copy(ring.at[slot], target.at[n], out_sem.at[side, slot])
+            pieces.append(((n, side), (side, n), take, give))
+    pieces.sort(key=lambda piece: piece[0])
+    given = {piece[1]: piece[3] for piece in pieces}
+    waited = set()
+    for k in range(len(pieces) + depth):
+        if k < len(pieces):
+            _, (side, n), take, _ = pieces[k]
+            if n >= depth:
+                given[side, n - depth].wait()
+                waited.add((side, n - depth))
+            take.start()
+        if k >= depth:
+            pieces[k - depth][2].wait()
+            pieces[k - depth][3].start()
+    for _, place, _, give in pieces:
+        if place not in waited:
+            give.wait()
 
 
 def any_specs(n):
@@ -919,12 +963,19 @@
             functools.partial(third_kernel, group, rows_local), name='third',
             out_shape=[jax.ShapeDtypeStruct(grad.shape, F32), jax.ShapeDtypeStruct((steps, ranks) + w_rect, F32)],
             in_specs=[any_spec] * 4 + [table_spec, any_spec], out_specs=[any_spec] * 2,
-            scratch_shapes=[w_t, blk_t, vmem(sums_shape, F32), vmem((steps // 2,) + w_rect, F32), vmem(coef_shape, F32), stage_t, flipped_t, turn_t,
+            scratch_shapes=[w_t, blk_t, vmem(sums_shape, F32), vmem((PIECES * steps // 2, channels * 2 // PIECES, channels), F32), vmem(coef_shape, F32), stage_t, flipped_t, turn_t,
                             vmem((3, lon_count // LANES, channels * rows_local, LANES), F32), bridged_t,
-                            dma((DEPTH,)), dma((DEPTH,)), dma(()), dma((2, 6, steps // 2)), dma((3, 2)), dma((3, 2)), dma(()),
+                            dma((DEPTH,)), dma((DEPTH,)), dma(()), dma((2, 6, PIECES * steps // 2)), dma((3, 2)), dma((3, 2)), dma(()),
                             bridged_sems, far_stage_t, dma(())],
             compiler_params=params(2))(mixed, sums, planes, p_fwd, base, grad)
 
+        gw_total = gw_total.reshape(steps, ranks * channels * 2, channels)
+        results = [jax.ShapeDtypeStruct(whole.shape, F32) for whole in (field_out, gw_total)]
+        field_out, gw_total = pl.pallas_call(
+            finish_kernel, name='finish', out_shape=results, in_specs=[any_spec] * 2, out_specs=[any_spec] * 2,
+            scratch_shapes=[vmem((RING,) + whole.shape[1:], F32) for whole in results] + [dma((2, RING)), dma((2, RING))],
+            compiler_params=params())(field_out, gw_total)
+
         grad_wmix = jnp.swapaxes(gw_total.reshape(degrees, channels, 2, channels), 2, 3)
         return field_out.reshape(grad_loc.shape), grad_wmix
 

time: 659 us -> 644 us (0.977)
  local copies, waits for them, and re-layouts: 22.2 us -> 0 us
    unnamed x2 -> x0, local copies, waits for them, and re-layouts: 22.2 us -> none
    pallas_call x0 -> x1, Pallas kernels: none -> 19.7 us  [local_step(): pl.pallas_call(finish_kernel, name='finish', out_shape=results, in_specs=...]
    pallas_call x1, Pallas kernels: 228 us -> 216 us  [local_step(): pl.pallas_call(functools.partial(third_kernel, group, rows_local), name='...]
where the time goes in v8:
time: 644 us; the launch traced here: 641 us
  Pallas kernels  641 us (100%)
    pallas_call x1, Pallas kernels, local_step(): pl.pallas_call(functools.partial(front_kernel, group, rows_local), name='...  404 us
    pallas_call x1, Pallas kernels, local_step(): pl.pallas_call(functools.partial(third_kernel, group, rows_local), name='...  216 us
    pallas_call x1, Pallas kernels, local_step(): pl.pallas_call(finish_kernel, name='finish', out_shape=results, in_specs=...  19.7 us

profile of v8, /device:TPU:0, one launch (start us, length us, event | category | flops | bytes accessed | tf_op | source)
XLA Modules:
  0.0 641.2 jit_solution(15118808995637217529)
XLA Ops:
  0.6 404.4 %front.1 = (f32[12,2,1024,128]{3,2,1,0:T(8,128)}, f32[16,256,128]{2,1,0:T(8,128)}, bf16[128,2,128,128]{3,2,1,0:T(8,128)(2,1)}, bf16[12,8,144,128]{3,2,1,0:T(8,128)(2,1)}, bf16[12,8,144,128]{3,2,1,0:T(8,128)(2,1)}) custom-call(f32[12,1024,256]{2,1,0:T(8,128)} %bitcast.14, f32[12,1024,256]{2,1,0:T(8,128)} %bitcast.10, ...), custom_call_target="tpu_custom_call" | custom-call | tf_op jit(solution)/shard_map/front/pallas_call | solution.py:946
  405.0 216.5 %third.1 = (f32[12,1024,256]{2,1,0:T(8,128)}, f32[16,8,256,128]{3,2,1,0:T(8,128)}) custom-call(f32[12,2,1024,128]{3,2,1,0:T(8,128)} %get-tuple-element.9.mixed, f32[16,256,128]{2,1,0:T(8,128)} %get-tuple-element.10.part_sums, bf16[128,2,128,128]{3,2,1,0:T(8,128)(2,1)} %get-tuple-element.11.w_mix, f32[128,128,128]{2,1,0:T(8,128)} %p_fwd.3, ...), custom_call_target="tpu_custom_call" | custom-call | tf_op jit(solution)/shard_map/third/pallas_call | solution.py:962
  621.5 19.7 %finish.1 = (f32[12,1024,256]{2,1,0:T(8,128)}, f32[16,2048,128]{2,1,0:T(8,128)}) custom-call(f32[12,1024,256]{2,1,0:T(8,128)} %get-tuple-element.12.first, f32[16,2048,128]{2,1,0:T(8,128)} %bitcast.13), custom_call_target="tpu_custom_call" | custom-call | tf_op jit(solution)/shard_map/finish/pallas_call | solution.py:974

commit v9 on v7

--- a/solution.py
+++ b/solution.py
@@ -12,9 +12,10 @@
 MESH = pl.DeviceIdType.MESH
 LANES = 128
 SLOTS = 3
-DEPTH = 4
 BUNCH = 3
-VMEM_LIMIT = 60 * 1024 * 1024
+PIECES = 2
+RING = 6
+VMEM_LIMIT = 67043328
 F32 = jnp.float32
 BF16 = jnp.bfloat16
 
@@ -100,7 +101,7 @@
 
         @pl.loop(1, self.group)
         def _(step):
-            target = lax.rem(self.me + step, self.group)
+            target = jnp.bitwise_xor(self.me, self.group - step)
             pltpu.make_async_remote_copy(
                 self.send.at[slot, target], self.recv.at[b, self.me], self.send_sem.at[slot], self.recv_sem.at[b],
                 device_id={'lat': target}, device_id_type=MESH).start()
@@ -162,13 +163,13 @@
 
         @pl.loop(0, self.half_size)
         def _(step):
-            target = (1 - self.half) * self.half_size + lax.rem(self.place + step, self.half_size)
+            target = jnp.bitwise_xor(self.me, 2 * self.half_size - 1 - step)
             self.copy(self.send.at[slot, target, early], self.recv.at[b, self.me, early], self.send_sem.at[slot],
                       self.recv_sem.at[b], target).start()
 
         @pl.loop(1, self.half_size)
         def _(step):
-            target = self.half * self.half_size + lax.rem(self.place + step, self.half_size)
+            target = jnp.bitwise_xor(self.me, self.half_size - step)
             self.copy(self.send.at[slot, target], self.recv.at[b, self.me], self.send_sem.at[slot], self.recv_sem.at[b],
                       target).start()
 
@@ -201,7 +202,7 @@
 
         @pl.loop(1, self.half_size)
         def _(step):
-            place = lax.rem(self.place + step, self.half_size)
+            place = jnp.bitwise_xor(self.place, self.half_size - step)
             self.copy(self.relay_send.at[slot, place], self.recv.at[b, self.twin, late_at], self.relay_send_sem.at[slot],
                       self.relay_recv_sem.at[b], self.half * self.half_size + place).start()
 
@@ -271,7 +272,7 @@
 
         @pl.loop(1, size)
         def _(step):
-            place = lax.rem(self.place + step, size)
+            place = jnp.bitwise_xor(self.place, size - step)
             self.copy(slot_b, self.rank(place), b, self.place, place).start()
 
         self.keep(b).wait()
@@ -410,254 +411,6 @@
     return jnp.concatenate([jnp.concatenate([real, -imag], axis=1), jnp.concatenate([imag, real], axis=1)], axis=0)
 
 
-def rows_of_degree(block, inner, m_local):
-    batch = block.shape[0]
-    lanes = block.shape[-1]
-    parts = [block[:, part, pl.ds(inner * m_local, m_local), :].reshape(batch * m_local, lanes) for part in range(2)]
-    return jnp.concatenate(parts, axis=1).astype(BF16)
-
-
-def front_kernel(group, rows_local, field, grad, base, gained, p_fwd, p_inv, w_mix, mixed_out, sums_out, planes_out, coef_shared,
-                 mixed_shared, field_buf, grad_buf, turn, stage, stage_far, expanded_fwd, expanded_inv, flipped, send_f, recv_f,
-                 padded, coef, mixed, w_in, planes, bridged, send_d, recv_d, message, share_send_a, share_send_d, halves,
-                 shared, sums, out_buf, field_sem, grad_sem, p_sem, far_sem, send_f_sem, recv_f_sem, w_sem, planes_sem,
-                 bridged_sems, send_d_sem, recv_d_sem, share_a_sems, share_d_sems, half_sem, out_sem, sums_sem):
-    me = lax.axis_index('lat')
-    batch = field.shape[0]
-    channels = field.shape[1] // rows_local
-    m_local, degrees = stage.shape[:2]
-    used = degrees * m_local
-    bunch = coef.shape[0]
-    sources, share_rows = coef_shared.shape[1:3]
-
-    def fetch_field(b):
-        return Halves(field, b, field_buf, lax.rem(b, 2), field_sem)
-
-    def fetch_grad(b):
-        return Halves(grad, b, grad_buf, lax.rem(b, 2), grad_sem)
-
-    def put(b):
-        return pltpu.make_async_copy(out_buf.at[lax.rem(b, 2)], mixed_out.at[b], out_sem.at[lax.rem(b, 2)])
-
-    def put_planes():
-        return pltpu.make_async_copy(planes, planes_out, planes_sem)
-
-    def fetch_shares(b):
-        slot = lax.rem(b, 2)
-        return [pltpu.make_async_copy(whole.at[b], halves.at[slot, which], half_sem.at[slot, which])
-                for which, whole in enumerate((mixed_shared, coef_shared))]
-
-    greet(me, group)
-    fetch_field(0).start()
-    fetch_grad(0).start()
-    loading = own_tables(me, group, p_fwd, stage, p_sem)
-    loading_inv = own_tables(me, group, p_inv, stage, p_sem)
-    loading.start()
-    swap_f = Exchange(me, group, batch, send_f, recv_f, send_f_sem, recv_f_sem)
-    swap_g = BridgedExchange(me, group, batch, bridged, bridged_sems)
-    swap_d = Exchange(me, group, batch, send_d, recv_d, send_d_sem, recv_d_sem)
-    share_a = Share(me, group, batch, share_send_a, message, coef_shared, share_a_sems)
-    share_d = Share(me, group, batch, share_send_d, message, mixed_shared, share_d_sems)
-    loading_far = far_tables(swap_g, p_inv, stage_far, far_sem)
-    loading_far.start()
-    clear_after(padded, used)
-    meet(group)
-
-    def build_planes():
-        depth, per = w_in.shape[:2]
-        blocks = degrees // per
-        half = w_in.shape[2] // 2
-
-        def fetch(k):
-            return pltpu.make_async_copy(w_mix.at[pl.ds(k * per, per)], w_in.at[lax.rem(k, depth)], w_sem.at[lax.rem(k, depth)])
-
-        for k in range(depth - 1):
-            fetch(k).start()
-
-        @pl.loop(0, blocks)
-        def _(k):
-            @pl.when(k + depth - 1 < blocks)
-            def _():
-                fetch(k + depth - 1).start()
-
-            fetch(k).wait()
-            for inner in range(per):
-                rows = w_in.at[lax.rem(k, depth), inner]
-                for part in range(2):
-                    planes[k * per + inner, part] = rows[pl.ds(part, half, stride=2), :].astype(BF16)
-
-        put_planes().start()
-
-    def mix_bunch():
-        @pl.loop(0, degrees // 8)
-        def _(k):
-            for inner in range(8):
-                at = pl.ds(pl.multiple_of((k * 8 + inner) * m_local, m_local), m_local)
-                rows = [coef[:, part, at, :].reshape(bunch * m_local, channels) for part in range(2)]
-                res = dot(jnp.concatenate(rows, axis=1).astype(BF16), mix_block(planes[k * 8 + inner]), NT)
-                for part in range(2):
-                    mixed[:, part, at, :] = res[:, part * channels:(part + 1) * channels].reshape(bunch, m_local, channels)
-
-    def weigh_sample(b):
-        for copy in fetch_shares(b):
-            copy.wait()
-        for which in range(2):
-            for source in range(sources):
-                at = pl.ds(source * (shared.shape[1] // sources), share_rows)
-                shared[which, at, :] = halves[lax.rem(b, 2), which, source].astype(F32)
-        weigh(shared, sources, sums, m_local)
-
-    def collect(b):
-        share_a.arrive(b)
-        share_d.arrive(b)
-        for copy in fetch_shares(b):
-            copy.start()
-
-    lag_a, lag_b, lag_c, lag_d = 2, 4, 6, 8
-
-    def body(i, carry):
-        @pl.when(i < batch)
-        def _():
-            @pl.when(i + 1 < batch)
-            def _():
-                fetch_field(i + 1).start()
-
-            fetch_field(i).wait()
-            half = lax.rem(i, 2)
-            analyse(lambda t: read_row(field_buf, half, t, channels, rows_local), base, turn, rows_local)
-            swap_f.reserve(i)
-            pack_blocks(turn, send_f, lax.rem(i, SLOTS))
-            swap_f.start(i)
-
-        @pl.when(i == 0)
-        def _():
-            loading.wait()
-            expand_rows(stage, expanded_fwd, rows_local)
-            loading_inv.start()
-            loading_far.wait()
-            flip_rows(stage_far, swap_g.flipped_far)
-
-        @pl.when(i == 1)
-        def _():
-            build_planes()
-            loading_inv.wait()
-            expand_rows(stage, expanded_inv, rows_local)
-            flip_rows(stage, flipped)
-            sums[...] = jnp.zeros_like(sums)
-
-        @pl.when((i >= lag_a) & (i < batch + lag_a))
-        def _():
-            b = i - lag_a
-            swap_f.arrive(b)
-            legendre_forward(recv_f, b, expanded_fwd, padded, rows_local)
-            coef[lax.rem(b, bunch)] = padded[:, pl.ds(0, used), :]
-            share_a.give(b, padded)
-
-            @pl.when(lax.rem(b, bunch) == bunch - 1)
-            def _():
-                mix_bunch()
-
-        @pl.when((i >= lag_b) & (i < batch + lag_b))
-        def _():
-            b = i - lag_b
-            swap_g.reserve(b)
-            legendre_inverse(mixed.at[lax.rem(b, bunch)], flipped, swap_g, lax.rem(b, SLOTS), rows_local)
-            swap_g.start(b)
-
-        @pl.when((i >= lag_b + 1) & (i < batch + lag_b + 1))
-        def _():
-            swap_g.relay(i - lag_b - 1)
-
-        @pl.when((i >= lag_c) & (i < batch + lag_c))
-        def _():
-            b = i - lag_c
-            half = lax.rem(b, 2)
-
-            @pl.when(b + 1 < batch)
-            def _():
-                fetch_grad(b + 1).start()
-
-            fetch_grad(b).wait()
-            swap_g.arrive(b)
-            unpack_blocks(swap_g.recv, b, turn)
-            for t in range(rows_local):
-                slope = gelu_slope(synthesise(turn, t, gained, rows_local))
-                given = read_row(grad_buf, half, t, channels, rows_local)
-                write_row(grad_buf, half, t, channels, rows_local, given * slope)
-            analyse(lambda t: read_row(grad_buf, half, t, channels, rows_local), gained, turn, rows_local)
-            swap_d.reserve(b)
-            pack_blocks(turn, send_d, lax.rem(b, SLOTS))
-            swap_d.start(b)
-
-        @pl.when(i >= lag_d)
-        def _():
-            b = i - lag_d
-
-            @pl.when(b >= 2)
-            def _():
-                weigh_sample(b - 2)
-
-            @pl.when(b >= 1)
-            def _():
-                collect(b - 1)
-
-            swap_d.arrive(b)
-
-            @pl.when(b >= 2)
-            def _():
-                put(b - 2).wait()
-
-            legendre_forward(recv_d, b, expanded_inv, padded, rows_local)
-            out_buf[lax.rem(b, 2)] = padded[:, pl.ds(0, used), :]
-            put(b).start()
-            share_d.give(b, padded)
-
-        return carry
-
-    lax.fori_loop(0, batch + lag_d, body, 0)
-    weigh_sample(batch - 2)
-    collect(batch - 1)
-    weigh_sample(batch - 1)
-    total = pltpu.make_async_copy(sums, sums_out, sums_sem)
-    total.start()
-    for swap in (swap_f, swap_g, swap_d, share_a, share_d):
-        swap.drain()
-    put_planes().wait()
-    put(batch - 2).wait()
-    put(batch - 1).wait()
-    total.wait()
-
-
-def mix_loop(w_hbm, in_hbms, bufs, w_buf, w_sem, in_sems, blocks, step, meanwhile):
-    depth, per = w_buf.shape[:2]
-
-    def copies(k):
-        slot = lax.rem(k, depth)
-        out = [pltpu.make_async_copy(w_hbm.at[pl.ds(k * per, per)], w_buf.at[slot], w_sem.at[slot])]
-        for src, buf, sem in zip(in_hbms, bufs, in_sems):
-            rows = buf.shape[3]
-            out.append(pltpu.make_async_copy(src.at[:, :, pl.ds(k * rows, rows), :], buf.at[slot], sem.at[slot]))
-        return out
-
-    for k in range(depth - 1):
-        for copy in copies(k):
-            copy.start()
-    meanwhile()
-
-    def body(k, carry):
-        @pl.when(k + depth - 1 < blocks)
-        def _():
-            for copy in copies(k + depth - 1):
-                copy.start()
-
-        for copy in copies(k):
-            copy.wait()
-        step(k, lax.rem(k, depth))
-        return carry
-
-    lax.fori_loop(0, blocks, body, 0)
-
-
 class WeightSum:
     def __init__(self, me, group, sums, got, out, sems):
         self.me, self.sums, self.got, self.out, self.sems = me, sums, got, out, sems
@@ -675,25 +428,34 @@
                                             device_id=self.peer(phase), device_id_type=MESH)
 
     def halving(self, k):
-        return self.remote(3, k, self.sums.at[2 * k + 1 - self.far], self.got.at[k], 4)
+        pair, at = self.piece(k)
+        return self.remote(3, k, self.sums.at[2 * pair + 1 - self.far, at], self.got.at[k], 4)
+
+    def piece(self, k):
+        rows = self.got.shape[1]
+        pieces = self.sums.shape[1] // rows
+        return k // pieces, pl.ds(pl.multiple_of(lax.rem(k, pieces) * rows, rows), rows)
 
     def settle(self, k):
-        mine = 2 * k + self.far
-        return pltpu.make_async_copy(self.sums.at[mine], self.out.at[mine, self.rank], self.sems.at[0, 5, k])
+        pair, at = self.piece(k)
+        mine = 2 * pair + self.far
+        return pltpu.make_async_copy(self.sums.at[mine, at], self.out.at[mine, self.rank, at], self.sems.at[0, 5, k])
 
     def doubling(self, phase, k):
+        pair, at = self.piece(k)
         if phase == 3:
-            mine = 2 * k + self.far
-            return self.remote(3, k, self.sums.at[mine], self.out.at[mine, self.rank], 3)
+            mine = 2 * pair + self.far
+            return self.remote(3, k, self.sums.at[mine, at], self.out.at[mine, self.rank, at], 3)
         width = (4, 2, 1)[phase]
         first = (4 * self.core, 4 * self.core + 2 * self.y, self.rank)[phase]
-        span = self.out.at[pl.ds(2 * k, 2), pl.ds(first, width)]
+        span = self.out.at[pl.ds(2 * pair, 2), pl.ds(first, width), at]
         return self.remote(phase, k, span, span, phase)
 
     def reduce_step(self, k):
         self.halving(k).wait()
-        mine = 2 * k + self.far
-        self.sums[mine] = self.sums[mine] + self.got[k]
+        pair, at = self.piece(k)
+        mine = 2 * pair + self.far
+        self.sums[mine, at] = self.sums[mine, at] + self.got[k]
         self.settle(k).start()
         self.doubling(3, k).start()
 
@@ -738,108 +500,349 @@
         sums[step, imag, :] = sums[step, imag, :] + (big[half:, :half] - big[:half, half:])
 
 
-def third_kernel(group, rows_local, mixed, part_sums, w_mix, p_fwd, table, grad, field_out, grad_w, w_buf, mixed_blk, sums, got,
-                 back, stage, flipped, turn, grad_buf, bridged, w_sem, m_sem, s_sem, gw_sem, in_sem, out_sem, p_sem, bridged_sems,
-                 stage_far, far_sem):
+def whole_kernel(group, rows_local, field, grad, base, gained, p_fwd, p_inv, w_mix, field_out, grad_w, back_out, coef_shared,
+                 mixed_shared, field_buf, grad_buf, turn, stage, stage_far, expanded_fwd, expanded_inv, flipped, send_f, recv_f,
+                 padded, coef, mixed, w_in, planes, bridged, send_d, recv_d, message, share_send_a, share_send_d, halves,
+                 shared, sums, back, got, field_sem, grad_sem, p_sem, far_sem, send_f_sem, recv_f_sem, w_sem, bridged_sems,
+                 send_d_sem, recv_d_sem, share_a_sems, share_d_sems, half_sem, out_sem, gw_sem, again_sems, back_sem, last_sem):
     me = lax.axis_index('lat')
-    batch = grad.shape[0]
-    channels = grad.shape[1] // rows_local
-    depth = grad_buf.shape[0]
-    per = w_buf.shape[1]
-    degrees = w_mix.shape[0]
-    m_local = stage.shape[0]
-
-    def fetch(b):
-        return Halves(grad, b, grad_buf, lax.rem(b, depth), in_sem)
+    batch = field.shape[0]
+    channels = field.shape[1] // rows_local
+    m_local, degrees = stage.shape[:2]
+    used = degrees * m_local
+    bunch = coef.shape[0]
+    sources, share_rows = coef_shared.shape[1:3]
+
+    def fetch_field(b):
+        return Halves(field, b, field_buf, lax.rem(b, 2), field_sem)
+
+    def fetch_grad(b):
+        return Halves(grad, b, grad_buf, lax.rem(b, 2), grad_sem)
 
     def put(b):
-        return Halves(field_out, b, grad_buf, lax.rem(b, depth), out_sem, outward=True)
-
-    load_sums = pltpu.make_async_copy(part_sums, sums, s_sem)
-    load_sums.start()
+        return pltpu.make_async_copy(back.at[lax.rem(b, bunch)], back_out.at[b], out_sem.at[lax.rem(b, bunch)])
+
+    def fetch_back(b):
+        return pltpu.make_async_copy(back_out.at[b], coef.at[lax.rem(b, 2)], back_sem.at[lax.rem(b, 2)])
+
+    def fetch_last(b):
+        return Halves(grad, b, field_buf, lax.rem(b, 2), field_sem)
+
+    def put_last(b):
+        return Halves(field_out, b, field_buf, lax.rem(b, 2), last_sem, outward=True)
+
+    def fetch_shares(b):
+        slot = lax.rem(b, 2)
+        return [pltpu.make_async_copy(whole.at[b], halves.at[slot, which], half_sem.at[slot, which])
+                for which, whole in enumerate((mixed_shared, coef_shared))]
+
     greet(me, group)
+    fetch_field(0).start()
+    fetch_grad(0).start()
+    loading = own_tables(me, group, p_fwd, stage, p_sem)
+    loading_inv = own_tables(me, group, p_inv, stage, p_sem)
+    loading.start()
+    swap_f = Exchange(me, group, batch, send_f, recv_f, send_f_sem, recv_f_sem)
+    swap_g = BridgedExchange(me, group, batch, bridged, bridged_sems)
+    swap_h = BridgedExchange(me, group, batch, bridged, again_sems)
     total = WeightSum(me, group, sums, got, grad_w, gw_sem)
-    swap = BridgedExchange(me, group, batch, bridged, bridged_sems)
-    loading = own_tables(me, group, p_fwd, stage, p_sem)
-    loading_far = far_tables(swap, p_fwd, stage_far, far_sem)
-    loading.start()
+    swap_d = Exchange(me, group, batch, send_d, recv_d, send_d_sem, recv_d_sem)
+    share_a = Share(me, group, batch, share_send_a, message, coef_shared, share_a_sems)
+    share_d = Share(me, group, batch, share_send_d, message, mixed_shared, share_d_sems)
+    loading_far = far_tables(swap_g, p_inv, stage_far, far_sem)
     loading_far.start()
-    load_sums.wait()
+    loading_fwd = own_tables(me, group, p_fwd, stage, p_sem)
+    loading_far_fwd = far_tables(swap_h, p_fwd, stage_far, far_sem)
+    chunks = got.shape[0]
+    clear_after(padded, used)
     meet(group)
-    chunks = sums.shape[0] // 2
-    for k in range(2):
-        total.halving(k).start()
-
-    def unmix(k, slot):
-        for inner in range(per):
-            rows = rows_of_degree(mixed_blk.at[slot], inner, m_local)
-            res = dot(rows, mix_block(w_buf[slot, inner]), NN)
-            at = pl.ds(pl.multiple_of((k * per + inner) * m_local, m_local), m_local)
-            half = res.shape[1] // 2
-            for part in range(2):
-                back[:, part, at, :] = res[:, part * half:(part + 1) * half].reshape(batch, m_local, half)
-
-    def prepare():
-        loading.wait()
-        flip_rows(stage, flipped)
-        loading_far.wait()
-        flip_rows(stage_far, swap.flipped_far)
-
-    mix_loop(w_mix, [mixed], [mixed_blk], w_buf, w_sem, [m_sem], degrees // per, unmix, prepare)
-    fetch(0).start()
-    lag = 2
+
+    def build_planes():
+        depth, per = w_in.shape[:2]
+        blocks = degrees // per
+        half = w_in.shape[2] // 2
+
+        def fetch(k):
+            return pltpu.make_async_copy(w_mix.at[pl.ds(k * per, per)], w_in.at[lax.rem(k, depth)], w_sem.at[lax.rem(k, depth)])
+
+        for k in range(depth - 1):
+            fetch(k).start()
+
+        @pl.loop(0, blocks)
+        def _(k):
+            @pl.when(k + depth - 1 < blocks)
+            def _():
+                fetch(k + depth - 1).start()
+
+            fetch(k).wait()
+            for inner in range(per):
+                rows = w_in.at[lax.rem(k, depth), inner]
+                for part in range(2):
+                    planes[k * per + inner, part] = rows[pl.ds(part, half, stride=2), :].astype(BF16)
+
+    def unmix_bunch():
+        @pl.loop(0, degrees // 8)
+        def _(k):
+            for inner in range(8):
+                at = pl.ds(pl.multiple_of((k * 8 + inner) * m_local, m_local), m_local)
+                rows = [back[:, part, at, :].reshape(bunch * m_local, channels) for part in range(2)]
+                res = dot(jnp.concatenate(rows, axis=1).astype(BF16), mix_block(planes[k * 8 + inner]), NN)
+                for part in range(2):
+                    back[:, part, at, :] = res[:, part * channels:(part + 1) * channels].reshape(bunch, m_local, channels)
+
+    def mix_bunch():
+        @pl.loop(0, degrees // 8)
+        def _(k):
+            for inner in range(8):
+                at = pl.ds(pl.multiple_of((k * 8 + inner) * m_local, m_local), m_local)
+                rows = [coef[:, part, at, :].reshape(bunch * m_local, channels) for part in range(2)]
+                res = dot(jnp.concatenate(rows, axis=1).astype(BF16), mix_block(planes[k * 8 + inner]), NT)
+                for part in range(2):
+                    mixed[:, part, at, :] = res[:, part * channels:(part + 1) * channels].reshape(bunch, m_local, channels)
+
+    def weigh_sample(b):
+        for copy in fetch_shares(b):
+            copy.wait()
+        for which in range(2):
+            for source in range(sources):
+                at = pl.ds(source * (shared.shape[1] // sources), share_rows)
+                shared[which, at, :] = halves[lax.rem(b, 2), which, source].astype(F32)
+        weigh(shared, sources, sums, m_local)
+
+    def collect(b):
+        share_a.arrive(b)
+        share_d.arrive(b)
+        for copy in fetch_shares(b):
+            copy.start()
+
+    lag_a, lag_b, lag_c, lag_d = 2, 4, 6, 8
+    lag_e = batch + lag_c
+    close = batch + lag_d
+    steps = [total.reduce_step] + [functools.partial(total.gather_step, p) for p in (2, 1, 0, -1)]
+
+    def advance(n, sub):
+        @pl.when((n >= 0) & (n * 2 + sub + 4 < chunks))
+        def _():
+            total.halving(n * 2 + sub + 4).start()
+
+        for late, step in reversed(list(enumerate(steps))):
+            k = (n - late) * 2 + sub
+
+            @pl.when((k >= 0) & (k < chunks))
+            def _():
+                step(k)
 
     def body(i, carry):
+        @pl.when((i >= lag_e) & (i < batch + lag_e))
+        def _():
+            b = i - lag_e
+
+            @pl.when(b + 1 < batch)
+            def _():
+                fetch_back(b + 1).start()
+
+            fetch_back(b).wait()
+            swap_h.reserve(b)
+            legendre_inverse(coef.at[lax.rem(b, 2)], flipped, swap_h, lax.rem(b, SLOTS), rows_local)
+            swap_h.start(b)
+
         @pl.when(i < batch)
         def _():
-            swap.reserve(i)
-            legendre_inverse(back.at[i], flipped, swap, lax.rem(i, SLOTS), rows_local)
-            swap.start(i)
-
-        @pl.when((i >= 1) & (i < batch + 1))
-        def _():
-            swap.relay(i - 1)
-
-        steps = [total.reduce_step] + [functools.partial(total.gather_step, p) for p in (2, 1, 0, -1)]
-        @pl.when((i >= lag) & (i < batch + lag))
-        def _():
-            b = i - lag
-            half = lax.rem(b, depth)
-
-            @pl.when(b >= depth - 1)
-            def _():
-                put(b - depth + 1).wait()
+            @pl.when(i + 1 < batch)
+            def _():
+                fetch_field(i + 1).start()
+
+            fetch_field(i).wait()
+            half = lax.rem(i, 2)
+            analyse(lambda t: read_row(field_buf, half, t, channels, rows_local), base, turn, rows_local)
+            swap_f.reserve(i)
+            pack_blocks(turn, send_f, lax.rem(i, SLOTS))
+            swap_f.start(i)
+
+        @pl.when(i == 0)
+        def _():
+            loading.wait()
+            expand_rows(stage, expanded_fwd, rows_local)
+            loading_inv.start()
+            loading_far.wait()
+            flip_rows(stage_far, swap_g.flipped_far)
+
+        @pl.when(i == 1)
+        def _():
+            build_planes()
+            loading_inv.wait()
+            expand_rows(stage, expanded_inv, rows_local)
+            flip_rows(stage, flipped)
+            sums[...] = jnp.zeros_like(sums)
+
+        @pl.when((i >= lag_a) & (i < batch + lag_a))
+        def _():
+            b = i - lag_a
+            swap_f.arrive(b)
+            legendre_forward(recv_f, b, expanded_fwd, padded, rows_local)
+            coef[lax.rem(b, bunch)] = padded[:, pl.ds(0, used), :]
+            share_a.give(b, padded)
+
+            @pl.when(lax.rem(b, bunch) == bunch - 1)
+            def _():
+                mix_bunch()
+
+        @pl.when((i >= lag_b) & (i < batch + lag_b))
+        def _():
+            b = i - lag_b
+            swap_g.reserve(b)
+            legendre_inverse(mixed.at[lax.rem(b, bunch)], flipped, swap_g, lax.rem(b, SLOTS), rows_local)
+            swap_g.start(b)
+
+        @pl.when((i >= lag_b + 1) & (i < batch + lag_b + 1))
+        def _():
+            swap_g.relay(i - lag_b - 1)
+
+        @pl.when((i >= lag_c) & (i < batch + lag_c))
+        def _():
+            b = i - lag_c
+            half = lax.rem(b, 2)
 
             @pl.when(b + 1 < batch)
             def _():
-                fetch(b + 1).start()
-
-            fetch(b).wait()
-            swap.arrive(b)
-            unpack_blocks(swap.recv, b, turn)
+                fetch_grad(b + 1).start()
+
+            fetch_grad(b).wait()
+            swap_g.arrive(b)
+            unpack_blocks(swap_g.recv, b, turn)
             for t in range(rows_local):
-                added = synthesise(turn, t, table, rows_local)
+                slope = gelu_slope(synthesise(turn, t, gained, rows_local))
                 given = read_row(grad_buf, half, t, channels, rows_local)
-                write_row(grad_buf, half, t, channels, rows_local, given + added)
-            put(b).start()
-
-        @pl.when(i + 2 < chunks)
-        def _():
-            total.halving(i + 2).start()
-
-        for late, step in reversed(list(enumerate(steps))):
-            k = i - late
-
-            @pl.when((k >= 0) & (k < chunks))
-            def _():
-                step(k)
-
+                write_row(grad_buf, half, t, channels, rows_local, given * slope)
+            analyse(lambda t: read_row(grad_buf, half, t, channels, rows_local), gained, turn, rows_local)
+            swap_d.reserve(b)
+            pack_blocks(turn, send_d, lax.rem(b, SLOTS))
+            swap_d.start(b)
+
+        @pl.when(i == lag_e - 2)
+        def _():
+            loading_fwd.start()
+            loading_far_fwd.start()
+
+        @pl.when(i == lag_e - 1)
+        def _():
+            loading_fwd.wait()
+            flip_rows(stage, flipped)
+            loading_far_fwd.wait()
+            flip_rows(stage_far, swap_h.flipped_far)
+            swap_g.drain()
+            fetch_back(0).start()
+
+        @pl.when((i >= lag_d) & (i < batch + lag_d))
+        def _():
+            b = i - lag_d
+
+            @pl.when((b >= bunch) & (lax.rem(b, bunch) == 0))
+            def _():
+                unmix_bunch()
+                for n in range(bunch):
+                    put(b - bunch + n).start()
+
+            @pl.when(b >= 2)
+            def _():
+                weigh_sample(b - 2)
+
+            @pl.when(b >= 1)
+            def _():
+                collect(b - 1)
+
+            swap_d.arrive(b)
+            legendre_forward(recv_d, b, expanded_inv, padded, rows_local)
+            share_d.give(b, padded)
+
+            @pl.when(b >= bunch)
+            def _():
+                put(b - bunch).wait()
+
+            back[lax.rem(b, bunch)] = padded[:, pl.ds(0, used), :]
+
+        @pl.when(i == close)
+        def _():
+            fetch_last(0).start()
+            weigh_sample(batch - 2)
+            collect(batch - 1)
+            weigh_sample(batch - 1)
+            for k in range(4):
+                total.halving(k).start()
+
+        advance(i - close, 0)
+
+        @pl.when((i >= lag_e + 1) & (i < batch + lag_e + 1))
+        def _():
+            swap_h.relay(i - lag_e - 1)
+
+        @pl.when((i >= close) & (i < batch + close))
+        def _():
+            b = i - close
+            half = lax.rem(b, 2)
+
+            @pl.when(b >= 1)
+            def _():
+                put_last(b - 1).wait()
+
+            @pl.when(b + 1 < batch)
+            def _():
+                fetch_last(b + 1).start()
+
+            fetch_last(b).wait()
+            swap_h.arrive(b)
+            unpack_blocks(swap_h.recv, b, turn)
+            for t in range(rows_local):
+                added = synthesise(turn, t, base, rows_local)
+                given = read_row(field_buf, half, t, channels, rows_local)
+                write_row(field_buf, half, t, channels, rows_local, given + added)
+            put_last(b).start()
+
+        @pl.when(i == close + 1)
+        def _():
+            unmix_bunch()
+            for n in range(bunch):
+                put(batch - bunch + n).start()
+
+        @pl.when(i == close + 3)
+        def _():
+            for n in range(bunch):
+                put(batch - bunch + n).wait()
+
+        advance(i - close, 1)
         return carry
 
-    lax.fori_loop(0, max(batch + lag, chunks + 4), body, 0)
-    swap.drain()
-    for b in range(batch - depth + 1, batch):
-        put(b).wait()
+    lax.fori_loop(0, close + max(batch, chunks // 2 + 4), body, 0)
+    for swap in (swap_f, swap_h, swap_d, share_a, share_d):
+        swap.drain()
+    put_last(batch - 1).wait()
+
+
+def finish_kernel(first, second, first_out, second_out, first_ring, second_ring, in_sem, out_sem):
+    depth = first_ring.shape[0]
+    pieces = []
+    for side, (source, target, ring) in enumerate(((first, first_out, first_ring), (second, second_out, second_ring))):
+        for n in range(source.shape[0]):
+            slot = n % depth
+            take = pltpu.make_async_copy(source.at[n], ring.at[slot], in_sem.at[side, slot])
+            give = pltpu.make_async_copy(ring.at[slot], target.at[n], out_sem.at[side, slot])
+            pieces.append(((n, side), (side, n), take, give))
+    pieces.sort(key=lambda piece: piece[0])
+    given = {piece[1]: piece[3] for piece in pieces}
+    waited = set()
+    for k in range(len(pieces) + depth):
+        if k < len(pieces):
+            _, (side, n), take, _ = pieces[k]
+            if n >= depth:
+                given[side, n - depth].wait()
+                waited.add((side, n - depth))
+            take.start()
+        if k >= depth:
+            pieces[k - depth][2].wait()
+            pieces[k - depth][3].start()
+    for _, place, _, give in pieces:
+        if place not in waited:
+            give.wait()
 
 
 def any_specs(n):
@@ -877,7 +880,6 @@
         field_t = vmem((2, lon_count // LANES, channels * rows_local, LANES), F32)
         table_spec = pl.BlockSpec(memory_space=pltpu.VMEM)
         any_spec = pl.BlockSpec(memory_space=pl.ANY)
-        per = 8
         late = sum(degrees - slot * group < lats // 2 for slot in range(m_local))
         far_rows = sum(degrees - slot * group for slot in range(m_local - late, m_local))
         late_rows = late * 2 * rows_local
@@ -890,8 +892,6 @@
         share_out = jax.ShapeDtypeStruct((batch, ranks, share_rows, channels), BF16)
         share_sems = (dma((SLOTS,)), dma((batch,)), dma((SLOTS,)))
 
-        blk_t = vmem((DEPTH, batch, 2, per * m_local, channels), F32)
-        w_t = vmem((DEPTH, per, 2, channels, channels), BF16)
         far_stage_t = vmem((late, degrees, lats), F32)
         steps = degrees // ranks
         sums_shape = (steps, channels * 2, channels)
@@ -899,31 +899,29 @@
         single_t = vmem((BUNCH,) + coef_shape[1:], F32)
         share_send_t = vmem((SLOTS, ranks, share_rows, channels), BF16)
         swap_sems = (dma((SLOTS,)), dma((batch,)))
-        mixed, sums, planes, _, _ = pl.pallas_call(
-            functools.partial(front_kernel, group, rows_local), name='front',
-            out_shape=[jax.ShapeDtypeStruct(coef_shape, F32), jax.ShapeDtypeStruct(sums_shape, F32),
-                       jax.ShapeDtypeStruct(planes_shape, BF16), share_out, share_out],
+        field_out, gw_total, _, _, _ = pl.pallas_call(
+            functools.partial(whole_kernel, group, rows_local), name='whole',
+            out_shape=[jax.ShapeDtypeStruct(grad.shape, F32),
+                       jax.ShapeDtypeStruct((steps, ranks, channels * 2, channels), F32),
+                       jax.ShapeDtypeStruct(coef_shape, F32), share_out, share_out],
             in_specs=[any_spec, any_spec, table_spec, table_spec, any_spec, any_spec, any_spec], out_specs=[any_spec] * 5,
             scratch_shapes=[field_t, field_t, turn_t, stage_t, far_stage_t, expanded_t, expanded_t, flipped_t, send_t, recv_t,
                             vmem((2, 2 * degrees * m_local, channels), F32), single_t, single_t,
                             vmem((4, 4, channels * 2, channels), F32), vmem(planes_shape, BF16), bridged_t, send_t, recv_t,
                             vmem((ranks, share_rows, channels), F32), share_send_t, share_send_t,
                             vmem((2, 2) + share_out.shape[1:], BF16), vmem((2, ranks * (share_rows + 8), channels), F32),
-                            vmem(sums_shape, F32), vmem((2,) + coef_shape[1:], F32),
-                            dma((2, 2)), dma((2, 2)), dma(()), dma(()), *swap_sems, dma((4,)), dma(()), bridged_sems, *swap_sems,
-                            share_sems, share_sems, dma((2, 2)), dma((2,)), dma(())],
+                            vmem(sums_shape, F32), single_t, vmem((PIECES * steps // 2, channels * 2 // PIECES, channels), F32),
+                            dma((2, 2)), dma((2, 2)), dma(()), dma(()), *swap_sems, dma((4,)), bridged_sems, *swap_sems,
+                            share_sems, share_sems, dma((2, 2)), dma((BUNCH,)), dma((2, 6, PIECES * steps // 2)), bridged_sems,
+                            dma((2,)), dma((2, 2))],
             compiler_params=params(0))(field, grad, base, gained, p_fwd, p_inv, w_rows)
 
-        w_rect = (channels * 2, channels)
+        gw_total = gw_total.reshape(steps, ranks * channels * 2, channels)
+        results = [jax.ShapeDtypeStruct(whole.shape, F32) for whole in (field_out, gw_total)]
         field_out, gw_total = pl.pallas_call(
-            functools.partial(third_kernel, group, rows_local), name='third',
-            out_shape=[jax.ShapeDtypeStruct(grad.shape, F32), jax.ShapeDtypeStruct((steps, ranks) + w_rect, F32)],
-            in_specs=[any_spec] * 4 + [table_spec, any_spec], out_specs=[any_spec] * 2,
-            scratch_shapes=[w_t, blk_t, vmem(sums_shape, F32), vmem((steps // 2,) + w_rect, F32), vmem(coef_shape, F32), stage_t, flipped_t, turn_t,
-                            vmem((3, lon_count // LANES, channels * rows_local, LANES), F32), bridged_t,
-                            dma((DEPTH,)), dma((DEPTH,)), dma(()), dma((2, 6, steps // 2)), dma((3, 2)), dma((3, 2)), dma(()),
-                            bridged_sems, far_stage_t, dma(())],
-            compiler_params=params(2))(mixed, sums, planes, p_fwd, base, grad)
+            finish_kernel, name='finish', out_shape=results, in_specs=[any_spec] * 2, out_specs=[any_spec] * 2,
+            scratch_shapes=[vmem((RING,) + whole.shape[1:], F32) for whole in results] + [dma((2, RING)), dma((2, RING))],
+            compiler_params=params())(field_out, gw_total)
 
         grad_wmix = jnp.swapaxes(gw_total.reshape(degrees, channels, 2, channels), 2, 3)
         return field_out.reshape(grad_loc.shape), grad_wmix

time: 659 us -> 632 us (0.959)
  local copies, waits for them, and re-layouts: 22.2 us -> 0 us
    unnamed x2 -> x0, local copies, waits for them, and re-layouts: 22.2 us -> none
where the time goes in v9:
time: 632 us
  Pallas kernels  631 us (100%)
    pallas_call x1, Pallas kernels, local_step(): pl.pallas_call(functools.partial(whole_kernel, group, rows_local), name='...  612 us
    pallas_call x1, Pallas kernels, local_step(): pl.pallas_call(finish_kernel, name='finish', out_shape=results, in_specs=...  19.7 us

profile of v9, /device:TPU:0, one launch (start us, length us, event | category | flops | bytes accessed | tf_op | source)
XLA Modules:
  0.0 632.1 jit_solution(15528025172746835464)
XLA Ops:
  0.6 611.8 %whole.1 = (f32[12,1024,256]{2,1,0:T(8,128)}, f32[16,8,256,128]{3,2,1,0:T(8,128)}, f32[12,2,1024,128]{3,2,1,0:T(8,128)}, bf16[12,8,144,128]{3,2,1,0:T(8,128)(2,1)}, bf16[12,8,144,128]{3,2,1,0:T(8,128)(2,1)}) custom-call(f32[12,1024,256]{2,1,0:T(8,128)} %bitcast.12, f32[12,1024,256]{2,1,0:T(8,128)} %bitcast.13, bf16[2,256,256]{2,1,0:T(8,128)(2,1)} %constant.14.base, ...), custom_call_target="tpu_custom_call" | custom-call | tf_op jit(solution)/shard_map/whole/pallas_call | solution.py:902
  612.4 19.7 %finish.1 = (f32[12,1024,256]{2,1,0:T(8,128)}, f32[16,2048,128]{2,1,0:T(8,128)}) custom-call(f32[12,1024,256]{2,1,0:T(8,128)} %get-tuple-element.6.first, f32[16,2048,128]{2,1,0:T(8,128)} %bitcast.11), custom_call_target="tpu_custom_call" | custom-call | tf_op jit(solution)/shard_map/finish/pallas_call | solution.py:921

commit v10 on v9

--- a/solution.py
+++ b/solution.py
@@ -344,8 +344,8 @@
     modes = table.shape[1]
     for t in range(0, rows_local, 2):
         pair = jnp.concatenate([values_at(t), values_at(t + 1)], axis=0)
-        high, low = split_halves(pair)
-        out = dot(table[0], high, NT) + dot(table[0], low, NT) + dot(table[1], high, NT)
+        high, low = split_halves(pair * 0.5)
+        out = 2.0 * (dot(table[0], high, NT) + dot(table[0], low, NT) + dot(table[1], high, NT))
         channels = out.shape[1] // 2
         turn[pl.ds(t, modes, stride=rows_local), :] = out[:, :channels]
         turn[pl.ds(t + 1, modes, stride=rows_local), :] = out[:, channels:]
@@ -621,9 +621,9 @@
     steps = [total.reduce_step] + [functools.partial(total.gather_step, p) for p in (2, 1, 0, -1)]
 
     def advance(n, sub):
-        @pl.when((n >= 0) & (n * 2 + sub + 4 < chunks))
-        def _():
-            total.halving(n * 2 + sub + 4).start()
+        @pl.when((n >= 0) & (n * 2 + sub + 2 < chunks))
+        def _():
+            total.halving(n * 2 + sub + 2).start()
 
         for late, step in reversed(list(enumerate(steps))):
             k = (n - late) * 2 + sub
@@ -767,7 +767,7 @@
             weigh_sample(batch - 2)
             collect(batch - 1)
             weigh_sample(batch - 1)
-            for k in range(4):
+            for k in range(2):
                 total.halving(k).start()
 
         advance(i - close, 0)

time: 632 us -> 627 us (level)
  no operation moved by 1% of the time
where the time goes in v10:
time: 627 us; the launch traced here: 626 us
  Pallas kernels  626 us (100%)
    pallas_call x1, Pallas kernels, local_step(): pl.pallas_call(functools.partial(whole_kernel, group, rows_local), name='...  606 us
    pallas_call x1, Pallas kernels, local_step(): pl.pallas_call(finish_kernel, name='finish', out_shape=results, in_specs=...  19.7 us

profile of v10, /device:TPU:0, one launch (start us, length us, event | category | flops | bytes accessed | tf_op | source)
XLA Modules:
  0.0 626.5 jit_solution(14927093736111855106)
XLA Ops:
  0.6 606.2 %whole.1 = (f32[12,1024,256]{2,1,0:T(8,128)}, f32[16,8,256,128]{3,2,1,0:T(8,128)}, f32[12,2,1024,128]{3,2,1,0:T(8,128)}, bf16[12,8,144,128]{3,2,1,0:T(8,128)(2,1)}, bf16[12,8,144,128]{3,2,1,0:T(8,128)(2,1)}) custom-call(f32[12,1024,256]{2,1,0:T(8,128)} %bitcast.12, f32[12,1024,256]{2,1,0:T(8,128)} %bitcast.13, bf16[2,256,256]{2,1,0:T(8,128)(2,1)} %constant.14.base, ...), custom_call_target="tpu_custom_call" | custom-call | tf_op jit(solution)/shard_map/whole/pallas_call | solution.py:902
  606.8 19.7 %finish.1 = (f32[12,1024,256]{2,1,0:T(8,128)}, f32[16,2048,128]{2,1,0:T(8,128)}) custom-call(f32[12,1024,256]{2,1,0:T(8,128)} %get-tuple-element.6.first, f32[16,2048,128]{2,1,0:T(8,128)} %bitcast.11), custom_call_target="tpu_custom_call" | custom-call | tf_op jit(solution)/shard_map/finish/pallas_call | solution.py:921

commit v11 on v10

--- a/solution.py
+++ b/solution.py
@@ -500,11 +500,12 @@
         sums[step, imag, :] = sums[step, imag, :] + (big[half:, :half] - big[:half, half:])
 
 
-def whole_kernel(group, rows_local, field, grad, base, gained, p_fwd, p_inv, w_mix, field_out, grad_w, back_out, coef_shared,
+def whole_kernel(group, rows_local, field, grad, base_hbm, gained_hbm, p_fwd, p_inv, w_mix, field_out, grad_w, back_out, coef_shared,
                  mixed_shared, field_buf, grad_buf, turn, stage, stage_far, expanded_fwd, expanded_inv, flipped, send_f, recv_f,
                  padded, coef, mixed, w_in, planes, bridged, send_d, recv_d, message, share_send_a, share_send_d, halves,
                  shared, sums, back, got, field_sem, grad_sem, p_sem, far_sem, send_f_sem, recv_f_sem, w_sem, bridged_sems,
-                 send_d_sem, recv_d_sem, share_a_sems, share_d_sems, half_sem, out_sem, gw_sem, again_sems, back_sem, last_sem):
+                 send_d_sem, recv_d_sem, share_a_sems, share_d_sems, half_sem, out_sem, gw_sem, again_sems, back_sem, last_sem, base, gained,
+                 table_sem):
     me = lax.axis_index('lat')
     batch = field.shape[0]
     channels = field.shape[1] // rows_local
@@ -536,8 +537,12 @@
         return [pltpu.make_async_copy(whole.at[b], halves.at[slot, which], half_sem.at[slot, which])
                 for which, whole in enumerate((mixed_shared, coef_shared))]
 
+    load_base = pltpu.make_async_copy(base_hbm, base, table_sem.at[0])
+    load_gained = pltpu.make_async_copy(gained_hbm, gained, table_sem.at[1])
+    fetch_field(0).start()
+    load_base.start()
     greet(me, group)
-    fetch_field(0).start()
+    load_gained.start()
     fetch_grad(0).start()
     loading = own_tables(me, group, p_fwd, stage, p_sem)
     loading_inv = own_tables(me, group, p_inv, stage, p_sem)
@@ -554,8 +559,6 @@
     loading_fwd = own_tables(me, group, p_fwd, stage, p_sem)
     loading_far_fwd = far_tables(swap_h, p_fwd, stage_far, far_sem)
     chunks = got.shape[0]
-    clear_after(padded, used)
-    meet(group)
 
     def build_planes():
         depth, per = w_in.shape[:2]
@@ -632,6 +635,21 @@
             def _():
                 step(k)
 
+    def take_modes(b):
+        @pl.when(b + 1 < batch)
+        def _():
+            fetch_field(b + 1).start()
+
+        fetch_field(b).wait()
+        half = lax.rem(b, 2)
+        analyse(lambda t: read_row(field_buf, half, t, channels, rows_local), base, turn, rows_local)
+        swap_f.reserve(b)
+        pack_blocks(turn, send_f, lax.rem(b, SLOTS))
+
+    load_base.wait()
+    take_modes(0)
+    meet(group)
+
     def body(i, carry):
         @pl.when((i >= lag_e) & (i < batch + lag_e))
         def _():
@@ -646,21 +664,18 @@
             legendre_inverse(coef.at[lax.rem(b, 2)], flipped, swap_h, lax.rem(b, SLOTS), rows_local)
             swap_h.start(b)
 
+        @pl.when((i >= 1) & (i < batch))
+        def _():
+            take_modes(i)
+
         @pl.when(i < batch)
         def _():
-            @pl.when(i + 1 < batch)
-            def _():
-                fetch_field(i + 1).start()
-
-            fetch_field(i).wait()
-            half = lax.rem(i, 2)
-            analyse(lambda t: read_row(field_buf, half, t, channels, rows_local), base, turn, rows_local)
-            swap_f.reserve(i)
-            pack_blocks(turn, send_f, lax.rem(i, SLOTS))
             swap_f.start(i)
 
         @pl.when(i == 0)
         def _():
+            clear_after(padded, used)
+            load_gained.wait()
             loading.wait()
             expand_rows(stage, expanded_fwd, rows_local)
             loading_inv.start()
@@ -878,7 +893,6 @@
         expanded_t = vmem((m_local, 2 * degrees, 2 * lats), BF16)
         flipped_t = vmem((m_local, lats, degrees), BF16)
         field_t = vmem((2, lon_count // LANES, channels * rows_local, LANES), F32)
-        table_spec = pl.BlockSpec(memory_space=pltpu.VMEM)
         any_spec = pl.BlockSpec(memory_space=pl.ANY)
         late = sum(degrees - slot * group < lats // 2 for slot in range(m_local))
         far_rows = sum(degrees - slot * group for slot in range(m_local - late, m_local))
@@ -904,7 +918,7 @@
             out_shape=[jax.ShapeDtypeStruct(grad.shape, F32),
                        jax.ShapeDtypeStruct((steps, ranks, channels * 2, channels), F32),
                        jax.ShapeDtypeStruct(coef_shape, F32), share_out, share_out],
-            in_specs=[any_spec, any_spec, table_spec, table_spec, any_spec, any_spec, any_spec], out_specs=[any_spec] * 5,
+            in_specs=[any_spec] * 7, out_specs=[any_spec] * 5,
             scratch_shapes=[field_t, field_t, turn_t, stage_t, far_stage_t, expanded_t, expanded_t, flipped_t, send_t, recv_t,
                             vmem((2, 2 * degrees * m_local, channels), F32), single_t, single_t,
                             vmem((4, 4, channels * 2, channels), F32), vmem(planes_shape, BF16), bridged_t, send_t, recv_t,
@@ -913,7 +927,7 @@
                             vmem(sums_shape, F32), single_t, vmem((PIECES * steps // 2, channels * 2 // PIECES, channels), F32),
                             dma((2, 2)), dma((2, 2)), dma(()), dma(()), *swap_sems, dma((4,)), bridged_sems, *swap_sems,
                             share_sems, share_sems, dma((2, 2)), dma((BUNCH,)), dma((2, 6, PIECES * steps // 2)), bridged_sems,
-                            dma((2,)), dma((2, 2))],
+                            dma((2,)), dma((2, 2)), vmem(base.shape, BF16), vmem(base.shape, BF16), dma((2,))],
             compiler_params=params(0))(field, grad, base, gained, p_fwd, p_inv, w_rows)
 
         gw_total = gw_total.reshape(steps, ranks * channels * 2, channels)

time: 627 us -> 626 us (level)
  no operation moved by 1% of the time
where the time goes in v11:
time: 626 us; the launch traced here: 625 us
  Pallas kernels  625 us (100%)
    pallas_call x1, Pallas kernels, local_step(): pl.pallas_call(functools.partial(whole_kernel, group, rows_local), name='...  605 us
    pallas_call x1, Pallas kernels, local_step(): pl.pallas_call(finish_kernel, name='finish', out_shape=results, in_specs=...  19.7 us

profile of v11, /device:TPU:0, one launch (start us, length us, event | category | flops | bytes accessed | tf_op | source)
XLA Modules:
  0.0 625.2 jit_solution(932875248522103131)
XLA Ops:
  0.6 604.9 %whole.1 = (f32[12,1024,256]{2,1,0:T(8,128)}, f32[16,8,256,128]{3,2,1,0:T(8,128)}, f32[12,2,1024,128]{3,2,1,0:T(8,128)}, bf16[12,8,144,128]{3,2,1,0:T(8,128)(2,1)}, bf16[12,8,144,128]{3,2,1,0:T(8,128)(2,1)}) custom-call(f32[12,1024,256]{2,1,0:T(8,128)} %bitcast.12, f32[12,1024,256]{2,1,0:T(8,128)} %bitcast.13, bf16[2,256,256]{2,1,0:T(8,128)(2,1)} %constant.14.base_hbm, ...), custom_call_target="tpu_custom_call" | custom-call | tf_op jit(solution)/shard_map/whole/pallas_call | solution.py:916
  605.5 19.7 %finish.1 = (f32[12,1024,256]{2,1,0:T(8,128)}, f32[16,2048,128]{2,1,0:T(8,128)}) custom-call(f32[12,1024,256]{2,1,0:T(8,128)} %get-tuple-element.6.first, f32[16,2048,128]{2,1,0:T(8,128)} %bitcast.11), custom_call_target="tpu_custom_call" | custom-call | tf_op jit(solution)/shard_map/finish/pallas_call | solution.py:935

commit v12 on v11

--- a/solution.py
+++ b/solution.py
@@ -101,7 +101,7 @@
 
         @pl.loop(1, self.group)
         def _(step):
-            target = jnp.bitwise_xor(self.me, self.group - step)
+            target = jnp.bitwise_xor(self.me, jnp.where(step <= 8, 16 - step, step - 8))
             pltpu.make_async_remote_copy(
                 self.send.at[slot, target], self.recv.at[b, self.me], self.send_sem.at[slot], self.recv_sem.at[b],
                 device_id={'lat': target}, device_id_type=MESH).start()

time: 626 us -> 624 us (level)
  no operation moved by 1% of the time
where the time goes in v12:
time: 624 us
  Pallas kernels  623 us (100%)
    pallas_call x1, Pallas kernels, local_step(): pl.pallas_call(functools.partial(whole_kernel, group, rows_local), name='...  603 us
    pallas_call x1, Pallas kernels, local_step(): pl.pallas_call(finish_kernel, name='finish', out_shape=results, in_specs=...  19.7 us

profile of v12, /device:TPU:0, one launch (start us, length us, event | category | flops | bytes accessed | tf_op | source)
XLA Modules:
  0.0 623.5 jit_solution(278965741430465616)
XLA Ops:
  0.6 603.2 %whole.1 = (f32[12,1024,256]{2,1,0:T(8,128)}, f32[16,8,256,128]{3,2,1,0:T(8,128)}, f32[12,2,1024,128]{3,2,1,0:T(8,128)}, bf16[12,8,144,128]{3,2,1,0:T(8,128)(2,1)}, bf16[12,8,144,128]{3,2,1,0:T(8,128)(2,1)}) custom-call(f32[12,1024,256]{2,1,0:T(8,128)} %bitcast.12, f32[12,1024,256]{2,1,0:T(8,128)} %bitcast.13, bf16[2,256,256]{2,1,0:T(8,128)(2,1)} %constant.14.base_hbm, ...), custom_call_target="tpu_custom_call" | custom-call | tf_op jit(solution)/shard_map/whole/pallas_call | solution.py:916
  603.9 19.7 %finish.1 = (f32[12,1024,256]{2,1,0:T(8,128)}, f32[16,2048,128]{2,1,0:T(8,128)}) custom-call(f32[12,1024,256]{2,1,0:T(8,128)} %get-tuple-element.6.first, f32[16,2048,128]{2,1,0:T(8,128)} %bitcast.11), custom_call_target="tpu_custom_call" | custom-call | tf_op jit(solution)/shard_map/finish/pallas_call | solution.py:935

commit v13 on v12

--- a/solution.py
+++ b/solution.py
@@ -12,7 +12,7 @@
 MESH = pl.DeviceIdType.MESH
 LANES = 128
 SLOTS = 3
-BUNCH = 3
+BUNCH = 2
 PIECES = 2
 RING = 6
 VMEM_LIMIT = 67043328
@@ -618,7 +618,7 @@
         for copy in fetch_shares(b):
             copy.start()
 
-    lag_a, lag_b, lag_c, lag_d = 2, 4, 6, 8
+    lag_a, lag_b, lag_c, lag_d = 2, 3, 5, 7
     lag_e = batch + lag_c
     close = batch + lag_d
     steps = [total.reduce_step] + [functools.partial(total.gather_step, p) for p in (2, 1, 0, -1)]

time: 624 us -> 626 us (level)
  no operation moved by 1% of the time
where the time goes in v13:
time: 626 us; the launch traced here: 625 us
  Pallas kernels  624 us (100%)
    pallas_call x1, Pallas kernels, local_step(): pl.pallas_call(functools.partial(whole_kernel, group, rows_local), name='...  604 us
    pallas_call x1, Pallas kernels, local_step(): pl.pallas_call(finish_kernel, name='finish', out_shape=results, in_specs=...  19.7 us

profile of v13, /device:TPU:0, one launch (start us, length us, event | category | flops | bytes accessed | tf_op | source)
XLA Modules:
  0.0 624.7 jit_solution(8421153289735531456)
XLA Ops:
  0.6 604.4 %whole.1 = (f32[12,1024,256]{2,1,0:T(8,128)}, f32[16,8,256,128]{3,2,1,0:T(8,128)}, f32[12,2,1024,128]{3,2,1,0:T(8,128)}, bf16[12,8,144,128]{3,2,1,0:T(8,128)(2,1)}, bf16[12,8,144,128]{3,2,1,0:T(8,128)(2,1)}) custom-call(f32[12,1024,256]{2,1,0:T(8,128)} %bitcast.12, f32[12,1024,256]{2,1,0:T(8,128)} %bitcast.13, bf16[2,256,256]{2,1,0:T(8,128)(2,1)} %constant.14.base_hbm, ...), custom_call_target="tpu_custom_call" | custom-call | tf_op jit(solution)/shard_map/whole/pallas_call | solution.py:916
  605.1 19.7 %finish.1 = (f32[12,1024,256]{2,1,0:T(8,128)}, f32[16,2048,128]{2,1,0:T(8,128)}) custom-call(f32[12,1024,256]{2,1,0:T(8,128)} %get-tuple-element.6.first, f32[16,2048,128]{2,1,0:T(8,128)} %bitcast.11), custom_call_target="tpu_custom_call" | custom-call | tf_op jit(solution)/shard_map/finish/pallas_call | solution.py:935
